TPU v7x, 32 devices: a whole 2x2x4 slice. The times are simulated.
32 devices in a mesh: gx: 8 (over z, core), gy: 4 (over y, x).
Axes of the slice: x: 2, y: 2, z: 4, core: 2. Of those that a mesh axis runs over, the one named last changes fastest.
Arguments:
- features: float32 [8, 4, 128, 256], P('gx', 'gy'), may hold values from -6 to 6
- offsets: float32 [8, 4, 3, 128], P('gx', 'gy'), may hold values from 0 to 1
- species: int32 [8, 4, 128], P('gx', 'gy'), may hold values from 0 to 63
- neighbours: int32 [8, 4, 128, 8], P('gx', 'gy'), may hold values from 0 to 4095, as said below
- edge_mask: int32 [8, 4, 128, 8], P('gx', 'gy'), may hold values 0 or 1
- wavevectors: int32 [3, 512], replicated, may hold values from -4 to 3, as said below
- value_weight: float32 [256, 256], replicated, may hold values from -0.375 to 0.375
- radial_weight: float32 [64, 256], replicated, may hold values from -3 to 3
- species_embed: float32 [64, 256], replicated, may hold values from -3 to 3
- mixing_weight: float32 [256, 256], replicated, may hold values from -0.375 to 0.375
- group_filter: float32 [8, 256, 256], P('gx'), may hold values from -0.375 to 0.375
Outputs:
- updated: float32 [8, 4, 128, 256], P('gx', 'gy')
Inputs may be any that keep to these rules, and one draw needn't show every extreme that they name: `neighbours`: every listed neighbour lies in a block whose first index differs from the atom's by at most one modulo 8 and whose second index differs by at most one modulo 4. `wavevectors`: the first component lies in -4 .. 3, the second in -2 .. 1, the third in -2 .. 2.
All inputs are finite; a program needn't handle non-finite values. No bound on the sum of `edge_mask` on one device may be relied on, other than what follows from the above.
Results may differ from a plain program's by a relative error of at most 0.0003.
Values sent between devices are 32-bit elements; how exact they have to be, the bound alone decides.
No kernel may reach another device: no remote copies, remote signals or barrier semaphores. Data moves between devices by JAX's collectives and lax.ppermute only.
A program may use at most 64 MiB of HBM per device.

v0:
```python
import functools
import math

import jax
import jax.numpy as jnp
import numpy as np
from jax import lax
from jax.experimental import pallas as pl
from jax.experimental.pallas import tpu as pltpu
from jax.sharding import PartitionSpec as P


FULL_TURN = 2.0 * math.pi
SMEARING = 0.01
RADIAL_REACH = 3.0
SOFTEN = 0.01
F32 = jnp.float32
BF16 = jnp.bfloat16
EXTRA = 8
NN = (((1,), (0,)), ((), ()))
NT = (((1,), (1,)), ((), ()))


def series(function):
    nodes = 0.125 + 0.125 * np.cos(np.pi * (np.arange(64) + 0.5) / 64)
    fit = np.polynomial.chebyshev.Chebyshev.fit(nodes, function(np.sqrt(nodes)), 8, domain=[0, 0.25])
    return [float(c) for c in fit.convert(kind=np.polynomial.Polynomial).coef]


COSINE = series(lambda r: np.cos(2 * np.pi * r))
SINE = series(lambda r: np.sin(2 * np.pi * r) / r)


def horner(coefficients, z):
    total = jnp.full_like(z, coefficients[-1])
    for c in coefficients[-2::-1]:
        total = total * z + c
    return total


def cos_sin(turns):
    r = turns - jnp.floor(turns + 0.5)
    z = r * r
    return horner(COSINE, z), horner(SINE, z) * r


def dot(a, b, dims=NN):
    return lax.dot_general(a, b, dims, preferred_element_type=F32)


def split(x):
    high = x.astype(BF16)
    return high, (x - high.astype(F32)).astype(BF16)


def dot3(a, b):
    a_high, a_low = a
    b_high, b_low = b
    return dot(a_high, b_high) + dot(a_low, b_high) + dot(a_high, b_low)


def quotient(x, n):
    return jnp.floor((x + 0.5) * (1.0 / n))


def iota(shape, dim):
    return lax.broadcasted_iota(jnp.int32, shape, dim)


def component(block, atoms, channels, which):
    row, lane = divmod(which * atoms, channels)
    return block[atoms + row : atoms + row + 1, lane : lane + atoms]


def mode_columns(vectors, picks):
    rows, modes = picks.shape[0], vectors.shape[1]
    chosen = (iota((rows, modes), 1).astype(F32) == picks).astype(BF16)
    padded = jnp.concatenate([vectors, jnp.zeros((5, modes), F32)], axis=0).astype(BF16)
    triples = dot(chosen, padded, NT)
    return [triples[:, n : n + 1] for n in range(3)]


def pack_kernel(sizes, features_ref, offsets_ref, species_ref, out_ref):
    atoms, channels = sizes[:2]
    out_ref[:atoms] = features_ref[0, 0]
    out_ref[atoms:] = jnp.zeros((EXTRA, channels), F32)
    for which in range(4):
        row, lane = divmod(which * atoms, channels)
        source = offsets_ref[0, which] if which < 3 else species_ref[0].astype(F32)
        out_ref[atoms + row : atoms + row + 1, lane : lane + atoms] = source


def structure_kernel(sizes, *refs):
    atoms, channels, span0, span1, group, share = sizes
    blocks, vectors_ref, outs = refs[:span1], refs[span1], refs[span1 + 1 :]
    pieces, (cos_ref, sin_ref) = outs[:span0], outs[span0:]
    lateral = lax.axis_index("gx").astype(F32)
    transverse = lax.axis_index("gy").astype(F32)
    count = span0 * share
    number = iota((count, 1), 0).astype(F32)
    turn = quotient(number, share)
    owner = lateral + turn
    owner = owner - span0 * quotient(owner, span0)
    picks = owner * group + transverse * share + (number - turn * share)
    n0, n1, n2 = mode_columns(vectors_ref[...].astype(F32), picks)
    whole0 = n0 * lateral
    whole0 = (whole0 - span0 * quotient(whole0, span0)) * (1.0 / span0)
    n0 = n0 * (1.0 / span0)
    scaled1 = n1 * (1.0 / span1)
    for back in range(span1):
        packed = blocks[back]
        whole1 = n1 * (transverse - back)
        whole1 = (whole1 - span1 * quotient(whole1, span1)) * (1.0 / span1)
        u = [component(packed, atoms, channels, n) for n in range(3)]
        turns = whole0 + whole1 + n0 * u[0] + scaled1 * u[1] + n2 * u[2]
        cosine, sine = cos_sin(turns)
        cos_ref[:, back * atoms : (back + 1) * atoms] = cosine
        sin_ref[:, back * atoms : (back + 1) * atoms] = sine
    features = split(jnp.concatenate([block[:atoms] for block in blocks], axis=0))
    cosines = dot3(split(cos_ref[...]), features)
    sines = dot3(split(sin_ref[...]), features)
    for turn in range(span0):
        pieces[turn][:share] = cosines[turn * share : (turn + 1) * share]
        pieces[turn][share:] = sines[turn * share : (turn + 1) * share]


def pair_kernel(before_ref, after_ref, out_ref):
    out_ref[0] = before_ref[...]
    out_ref[1] = after_ref[...]


def table_kernel(sizes, cos_ref, sin_ref, high_ref, low_ref):
    atoms, _, span0, span1, _, share = sizes
    count = span0 * share
    for ref, lane in ((cos_ref, 0), (sin_ref, count)):
        for block in range(span1):
            rows = slice(block * atoms, (block + 1) * atoms)
            high, low = split(jnp.transpose(ref[:, rows]))
            high_ref[rows, lane : lane + count] = high
            low_ref[rows, lane : lane + count] = low


def filter_kernel(sizes, *refs):
    _, _, span0, span1, group, share = sizes
    pieces, (weight_ref, vectors_ref, out_ref) = refs[:span0], refs[span0:]
    total = pieces[0][...]
    for piece in pieces[1:]:
        total = total + piece[...]
    lateral = lax.axis_index("gx").astype(F32)
    transverse = lax.axis_index("gy").astype(F32)
    rows = max(share, 8)
    picks = lateral * group + transverse * share + iota((rows, 1), 0).astype(F32)
    n0, n1, n2 = mode_columns(vectors_ref[...].astype(F32), picks)
    waves = (FULL_TURN * n0 / span0, FULL_TURN * n1 / span1, FULL_TURN * n2)
    damp = jnp.exp(-SMEARING * sum(w * w for w in waves))[:share]
    mixed = dot3(split(total), split(weight_ref[0]))
    out_ref[:share] = damp * mixed[:share]
    out_ref[share:] = damp * mixed[share:]


def project_kernel(sizes, scale, *refs):
    atoms, _, span0, span1, _, share = sizes
    pieces, (high_ref, low_ref), outs = refs[:span0], refs[span0 : span0 + 2], refs[span0 + 2 :]
    filtered = split(
        jnp.concatenate(
            [piece[:share] for piece in pieces] + [piece[share:] for piece in pieces], axis=0
        )
        * scale
    )
    everything = dot3((high_ref[...], low_ref[...]), filtered)
    for back in range(span1):
        outs[back][...] = everything[back * atoms : (back + 1) * atoms]


def edge_kernel(
    sizes,
    own_refs,
    before_ref,
    after_ref,
    left_ref,
    right_ref,
    listed_ref,
    mask_ref,
    value_ref,
    radial_ref,
    embed_ref,
    mixing_ref,
    out_ref,
    feature_scratch,
    place_scratch,
    hot_scratch,
):
    atoms, channels, span0, span1, slots, basis_count, _, lanes = sizes
    lateral = lax.axis_index("gx").astype(F32)
    transverse = lax.axis_index("gy").astype(F32)
    low_lane = iota((lanes, atoms), 0)
    own_rows = None
    table = (
        (left_ref.at[0], before_ref, right_ref.at[0]),
        own_refs,
        (left_ref.at[1], after_ref, right_ref.at[1]),
    )
    for r, row_refs in enumerate(table):
        for d, packed in enumerate(row_refs):
            at = (r * 3 + d) * atoms
            feature_scratch[at : at + atoms] = packed[:atoms]
            place = jnp.where(
                low_lane - basis_count == component(packed, atoms, channels, 3).astype(jnp.int32),
                1.0,
                0.0,
            )
            if r == 1 and d == 1:
                own_rows = place
            for n, shift in enumerate((r - 1.0, d - 1.0, 0.0)):
                u = component(packed, atoms, channels, n)
                if r == 1 and d == 1:
                    own_rows = jnp.where(low_lane == n, u, own_rows)
                rest = u + shift
                for piece in range(3):
                    part = rest.astype(BF16).astype(F32)
                    place = jnp.where(low_lane == n + 4 * piece, part, place)
                    rest = rest - part
            place_scratch[:, at : at + atoms] = place.astype(BF16)

    own = jnp.transpose(own_rows)
    lane = iota((atoms, lanes), 1)
    own_place = jnp.where(lane < 3, own, 0.0)
    first = split(jnp.concatenate([radial_ref[...], embed_ref[...]], axis=0))
    own_kind = jnp.where(lane >= basis_count, own, 0.0).astype(BF16)
    own_before = dot(own_kind, first[0]) + dot(own_kind, first[1])

    listed = listed_ref[...].astype(F32)
    source = quotient(listed, atoms)
    source0 = quotient(source, span1)
    shift0 = source0 - lateral + 1.0
    shift0 = shift0 - span0 * quotient(shift0, span0)
    shift1 = source - source0 * span1 - transverse + 1.0
    shift1 = shift1 - span1 * quotient(shift1, span1)
    row = (shift0 * 3.0 + shift1) * atoms + (listed - source * atoms)
    row = jnp.transpose(jnp.where(mask_ref[...] != 0, row, -1.0)).astype(jnp.int32)
    table_rows = 9 * atoms
    for slot in range(slots):
        hot = iota((atoms, table_rows), 1) == row[:, slot : slot + 1]
        hot_scratch[slot * atoms : (slot + 1) * atoms] = jnp.where(hot, 1.0, 0.0).astype(BF16)

    values = split(dot3(split(feature_scratch[...]), split(value_ref[...])))
    mixing = split(mixing_ref[...])
    centres = lane.astype(F32) * (RADIAL_REACH / (basis_count - 1))
    spread = 2.0 * RADIAL_REACH / (basis_count - 1)
    chunk = slots // 2
    total = jnp.zeros((atoms, channels), F32)
    for start in range(0, slots, chunk):
        rows = chunk * atoms
        hot = hot_scratch[start * atoms : start * atoms + rows]
        near_values = dot(hot, values[0]) + dot(hot, values[1])
        place = dot(hot, place_scratch[...], NT)
        gap = place + pltpu.roll(place, lanes - 4, 1) + pltpu.roll(place, lanes - 8, 1)
        gap = gap.reshape(chunk, atoms, lanes) - own_place[None]
        gap = jnp.where((lane < 3)[None], gap, 0.0)
        distance = jnp.sqrt(jnp.sum(gap * gap, axis=2, keepdims=True) + SOFTEN)
        scaled = (distance - centres[None]) * (1.0 / spread)
        inner = jnp.where(
            (lane < basis_count)[None],
            jnp.exp(-scaled * scaled),
            place.reshape(chunk, atoms, lanes),
        ).reshape(rows, lanes)
        before = dot3(split(inner), first).reshape(chunk, atoms, channels) + own_before[None]
        hidden = (before / (1.0 + jnp.exp(-before))).reshape(rows, channels)
        filters = dot3(split(hidden), mixing)
        total = total + jnp.sum((filters * near_values).reshape(chunk, atoms, channels), axis=0)
    out_ref[...] = total * (1.0 / math.sqrt(slots))


def call(kernel, out_shape, operands, flops, scratch=(), room=8):
    moved = sum(x.size * 4 for x in operands)
    return pl.pallas_call(
        kernel,
        out_shape=out_shape,
        scratch_shapes=list(scratch),
        compiler_params=pltpu.CompilerParams(vmem_limit_bytes=room * 2**20),
        cost_estimate=pl.CostEstimate(flops=flops, bytes_accessed=moved, transcendentals=0),
    )(*operands)


def shift(x, axis, by):
    count = lax.axis_size(axis)
    return lax.ppermute(x, axis, [(i, (i + by) % count) for i in range(count)])


def shards(
    features,
    offsets,
    species,
    neighbours,
    edge_mask,
    wavevectors,
    value_weight,
    radial_weight,
    species_embed,
    mixing_weight,
    group_filter,
):
    span0 = lax.axis_size("gx")
    span1 = lax.axis_size("gy")
    atoms, channels = features.shape[2:]
    slots = neighbours.shape[3]
    modes = wavevectors.shape[1]
    basis_count, kinds = radial_weight.shape[0], species_embed.shape[0]
    group = modes // span0
    share = group // span1
    sizes = (atoms, channels, span0, span1, group, share)
    count = span0 * share

    packed = call(
        functools.partial(pack_kernel, sizes),
        jax.ShapeDtypeStruct((atoms + EXTRA, channels), F32),
        (features, jnp.transpose(offsets, (0, 2, 1, 3)), species),
        10**6,
    )
    column = [packed] + [shift(packed, "gy", k) for k in range(1, span1)]
    from_before = shift(packed, "gx", 1)
    from_after = shift(packed, "gx", -1)

    piece = jax.ShapeDtypeStruct((2 * share, channels), F32)
    wide = jax.ShapeDtypeStruct((count, span1 * atoms), F32)
    *pieces, cosines, sines = call(
        functools.partial(structure_kernel, sizes),
        [piece] * span0 + [wide] * 2,
        (*column, wavevectors),
        12 * count * span1 * atoms * channels,
    )
    received = [pieces[0]] + [shift(pieces[k], "gx", k) for k in range(1, span0)]
    pair = call(
        pair_kernel, jax.ShapeDtypeStruct((2, *packed.shape), F32), (from_before, from_after), 10**6
    )
    from_left = shift(pair, "gy", 1)
    from_right = shift(pair, "gy", -1)

    table = jax.ShapeDtypeStruct((span1 * atoms, 2 * count), BF16)
    high, low = call(functools.partial(table_kernel, sizes), [table] * 2, (cosines, sines), 10**8)

    filtered = call(
        functools.partial(filter_kernel, sizes),
        piece,
        (*received, group_filter, wavevectors),
        12 * share * channels * channels,
    )
    gathered = [filtered] + [shift(filtered, "gx", -k) for k in range(1, span0)]

    lanes = -(-(basis_count + kinds) // 128) * 128
    edge_sizes = (atoms, channels, span0, span1, slots, basis_count, kinds, lanes)
    nearby = call(
        lambda left, here, right, *refs: edge_kernel(edge_sizes, (left, here, right), *refs),
        jax.ShapeDtypeStruct((atoms, channels), F32),
        (
            column[1],
            column[0],
            column[-1],
            from_before,
            from_after,
            from_left,
            from_right,
            jnp.transpose(neighbours[0, 0]),
            jnp.transpose(edge_mask[0, 0]),
            value_weight,
            radial_weight,
            species_embed,
            mixing_weight,
        ),
        4 * 10**9,
        (
            pltpu.VMEM((9 * atoms, channels), F32),
            pltpu.VMEM((lanes, 9 * atoms), BF16),
            pltpu.VMEM((slots * atoms, 9 * atoms), BF16),
        ),
        24,
    )

    block = jax.ShapeDtypeStruct((atoms, channels), F32)
    scale = 1.0 / math.sqrt(atoms * span0 * span1 * modes)
    distant = call(
        functools.partial(project_kernel, sizes, scale),
        [block] * span1,
        (*gathered, high, low),
        12 * count * span1 * atoms * channels,
    )
    total = nearby + distant[0]
    for k in range(1, span1):
        total = total + shift(distant[k], "gy", -k)
    return total[None, None]


def solution(mesh):
    placed = (
        P("gx", "gy", None, None),
        P("gx", "gy", None, None),
        P("gx", "gy", None),
        P("gx", "gy", None, None),
        P("gx", "gy", None, None),
        P(),
        P(),
        P(),
        P(),
        P(),
        P("gx", None, None),
    )
    return jax.shard_map(
        shards, mesh=mesh, in_specs=placed, out_specs=P("gx", "gy", None, None), check_vma=False
    )
```

profile of v0, /device:TPU:0, one launch (start us, length us, event | category | flops | bytes accessed | tf_op | source)
XLA Modules:
  0.0 55.1 jit_solution(3289991578322371357)
XLA Ops:
  0.7 0.9 %copy-done.1 = f32[1,1,128,256]{3,2,1,0:T(8,128)S(1)} copy-done((f32[1,1,128,256]{3,2,1,0:T(8,128)S(1)}, f32[1,1,128,256]{3,2,1,0:T(8,128)}, u32[]{:S(2)}) %copy-start.1) | copy-done | bytes 131096
  2.3 4.6 %collective-permute-start.3 = (f32[136,256]{1,0:T(8,128)S(1)}, f32[136,256]{1,0:T(8,128)S(1)}, u32[]{:S(2)}, u32[]{:S(2)}) collective-permute-start(f32[136,256]{1,0:T(8,128)S(1)} %shard_map.109.here.refs_0_), channel_id=1, source_target_pairs={{0,28},{4,0},{8,4},{12,8},{16,12},{20,16},{24,20},{28,24},{1,29},{... | collective-permute-start | bytes 417800 | tf_op jit(solution)/shard_map/ppermute | solution.py:287
  6.8 1.5 %collective-permute-start.6 = (f32[136,256]{1,0:T(8,128)S(1)}, f32[136,256]{1,0:T(8,128)S(1)}, u32[]{:S(2)}, u32[]{:S(2)}) collective-permute-start(f32[136,256]{1,0:T(8,128)S(1)} %shard_map.109.here.refs_0_), channel_id=1, source_target_pairs={{0,2},{1,3},{2,0},{3,1},{4,6},{5,7},{6,4},{7,5},{8,10},{9,11},{10,... | collective-permute-start | bytes 417800 | tf_op jit(solution)/shard_map/ppermute | solution.py:287
  8.4 1.4 %collective-permute-start.1 = (f32[136,256]{1,0:T(8,128)S(1)}, f32[136,256]{1,0:T(8,128)S(1)}, u32[]{:S(2)}, u32[]{:S(2)}) collective-permute-start(f32[136,256]{1,0:T(8,128)S(1)} %shard_map.109.here.refs_0_), channel_id=1, source_target_pairs={{0,3},{1,0},{2,1},{3,2},{4,7},{5,4},{6,5},{7,6},{8,11},{9,8},{10,9... | collective-permute-start | bytes 417800 | tf_op jit(solution)/shard_map/ppermute | solution.py:287
  10.4 2.7 %collective-permute-done.2.before_ref.refs_0_ = f32[136,256]{1,0:T(8,128)S(1)} collective-permute-done((f32[136,256]{1,0:T(8,128)S(1)}, f32[136,256]{1,0:T(8,128)S(1)}, u32[]{:S(2)}, u32[]{:S(2)}) %collective-permute-start.2) | collective-permute-done | bytes 139296 | tf_op jit(solution)/shard_map/ppermute | solution.py:287
  13.2 2.5 %collective-permute-start.5 = (f32[2,136,256]{2,1,0:T(8,128)S(1)}, f32[2,136,256]{2,1,0:T(8,128)S(1)}, u32[]{:S(2)}, u32[]{:S(2)}) collective-permute-start(f32[2,136,256]{2,1,0:T(8,128)S(1)} %shard_map.110), channel_id=1, source_target_pairs={{0,3},{1,0},{2,1},{3,2},{4,7},{5,4},{6,5},{7,6},{8,11},{9,8},{10,9... | collective-permute-start | bytes 835592 | tf_op jit(solution)/shard_map/ppermute | solution.py:287
  15.7 2.2 %collective-permute-done.left.refs_1_ = f32[136,256]{1,0:T(8,128)S(1)} collective-permute-done((f32[136,256]{1,0:T(8,128)S(1)}, f32[136,256]{1,0:T(8,128)S(1)}, u32[]{:S(2)}, u32[]{:S(2)}) %collective-permute-start) | collective-permute-done | bytes 139296 | tf_op jit(solution)/shard_map/ppermute | solution.py:287
  17.8 1.0 %shard_map.112 = (f32[32,256]{1,0:T(8,128)S(1)}, f32[32,256]{1,0:T(8,128)S(1)}, f32[32,256]{1,0:T(8,128)S(1)}, f32[32,256]{1,0:T(8,128)S(1)}, f32[32,256]{1,0:T(...) custom-call(f32[136,256]{1,0:T(8,128)S(1)} %shard_map.109.here.refs_, ...), custom_call_target="tpu_custom_call" | custom-call | flops 201326592 | bytes 563200 | tf_op jit(solution)/shard_map/pallas_call | solution.py:276
  19.0 1.0 %collective-permute-start.9 = (f32[32,256]{1,0:T(8,128)S(1)}, f32[32,256]{1,0:T(8,128)S(1)}, u32[]{:S(2)}, u32[]{:S(2)}) collective-permute-start(f32[32,256]{1,0:T(8,128)S(1)} %get-tuple-element.24), channel_id=1, source_target_pairs={{0,12},{4,16},{8,20},{12,24},{16,28},{20,0},{24,4},{28,8},{1,13},{... | collective-permute-start | bytes 98312 | tf_op jit(solution)/shard_map/ppermute | solution.py:287
  20.0 4.1 %collective-permute-done.7.refs_1_ = f32[32,256]{1,0:T(8,128)S(1)} collective-permute-done((f32[32,256]{1,0:T(8,128)S(1)}, f32[32,256]{1,0:T(8,128)S(1)}, u32[]{:S(2)}, u32[]{:S(2)}) %collective-permute-start.7) | collective-permute-done | bytes 32800 | tf_op jit(solution)/shard_map/ppermute | solution.py:287
  24.1 1.1 %collective-permute-done.8.refs_2_ = f32[32,256]{1,0:T(8,128)S(1)} collective-permute-done((f32[32,256]{1,0:T(8,128)S(1)}, f32[32,256]{1,0:T(8,128)S(1)}, u32[]{:S(2)}, u32[]{:S(2)}) %collective-permute-start.8) | collective-permute-done | bytes 32800 | tf_op jit(solution)/shard_map/ppermute | solution.py:287
  25.8 1.2 %collective-permute-start.12 = (f32[32,256]{1,0:T(8,128)S(1)}, f32[32,256]{1,0:T(8,128)S(1)}, u32[]{:S(2)}, u32[]{:S(2)}) collective-permute-start(f32[32,256]{1,0:T(8,128)S(1)} %get-tuple-element.27), channel_id=1, source_target_pairs={{0,24},{4,28},{8,0},{12,4},{16,8},{20,12},{24,16},{28,20},{1,25},{... | collective-permute-start | bytes 98312 | tf_op jit(solution)/shard_map/ppermute | solution.py:287
  27.1 1.9 %collective-permute-done.10.refs_4_ = f32[32,256]{1,0:T(8,128)S(1)} collective-permute-done((f32[32,256]{1,0:T(8,128)S(1)}, f32[32,256]{1,0:T(8,128)S(1)}, u32[]{:S(2)}, u32[]{:S(2)}) %collective-permute-start.10) | collective-permute-done | bytes 32800 | tf_op jit(solution)/shard_map/ppermute | solution.py:287
  29.0 0.9 %collective-permute-done.12.refs_6_ = f32[32,256]{1,0:T(8,128)S(1)} collective-permute-done((f32[32,256]{1,0:T(8,128)S(1)}, f32[32,256]{1,0:T(8,128)S(1)}, u32[]{:S(2)}, u32[]{:S(2)}) %collective-permute-start.12) | collective-permute-done | bytes 32800 | tf_op jit(solution)/shard_map/ppermute | solution.py:287
  30.9 1.1 %collective-permute-start.20 = (f32[32,256]{1,0:T(8,128)S(1)}, f32[32,256]{1,0:T(8,128)S(1)}, u32[]{:S(2)}, u32[]{:S(2)}) collective-permute-start(f32[32,256]{1,0:T(8,128)S(1)} %shard_map.113.refs_0_), channel_id=1, source_target_pairs={{0,4},{4,8},{8,12},{12,16},{16,20},{20,24},{24,28},{28,0},{1,5},{5... | collective-permute-start | bytes 98312 | tf_op jit(solution)/shard_map/ppermute | solution.py:287
  32.0 1.7 %collective-permute-start.18 = (f32[32,256]{1,0:T(8,128)S(1)}, f32[32,256]{1,0:T(8,128)S(1)}, u32[]{:S(2)}, u32[]{:S(2)}) collective-permute-start(f32[32,256]{1,0:T(8,128)S(1)} %shard_map.113.refs_0_), channel_id=1, source_target_pairs={{0,12},{4,16},{8,20},{12,24},{16,28},{20,0},{24,4},{28,8},{1,13},{... | collective-permute-start | bytes 98312 | tf_op jit(solution)/shard_map/ppermute | solution.py:287
  33.6 2.4 %collective-permute-done.20.refs_7_ = f32[32,256]{1,0:T(8,128)S(1)} collective-permute-done((f32[32,256]{1,0:T(8,128)S(1)}, f32[32,256]{1,0:T(8,128)S(1)}, u32[]{:S(2)}, u32[]{:S(2)}) %collective-permute-start.20) | collective-permute-done | bytes 32800 | tf_op jit(solution)/shard_map/ppermute | solution.py:287
  36.0 1.6 %collective-permute-done.19.refs_6_ = f32[32,256]{1,0:T(8,128)S(1)} collective-permute-done((f32[32,256]{1,0:T(8,128)S(1)}, f32[32,256]{1,0:T(8,128)S(1)}, u32[]{:S(2)}, u32[]{:S(2)}) %collective-permute-start.19) | collective-permute-done | bytes 32800 | tf_op jit(solution)/shard_map/ppermute | solution.py:287
  37.8 2.2 %collective-permute-start.15 = (f32[32,256]{1,0:T(8,128)S(1)}, f32[32,256]{1,0:T(8,128)S(1)}, u32[]{:S(2)}, u32[]{:S(2)}) collective-permute-start(f32[32,256]{1,0:T(8,128)S(1)} %shard_map.113.refs_0_), channel_id=1, source_target_pairs={{0,24},{4,28},{8,0},{12,4},{16,8},{20,12},{24,16},{28,20},{1,25},{... | collective-permute-start | bytes 98312 | tf_op jit(solution)/shard_map/ppermute | solution.py:287
  40.0 1.2 %collective-permute-done.17.refs_4_ = f32[32,256]{1,0:T(8,128)S(1)} collective-permute-done((f32[32,256]{1,0:T(8,128)S(1)}, f32[32,256]{1,0:T(8,128)S(1)}, u32[]{:S(2)}, u32[]{:S(2)}) %collective-permute-start.17) | collective-permute-done | bytes 32800 | tf_op jit(solution)/shard_map/ppermute | solution.py:287
  43.2 2.4 %collective-permute-start.21 = (f32[128,256]{1,0:T(8,128)S(1)}, f32[128,256]{1,0:T(8,128)S(1)}, u32[]{:S(2)}, u32[]{:S(2)}) collective-permute-start(f32[128,256]{1,0:T(8,128)S(1)} %get-tuple-element.34), channel_id=1, source_target_pairs={{0,3},{1,0},{2,1},{3,2},{4,7},{5,4},{6,5},{7,6},{8,11},{9,8},{10,9... | collective-permute-start | bytes 393224 | tf_op jit(solution)/shard_map/ppermute | solution.py:287
  46.9 5.6 %shard_map.111 = f32[128,256]{1,0:T(8,128)S(1)} custom-call(f32[136,256]{1,0:T(8,128)S(1)} %collective-permute-done.left.refs_1_, f32[136,256]{1,0:T(8,128)S(1)} %shard_map.109.here.refs_0_, f32[136,256]{1,0:T(8,128)S(1)} %collective-permute-done.1.right.refs_3_, f32[136,256]{1,0:T(8,128)S(1)} %collective-permute-done.2.before_ref.refs_0_, ...), custom_call_target="tpu_custom_call" | custom-call | flops 4000000000 | bytes 1916928 | tf_op jit(solution)/shard_map/pallas_call | solution.py:276
  52.5 1.8 %collective-permute-done.22 = f32[128,256]{1,0:T(8,128)S(1)} collective-permute-done((f32[128,256]{1,0:T(8,128)S(1)}, f32[128,256]{1,0:T(8,128)S(1)}, u32[]{:S(2)}, u32[]{:S(2)}) %collective-permute-start.22) | collective-permute-done | bytes 131104 | tf_op jit(solution)/shard_map/ppermute | solution.py:287
  54.4 0.7 %add_bitcast_fusion = f32[1,1,128,256]{3,2,1,0:T(8,128)} fusion(f32[128,256]{1,0:T(8,128)S(1)} %collective-permute-done.23, f32[128,256]{1,0:T(8,128)S(1)} %collective-permute-done.22, f32[128,256]{1,0:T(8,128)S(1)} %collective-permute-done.21, f32[128,256]{1,0:T(8,128)S(1)} %shard_map.111, f32[128,256]{1,0:T(8,128)S(1)} %get-tuple-element.33), kind=kLoop, calls=%fused_computation | loop fusion | flops 131072 | bytes 786432 | tf_op jit(solution)/shard_map/broadcast_in_dim | solution.py:390
  (54 shorter events, 7.0 us)
Async XLA Ops:
  2.3 8.1 %collective-permute-start.3 = (f32[136,256]{1,0:T(8,128)S(1)}, f32[136,256]{1,0:T(8,128)S(1)}, u32[]{:S(2)}, u32[]{:S(2)}) collective-permute-start(f32[136,256]{1,0:T(8,128)S(1)} %shard_map.109.here.refs_0_), channel_id=1, source_target_pairs={{0,28},{4,0},{8,4},{12,8},{16,12},{20,16},{24,20},{28,24},{1,29},{... | collective-permute-start | bytes 417800 | tf_op jit(solution)/shard_map/ppermute | solution.py:287
  6.8 6.3 %collective-permute-start.2 = (f32[136,256]{1,0:T(8,128)S(1)}, f32[136,256]{1,0:T(8,128)S(1)}, u32[]{:S(2)}, u32[]{:S(2)}) collective-permute-start(f32[136,256]{1,0:T(8,128)S(1)} %shard_map.109.here.refs_0_), channel_id=1, source_target_pairs={{0,4},{4,8},{8,12},{12,16},{16,20},{20,24},{24,28},{28,0},{1,5},{5... | collective-permute-start | bytes 417800 | tf_op jit(solution)/shard_map/ppermute | solution.py:287
  6.8 8.8 %collective-permute-start.6 = (f32[136,256]{1,0:T(8,128)S(1)}, f32[136,256]{1,0:T(8,128)S(1)}, u32[]{:S(2)}, u32[]{:S(2)}) collective-permute-start(f32[136,256]{1,0:T(8,128)S(1)} %shard_map.109.here.refs_0_), channel_id=1, source_target_pairs={{0,2},{1,3},{2,0},{3,1},{4,6},{5,7},{6,4},{7,5},{8,10},{9,11},{10,... | collective-permute-start | bytes 417800 | tf_op jit(solution)/shard_map/ppermute | solution.py:287
  8.4 7.3 %collective-permute-start.1 = (f32[136,256]{1,0:T(8,128)S(1)}, f32[136,256]{1,0:T(8,128)S(1)}, u32[]{:S(2)}, u32[]{:S(2)}) collective-permute-start(f32[136,256]{1,0:T(8,128)S(1)} %shard_map.109.here.refs_0_), channel_id=1, source_target_pairs={{0,3},{1,0},{2,1},{3,2},{4,7},{5,4},{6,5},{7,6},{8,11},{9,8},{10,9... | collective-permute-start | bytes 417800 | tf_op jit(solution)/shard_map/ppermute | solution.py:287
  9.8 8.0 %collective-permute-start = (f32[136,256]{1,0:T(8,128)S(1)}, f32[136,256]{1,0:T(8,128)S(1)}, u32[]{:S(2)}, u32[]{:S(2)}) collective-permute-start(f32[136,256]{1,0:T(8,128)S(1)} %shard_map.109.here.refs_0_), channel_id=1, source_target_pairs={{0,1},{1,2},{2,3},{3,0},{4,5},{5,6},{6,7},{7,4},{8,9},{9,10},{10,1... | collective-permute-start | bytes 417800 | tf_op jit(solution)/shard_map/ppermute | solution.py:287
  13.2 33.7 %collective-permute-start.5 = (f32[2,136,256]{2,1,0:T(8,128)S(1)}, f32[2,136,256]{2,1,0:T(8,128)S(1)}, u32[]{:S(2)}, u32[]{:S(2)}) collective-permute-start(f32[2,136,256]{2,1,0:T(8,128)S(1)} %shard_map.110), channel_id=1, source_target_pairs={{0,3},{1,0},{2,1},{3,2},{4,7},{5,4},{6,5},{7,6},{8,11},{9,8},{10,9... | collective-permute-start | bytes 835592 | tf_op jit(solution)/shard_map/ppermute | solution.py:287
  15.7 31.2 %collective-permute-start.4 = (f32[2,136,256]{2,1,0:T(8,128)S(1)}, f32[2,136,256]{2,1,0:T(8,128)S(1)}, u32[]{:S(2)}, u32[]{:S(2)}) collective-permute-start(f32[2,136,256]{2,1,0:T(8,128)S(1)} %shard_map.110), channel_id=1, source_target_pairs={{0,1},{1,2},{2,3},{3,0},{4,5},{5,6},{6,7},{7,4},{8,9},{9,10},{10,1... | collective-permute-start | bytes 835592 | tf_op jit(solution)/shard_map/ppermute | solution.py:287
  18.9 5.2 %collective-permute-start.7 = (f32[32,256]{1,0:T(8,128)S(1)}, f32[32,256]{1,0:T(8,128)S(1)}, u32[]{:S(2)}, u32[]{:S(2)}) collective-permute-start(f32[32,256]{1,0:T(8,128)S(1)} %get-tuple-element.22), channel_id=1, source_target_pairs={{0,4},{4,8},{8,12},{12,16},{16,20},{20,24},{24,28},{28,0},{1,5},{5... | collective-permute-start | bytes 98312 | tf_op jit(solution)/shard_map/ppermute | solution.py:287
  18.9 6.2 %collective-permute-start.8 = (f32[32,256]{1,0:T(8,128)S(1)}, f32[32,256]{1,0:T(8,128)S(1)}, u32[]{:S(2)}, u32[]{:S(2)}) collective-permute-start(f32[32,256]{1,0:T(8,128)S(1)} %get-tuple-element.23), channel_id=1, source_target_pairs={{0,8},{4,12},{8,16},{12,20},{16,24},{20,28},{24,0},{28,4},{1,9},{5... | collective-permute-start | bytes 98312 | tf_op jit(solution)/shard_map/ppermute | solution.py:287
  19.0 6.8 %collective-permute-start.9 = (f32[32,256]{1,0:T(8,128)S(1)}, f32[32,256]{1,0:T(8,128)S(1)}, u32[]{:S(2)}, u32[]{:S(2)}) collective-permute-start(f32[32,256]{1,0:T(8,128)S(1)} %get-tuple-element.24), channel_id=1, source_target_pairs={{0,12},{4,16},{8,20},{12,24},{16,28},{20,0},{24,4},{28,8},{1,13},{... | collective-permute-start | bytes 98312 | tf_op jit(solution)/shard_map/ppermute | solution.py:287
  24.1 4.9 %collective-permute-start.10 = (f32[32,256]{1,0:T(8,128)S(1)}, f32[32,256]{1,0:T(8,128)S(1)}, u32[]{:S(2)}, u32[]{:S(2)}) collective-permute-start(f32[32,256]{1,0:T(8,128)S(1)} %get-tuple-element.25), channel_id=1, source_target_pairs={{0,16},{4,20},{8,24},{12,28},{16,0},{20,4},{24,8},{28,12},{1,17},{... | collective-permute-start | bytes 98312 | tf_op jit(solution)/shard_map/ppermute | solution.py:287
  25.2 3.8 %collective-permute-start.11 = (f32[32,256]{1,0:T(8,128)S(1)}, f32[32,256]{1,0:T(8,128)S(1)}, u32[]{:S(2)}, u32[]{:S(2)}) collective-permute-start(f32[32,256]{1,0:T(8,128)S(1)} %get-tuple-element.26), channel_id=1, source_target_pairs={{0,20},{4,24},{8,28},{12,0},{16,4},{20,8},{24,12},{28,16},{1,21},{... | collective-permute-start | bytes 98312 | tf_op jit(solution)/shard_map/ppermute | solution.py:287
  25.8 4.1 %collective-permute-start.12 = (f32[32,256]{1,0:T(8,128)S(1)}, f32[32,256]{1,0:T(8,128)S(1)}, u32[]{:S(2)}, u32[]{:S(2)}) collective-permute-start(f32[32,256]{1,0:T(8,128)S(1)} %get-tuple-element.27), channel_id=1, source_target_pairs={{0,24},{4,28},{8,0},{12,4},{16,8},{20,12},{24,16},{28,20},{1,25},{... | collective-permute-start | bytes 98312 | tf_op jit(solution)/shard_map/ppermute | solution.py:287
  29.0 1.6 %collective-permute-start.13 = (f32[32,256]{1,0:T(8,128)S(1)}, f32[32,256]{1,0:T(8,128)S(1)}, u32[]{:S(2)}, u32[]{:S(2)}) collective-permute-start(f32[32,256]{1,0:T(8,128)S(1)} %get-tuple-element.28), channel_id=1, source_target_pairs={{0,28},{4,0},{8,4},{12,8},{16,12},{20,16},{24,20},{28,24},{1,29},{... | collective-permute-start | bytes 98312 | tf_op jit(solution)/shard_map/ppermute | solution.py:287
  30.9 5.2 %collective-permute-start.20 = (f32[32,256]{1,0:T(8,128)S(1)}, f32[32,256]{1,0:T(8,128)S(1)}, u32[]{:S(2)}, u32[]{:S(2)}) collective-permute-start(f32[32,256]{1,0:T(8,128)S(1)} %shard_map.113.refs_0_), channel_id=1, source_target_pairs={{0,4},{4,8},{8,12},{12,16},{16,20},{20,24},{24,28},{28,0},{1,5},{5... | collective-permute-start | bytes 98312 | tf_op jit(solution)/shard_map/ppermute | solution.py:287
  31.9 5.7 %collective-permute-start.19 = (f32[32,256]{1,0:T(8,128)S(1)}, f32[32,256]{1,0:T(8,128)S(1)}, u32[]{:S(2)}, u32[]{:S(2)}) collective-permute-start(f32[32,256]{1,0:T(8,128)S(1)} %shard_map.113.refs_0_), channel_id=1, source_target_pairs={{0,8},{4,12},{8,16},{12,20},{16,24},{20,28},{24,0},{28,4},{1,9},{5... | collective-permute-start | bytes 98312 | tf_op jit(solution)/shard_map/ppermute | solution.py:287
  32.0 5.8 %collective-permute-start.18 = (f32[32,256]{1,0:T(8,128)S(1)}, f32[32,256]{1,0:T(8,128)S(1)}, u32[]{:S(2)}, u32[]{:S(2)}) collective-permute-start(f32[32,256]{1,0:T(8,128)S(1)} %shard_map.113.refs_0_), channel_id=1, source_target_pairs={{0,12},{4,16},{8,20},{12,24},{16,28},{20,0},{24,4},{28,8},{1,13},{... | collective-permute-start | bytes 98312 | tf_op jit(solution)/shard_map/ppermute | solution.py:287
  36.0 5.2 %collective-permute-start.17 = (f32[32,256]{1,0:T(8,128)S(1)}, f32[32,256]{1,0:T(8,128)S(1)}, u32[]{:S(2)}, u32[]{:S(2)}) collective-permute-start(f32[32,256]{1,0:T(8,128)S(1)} %shard_map.113.refs_0_), channel_id=1, source_target_pairs={{0,16},{4,20},{8,24},{12,28},{16,0},{20,4},{24,8},{28,12},{1,17},{... | collective-permute-start | bytes 98312 | tf_op jit(solution)/shard_map/ppermute | solution.py:287
  37.7 4.2 %collective-permute-start.16 = (f32[32,256]{1,0:T(8,128)S(1)}, f32[32,256]{1,0:T(8,128)S(1)}, u32[]{:S(2)}, u32[]{:S(2)}) collective-permute-start(f32[32,256]{1,0:T(8,128)S(1)} %shard_map.113.refs_0_), channel_id=1, source_target_pairs={{0,20},{4,24},{8,28},{12,0},{16,4},{20,8},{24,12},{28,16},{1,21},{... | collective-permute-start | bytes 98312 | tf_op jit(solution)/shard_map/ppermute | solution.py:287
  37.8 4.5 %collective-permute-start.15 = (f32[32,256]{1,0:T(8,128)S(1)}, f32[32,256]{1,0:T(8,128)S(1)}, u32[]{:S(2)}, u32[]{:S(2)}) collective-permute-start(f32[32,256]{1,0:T(8,128)S(1)} %shard_map.113.refs_0_), channel_id=1, source_target_pairs={{0,24},{4,28},{8,0},{12,4},{16,8},{20,12},{24,16},{28,20},{1,25},{... | collective-permute-start | bytes 98312 | tf_op jit(solution)/shard_map/ppermute | solution.py:287
  41.2 1.6 %collective-permute-start.14 = (f32[32,256]{1,0:T(8,128)S(1)}, f32[32,256]{1,0:T(8,128)S(1)}, u32[]{:S(2)}, u32[]{:S(2)}) collective-permute-start(f32[32,256]{1,0:T(8,128)S(1)} %shard_map.113.refs_0_), channel_id=1, source_target_pairs={{0,28},{4,0},{8,4},{12,8},{16,12},{20,16},{24,20},{28,24},{1,29},{... | collective-permute-start | bytes 98312 | tf_op jit(solution)/shard_map/ppermute | solution.py:287
  43.2 9.3 %collective-permute-start.21 = (f32[128,256]{1,0:T(8,128)S(1)}, f32[128,256]{1,0:T(8,128)S(1)}, u32[]{:S(2)}, u32[]{:S(2)}) collective-permute-start(f32[128,256]{1,0:T(8,128)S(1)} %get-tuple-element.34), channel_id=1, source_target_pairs={{0,3},{1,0},{2,1},{3,2},{4,7},{5,4},{6,5},{7,6},{8,11},{9,8},{10,9... | collective-permute-start | bytes 393224 | tf_op jit(solution)/shard_map/ppermute | solution.py:287
  45.7 8.7 %collective-permute-start.22 = (f32[128,256]{1,0:T(8,128)S(1)}, f32[128,256]{1,0:T(8,128)S(1)}, u32[]{:S(2)}, u32[]{:S(2)}) collective-permute-start(f32[128,256]{1,0:T(8,128)S(1)} %get-tuple-element.35), channel_id=1, source_target_pairs={{0,2},{1,3},{2,0},{3,1},{4,6},{5,7},{6,4},{7,5},{8,10},{9,11},{10,... | collective-permute-start | bytes 393224 | tf_op jit(solution)/shard_map/ppermute | solution.py:287
  46.3 8.1 %collective-permute-start.23 = (f32[128,256]{1,0:T(8,128)S(1)}, f32[128,256]{1,0:T(8,128)S(1)}, u32[]{:S(2)}, u32[]{:S(2)}) collective-permute-start(f32[128,256]{1,0:T(8,128)S(1)} %get-tuple-element.36), channel_id=1, source_target_pairs={{0,1},{1,2},{2,3},{3,0},{4,5},{5,6},{6,7},{7,4},{8,9},{9,10},{10,1... | collective-permute-start | bytes 393224 | tf_op jit(solution)/shard_map/ppermute | solution.py:287
  (11 other events, 58.8 us)
where the time goes:
time: 55.3 us; the launch traced here: 55.1 us
  waiting for transfers between devices  22.7 us (41%)
  starting transfers between devices  21.7 us (39%)
  Pallas kernels  7.55 us (14%)
  local copies, waits for them, and re-layouts  2.28 us (4%)
  other arithmetic  0.71 us (1%)
    ppermute x24, waiting for transfers between devices, shift(): return lax.ppermute(x, axis, [(i, (i + by) % count) for i in range(count)])  22.7 us
    ppermute x24, starting transfers between devices, shift(): return lax.ppermute(x, axis, [(i, (i + by) % count) for i in range(count)])  21.7 us
    pallas_call x7, Pallas kernels, call(): pl.pallas_call(kernel, out_shape=out_shape, scratch_shapes=list(scratch),...  7.55 us
    unnamed x22, local copies, waits for them, and re-layouts  2.28 us
  transfers between devices with their start and end apart: 24, of which 15 were waited for; matrix products, arithmetic and copies ran while one was open for 0% of the time, Pallas kernels for 14%

commit v1 on v0

v1 whole, which is shorter than its diff:
```python
import functools
import math

import jax
import jax.numpy as jnp
import numpy as np
from jax import lax
from jax.experimental import pallas as pl
from jax.experimental.pallas import tpu as pltpu
from jax.sharding import PartitionSpec as P


FULL_TURN = 2.0 * math.pi
SMEARING = 0.01
RADIAL_REACH = 3.0
SOFTEN = 0.01
VERTICAL = 2
F32 = jnp.float32
BF16 = jnp.bfloat16
EXTRA = 8
NN = (((1,), (0,)), ((), ()))
NT = (((1,), (1,)), ((), ()))


def series(function):
    nodes = 0.125 + 0.125 * np.cos(np.pi * (np.arange(64) + 0.5) / 64)
    fit = np.polynomial.chebyshev.Chebyshev.fit(nodes, function(np.sqrt(nodes)), 8, domain=[0, 0.25])
    return [float(c) for c in fit.convert(kind=np.polynomial.Polynomial).coef]


COSINE = series(lambda r: np.cos(2 * np.pi * r))
SINE = series(lambda r: np.sin(2 * np.pi * r) / r)


def horner(coefficients, z):
    total = jnp.full_like(z, coefficients[-1])
    for c in coefficients[-2::-1]:
        total = total * z + c
    return total


def cos_sin(turns):
    r = turns - jnp.floor(turns + 0.5)
    z = r * r
    return horner(COSINE, z), horner(SINE, z) * r


def dot(a, b, dims=NN):
    return lax.dot_general(a, b, dims, preferred_element_type=F32)


def split(x):
    high = x.astype(BF16)
    return high, (x - high.astype(F32)).astype(BF16)


def dot3(a, b):
    a_high, a_low = a
    b_high, b_low = b
    return dot(a_high, b_high) + dot(a_low, b_high) + dot(a_high, b_low)


def quotient(x, n):
    return jnp.floor((x + 0.5) * (1.0 / n))


def iota(shape, dim):
    return lax.broadcasted_iota(jnp.int32, shape, dim)


def component(block, atoms, channels, which):
    row, lane = divmod(which * atoms, channels)
    return block[atoms + row : atoms + row + 1, lane : lane + atoms]


def mode_columns(vectors, picks):
    rows, modes = picks.shape[0], vectors.shape[1]
    chosen = (iota((rows, modes), 1).astype(F32) == picks).astype(BF16)
    padded = jnp.concatenate([vectors, jnp.zeros((5, modes), F32)], axis=0).astype(BF16)
    triples = dot(chosen, padded, NT)
    return [triples[:, n : n + 1] for n in range(3)]


def distinct_triples(span0, span1):
    kept = {}
    for n0 in range(-(span0 // 2), span0 - span0 // 2):
        for n1 in range(-(span1 // 2), span1 - span1 // 2):
            for n2 in range(-VERTICAL, VERTICAL + 1):
                if (-n0, -n1, -n2) not in kept:
                    kept[(n0, n1, n2)] = None
    return list(kept)


def key_of(n0, n1, n2):
    return jnp.abs(n0 + 128.0 * n1 + 16384.0 * n2)


def rows_of(basis_ref, vectors_ref, rows, parity):
    if basis_ref is None:
        picks = parity.astype(F32) * rows + iota((rows, 1), 0).astype(F32)
        return mode_columns(vectors_ref[...].astype(F32), picks)
    triples = basis_ref[parity]
    return [triples[:, n : n + 1] for n in range(3)]


def phases(sizes, triples, lateral, transverse, packed):
    atoms, channels, span0, span1 = sizes[:4]
    n0, n1, n2 = triples
    whole0 = n0 * lateral
    whole0 = (whole0 - span0 * quotient(whole0, span0)) * (1.0 / span0)
    whole1 = n1 * transverse
    whole1 = (whole1 - span1 * quotient(whole1, span1)) * (1.0 / span1)
    u = [component(packed, atoms, channels, n) for n in range(3)]
    turns = whole0 + whole1 + n0 * (1.0 / span0) * u[0] + n1 * (1.0 / span1) * u[1] + n2 * u[2]
    return cos_sin(turns)


def place():
    lateral, transverse = lax.axis_index("gx"), lax.axis_index("gy")
    parity = lax.rem(lateral, 2)
    return lateral.astype(F32), transverse.astype(F32), parity


def pack_kernel(
    sizes, features_ref, offsets_ref, species_ref, weight_ref, out_ref, rows_ref, *scratch
):
    atoms, channels, _, span1 = sizes[:4]
    offsets_scratch, species_scratch, sems = scratch
    width = channels // span1
    start = pl.multiple_of(lax.axis_index("gy") * width, math.gcd(width, 8))
    copies = [
        pltpu.make_async_copy(offsets_ref.at[0], offsets_scratch, sems.at[0]),
        pltpu.make_async_copy(species_ref.at[0], species_scratch, sems.at[1]),
        pltpu.make_async_copy(features_ref.at[0, 0], out_ref.at[0:atoms], sems.at[2]),
        pltpu.make_async_copy(weight_ref.at[0, pl.ds(start, width)], rows_ref, sems.at[3]),
    ]
    for copy in copies:
        copy.start()
    out_ref[atoms:] = jnp.zeros((EXTRA, channels), F32)
    for copy in copies[:2]:
        copy.wait()
    for which in range(4):
        row, lane = divmod(which * atoms, channels)
        source = offsets_scratch[which] if which < 3 else species_scratch[...].astype(F32)
        out_ref[atoms + row : atoms + row + 1, lane : lane + atoms] = source
    for copy in copies[2:]:
        copy.wait()


def join_kernel(*refs):
    for n, ref in enumerate(refs[:-1]):
        refs[-1][n] = ref[...]


def structure_kernel(sizes, rows, canonical, *refs):
    atoms, channels, _, span1 = sizes[:4]
    own_ref, pair_ref, vectors_ref = refs[:3]
    basis_ref, out_ref = refs[3] if canonical else None, refs[-1]
    lateral, transverse, parity = place()
    triples = rows_of(basis_ref, vectors_ref, rows, parity)
    cosines, sines, features = [], [], []
    for ref, row in ((own_ref, lateral), (pair_ref, lateral + 1.0 - 2.0 * parity.astype(F32))):
        for back in range(span1):
            packed = ref.at[back]
            cosine, sine = phases(sizes, triples, row, transverse - back, packed)
            cosines.append(cosine)
            sines.append(sine)
            features.append(packed[:atoms])
    table = jnp.concatenate(
        [jnp.concatenate(cosines, axis=1), jnp.concatenate(sines, axis=1)], axis=0
    )
    sums = dot3(split(table), split(jnp.concatenate(features, axis=0)))
    width = channels // span1
    for half in range(2):
        part = sums[half * rows : (half + 1) * rows]
        mine = jnp.zeros((rows, width), F32)
        for c in range(span1):
            mine = jnp.where(transverse == c, part[:, c * width : (c + 1) * width], mine)
        out_ref[:, half * width : (half + 1) * width] = mine


def table_kernel(sizes, rows, canonical, *refs):
    atoms, _, _, span1 = sizes[:4]
    own_ref, vectors_ref = refs[:2]
    basis_ref, (high_ref, low_ref) = refs[2] if canonical else None, refs[-2:]
    lateral, transverse, parity = place()
    sides = [rows_of(basis_ref, vectors_ref, rows, p) for p in (parity, 1 - parity)]
    for back in range(span1):
        packed = own_ref.at[back]
        parts = []
        for triples in sides:
            parts.extend(phases(sizes, triples, lateral, transverse - back, packed))
        at = slice(back * atoms, (back + 1) * atoms)
        high_ref[at], low_ref[at] = split(jnp.transpose(jnp.concatenate(parts, axis=0)))


def filter_kernel(sizes, rows, canonical, *refs):
    _, channels, span0, span1, group = sizes
    pairs = span0 // 2
    sums, (own_ref, pair_ref, vectors_ref) = refs[:pairs], refs[pairs : pairs + 3]
    basis_ref, out_ref = refs[pairs + 3] if canonical else None, refs[-1]
    lateral, _, parity = place()
    triples = rows_of(basis_ref, vectors_ref, rows, parity)
    n0, n1, n2 = triples
    waves = (FULL_TURN * n0 / span0, FULL_TURN * n1 / span1, FULL_TURN * n2)
    damp = jnp.exp(-SMEARING * sum(w * w for w in waves))

    number = iota((1, span0), 1).astype(F32)
    side = quotient(number, pairs)
    turn = number - pairs * side
    kind = parity.astype(F32)
    row = quotient(lateral, 2) + turn
    row = 2.0 * (row - pairs * quotient(row, pairs)) + jnp.where(side == 0.0, kind, 1.0 - kind)
    modes = vectors_ref.shape[1]
    if canonical:
        listed = vectors_ref[...].astype(F32)
        keys = key_of(listed[0:1], listed[1:2], listed[2:3])
        matches = (key_of(n0, n1, n2) == keys).astype(BF16)
        groups = quotient(iota((modes, span0), 0).astype(F32), group)
        counts = dot(matches, (groups == row).astype(BF16))
    else:
        picks = kind * rows + iota((rows, 1), 0).astype(F32)
        counts = (quotient(picks, group) == row).astype(F32)
    weights = counts * damp

    total = sums[0][...]
    for ref in sums[1:]:
        total = total + ref[...]
    width = channels // span1
    mixed = jnp.zeros((2 * rows, channels), F32)
    for n in range(span0):
        scaled = total * weights[:, n : n + 1]
        both = jnp.concatenate([scaled[:, :width], scaled[:, width:]], axis=0)
        weight = own_ref[n] if n < pairs else pair_ref[n - pairs]
        mixed = mixed + dot3(split(both), split(weight))
    out_ref[...] = mixed


def project_kernel(sizes, scale, own_ref, pair_ref, high_ref, low_ref, *outs):
    atoms, span1 = sizes[0], sizes[3]
    filtered = split(jnp.concatenate([own_ref[...], pair_ref[...]], axis=0) * scale)
    everything = dot3((high_ref[...], low_ref[...]), filtered)
    for back in range(span1):
        outs[back][...] = everything[back * atoms : (back + 1) * atoms]


def edge_kernel(
    sizes,
    own_ref,
    pair_ref,
    across_ref,
    left_ref,
    right_ref,
    listed_ref,
    mask_ref,
    value_ref,
    radial_ref,
    embed_ref,
    mixing_ref,
    out_ref,
    feature_scratch,
    place_scratch,
    hot_scratch,
):
    atoms, channels, span0, span1, slots, basis_count, _, lanes = sizes
    lateral, transverse, parity = place()
    toward = 1.0 - 2.0 * parity.astype(F32)
    last = span1 - 1
    low_lane = iota((lanes, atoms), 0)
    own_rows = None
    table = (
        (left_ref, across_ref, right_ref),
        (own_ref.at[1], own_ref.at[0], own_ref.at[last]),
        (pair_ref.at[1], pair_ref.at[0], pair_ref.at[last]),
    )
    for r, row_refs in enumerate(table):
        for d, packed in enumerate(row_refs):
            at = (r * 3 + d) * atoms
            feature_scratch[at : at + atoms] = packed[:atoms]
            where = jnp.where(
                low_lane - basis_count == component(packed, atoms, channels, 3).astype(jnp.int32),
                1.0,
                0.0,
            )
            if r == 1 and d == 1:
                own_rows = where
            for n, shift in enumerate(((r - 1.0) * toward, d - 1.0, 0.0)):
                u = component(packed, atoms, channels, n)
                if r == 1 and d == 1:
                    own_rows = jnp.where(low_lane == n, u, own_rows)
                rest = u + shift
                for piece in range(3):
                    part = rest.astype(BF16).astype(F32)
                    where = jnp.where(low_lane == n + 4 * piece, part, where)
                    rest = rest - part
            place_scratch[:, at : at + atoms] = where.astype(BF16)

    own = jnp.transpose(own_rows)
    lane = iota((atoms, lanes), 1)
    own_place = jnp.where(lane < 3, own, 0.0)
    first = split(jnp.concatenate([radial_ref[...], embed_ref[...]], axis=0))
    own_kind = jnp.where(lane >= basis_count, own, 0.0).astype(BF16)
    own_before = dot(own_kind, first[0]) + dot(own_kind, first[1])

    listed = listed_ref[...].astype(F32)
    source = quotient(listed, atoms)
    source0 = quotient(source, span1)
    shift0 = source0 - lateral + 1.0
    shift0 = shift0 - span0 * quotient(shift0, span0)
    shift1 = source - source0 * span1 - transverse + 1.0
    shift1 = shift1 - span1 * quotient(shift1, span1)
    line = (shift0 - 1.0) * toward + 1.0
    row = (line * 3.0 + shift1) * atoms + (listed - source * atoms)
    row = jnp.transpose(jnp.where(mask_ref[...] != 0, row, -1.0)).astype(jnp.int32)
    table_rows = 9 * atoms
    for slot in range(slots):
        hot = iota((atoms, table_rows), 1) == row[:, slot : slot + 1]
        hot_scratch[slot * atoms : (slot + 1) * atoms] = jnp.where(hot, 1.0, 0.0).astype(BF16)

    values = split(dot3(split(feature_scratch[...]), split(value_ref[...])))
    mixing = split(mixing_ref[...])
    centres = lane.astype(F32) * (RADIAL_REACH / (basis_count - 1))
    spread = 2.0 * RADIAL_REACH / (basis_count - 1)
    chunk = slots // 2
    total = jnp.zeros((atoms, channels), F32)
    for start in range(0, slots, chunk):
        rows = chunk * atoms
        hot = hot_scratch[start * atoms : start * atoms + rows]
        near_values = dot(hot, values[0]) + dot(hot, values[1])
        where = dot(hot, place_scratch[...], NT)
        gap = where + pltpu.roll(where, lanes - 4, 1) + pltpu.roll(where, lanes - 8, 1)
        gap = gap.reshape(chunk, atoms, lanes) - own_place[None]
        gap = jnp.where((lane < 3)[None], gap, 0.0)
        distance = jnp.sqrt(jnp.sum(gap * gap, axis=2, keepdims=True) + SOFTEN)
        scaled = (distance - centres[None]) * (1.0 / spread)
        inner = jnp.where(
            (lane < basis_count)[None],
            jnp.exp(-scaled * scaled),
            where.reshape(chunk, atoms, lanes),
        ).reshape(rows, lanes)
        before = dot3(split(inner), first).reshape(chunk, atoms, channels) + own_before[None]
        hidden = (before / (1.0 + jnp.exp(-before))).reshape(rows, channels)
        filters = dot3(split(hidden), mixing)
        total = total + jnp.sum((filters * near_values).reshape(chunk, atoms, channels), axis=0)
    out_ref[...] = total * (1.0 / math.sqrt(slots))


def call(kernel, out_shape, operands, flops, scratch=(), room=24, specs=None):
    moved = sum(x.size * 4 for x in operands)
    if specs is None:
        specs = [pl.BlockSpec(memory_space=pltpu.VMEM)] * len(operands)
    return pl.pallas_call(
        kernel,
        out_shape=out_shape,
        in_specs=specs,
        scratch_shapes=list(scratch),
        compiler_params=pltpu.CompilerParams(vmem_limit_bytes=room * 2**20),
        cost_estimate=pl.CostEstimate(flops=flops, bytes_accessed=moved, transcendentals=0),
    )(*operands)


def shift(x, axis, by):
    count = lax.axis_size(axis)
    return lax.ppermute(x, axis, [(i, (i + by) % count) for i in range(count)])


def swap(x, first=0):
    count = lax.axis_size("gx")
    one = [((i + first) % count, (i + first + 1) % count) for i in range(0, count, 2)]
    return lax.ppermute(x, "gx", one + [(b, a) for a, b in one])


def shards(
    features,
    offsets,
    species,
    neighbours,
    edge_mask,
    wavevectors,
    value_weight,
    radial_weight,
    species_embed,
    mixing_weight,
    group_filter,
):
    span0 = lax.axis_size("gx")
    span1 = lax.axis_size("gy")
    atoms, channels = features.shape[2:]
    slots = neighbours.shape[3]
    modes = wavevectors.shape[1]
    basis_count, kinds = radial_weight.shape[0], species_embed.shape[0]
    sizes = (atoms, channels, span0, span1, modes // span0)
    pairs = span0 // 2
    width = channels // span1

    distinct = distinct_triples(span0, span1)
    canonical = len(distinct) < modes
    vectors = (wavevectors,)
    rows = modes // 2
    if canonical:
        rows = -(-len(distinct) // 16) * 8
        basis = np.full((2 * rows, 8), 99.0, np.float32)
        basis[: len(distinct), :3] = distinct
        vectors = (wavevectors, jnp.asarray(basis.reshape(2, rows, 8)))

    anywhere = pl.BlockSpec(memory_space=pltpu.HBM)
    packed_shape = (atoms + EXTRA, channels)
    packed, weights = call(
        functools.partial(pack_kernel, sizes),
        [
            jax.ShapeDtypeStruct(packed_shape, F32),
            jax.ShapeDtypeStruct((width, channels), F32),
        ],
        tuple(
            pltpu.with_memory_space_constraint(x, pltpu.HBM)
            for x in (features, jnp.transpose(offsets, (0, 2, 1, 3)), species, group_filter)
        ),
        10**6,
        (
            pltpu.VMEM((3, 1, atoms), F32),
            pltpu.VMEM((1, atoms), jnp.int32),
            pltpu.SemaphoreType.DMA((4,)),
        ),
        specs=[anywhere] * 4,
    )
    column = [packed] + [shift(packed, "gy", k) for k in range(1, span1)]
    across = swap(packed, first=1)
    weights = [weights] + [shift(weights, "gx", -2 * k) for k in range(1, pairs)]

    own = call(join_kernel, jax.ShapeDtypeStruct((span1, *packed_shape), F32), column, 10**6)
    pair = swap(own)
    total = call(
        functools.partial(structure_kernel, sizes, rows, canonical),
        jax.ShapeDtypeStruct((rows, 2 * width), F32),
        (own, pair, *vectors),
        24 * rows * span1 * atoms * channels,
    )
    totals = [total] + [shift(total, "gx", 2 * k) for k in range(1, pairs)]
    weights = call(join_kernel, jax.ShapeDtypeStruct((pairs, width, channels), F32), weights, 10**6)
    pair_weights = swap(weights)
    left = shift(across, "gy", 1)
    right = shift(across, "gy", -1)

    table = jax.ShapeDtypeStruct((span1 * atoms, 4 * rows), BF16)
    high, low = call(
        functools.partial(table_kernel, sizes, rows, canonical), [table] * 2, (own, *vectors), 10**8
    )
    filtered = call(
        functools.partial(filter_kernel, sizes, rows, canonical),
        jax.ShapeDtypeStruct((2 * rows, channels), F32),
        (*totals, weights, pair_weights, *vectors),
        12 * rows * span0 * width * channels,
    )
    pair_filtered = swap(filtered)

    lanes = -(-(basis_count + kinds) // 128) * 128
    edge_sizes = (atoms, channels, span0, span1, slots, basis_count, kinds, lanes)
    nearby = call(
        functools.partial(edge_kernel, edge_sizes),
        jax.ShapeDtypeStruct((atoms, channels), F32),
        (
            own,
            pair,
            across,
            left,
            right,
            jnp.transpose(neighbours[0, 0]),
            jnp.transpose(edge_mask[0, 0]),
            value_weight,
            radial_weight,
            species_embed,
            mixing_weight,
        ),
        4 * 10**9,
        (
            pltpu.VMEM((9 * atoms, channels), F32),
            pltpu.VMEM((lanes, 9 * atoms), BF16),
            pltpu.VMEM((slots * atoms, 9 * atoms), BF16),
        ),
        24,
    )

    block = jax.ShapeDtypeStruct((atoms, channels), F32)
    scale = 1.0 / math.sqrt(atoms * span0 * span1 * modes)
    distant = call(
        functools.partial(project_kernel, sizes, scale),
        [block] * span1,
        (filtered, pair_filtered, high, low),
        24 * rows * span1 * atoms * channels,
    )
    result = nearby + distant[0]
    for k in range(1, span1):
        result = result + shift(distant[k], "gy", -k)
    return result[None, None]


def solution(mesh):
    placed = (
        P("gx", "gy", None, None),
        P("gx", "gy", None, None),
        P("gx", "gy", None),
        P("gx", "gy", None, None),
        P("gx", "gy", None, None),
        P(),
        P(),
        P(),
        P(),
        P(),
        P("gx", None, None),
    )
    return jax.shard_map(
        shards, mesh=mesh, in_specs=placed, out_specs=P("gx", "gy", None, None), check_vma=False
    )
```

time: 55.3 us -> 46.5 us (0.84)
  waiting for transfers between devices: 22.7 us -> 12.5 us
  local copies, waits for them, and re-layouts: 2.28 us -> 0.04 us
  Pallas kernels: 7.55 us -> 9.72 us
  starting transfers between devices: 21.7 us -> 23.2 us
    ppermute x24 -> x14, waiting for transfers between devices: 22.7 us -> 11 us  [shift(): return lax.ppermute(x, axis, [(i, (i + by) % count) for i in range(count)])]
    unnamed x22 -> x16, local copies, waits for them, and re-layouts: 2.28 us -> 0.04 us
    ppermute x0 -> x4, starting transfers between devices: none -> 2.19 us  [swap(): return lax.ppermute(x, 'gx', one + [(b, a) for a, b in one])]
    pallas_call x7 -> x8, Pallas kernels: 7.55 us -> 9.72 us  [call(): pl.pallas_call(kernel, out_shape=out_shape, in_specs=specs, scratch_shape...]
    ppermute x0 -> x4, waiting for transfers between devices: none -> 1.48 us  [swap(): return lax.ppermute(x, 'gx', one + [(b, a) for a, b in one])]
    ppermute x24 -> x14, starting transfers between devices: 21.7 us -> 21 us  [shift(): return lax.ppermute(x, axis, [(i, (i + by) % count) for i in range(count)])]
  transfers between devices with their start and end apart: 24 -> 18, of which waited for: 15 -> 7; matrix products, arithmetic and copies ran while one was open for 0% -> 0% of each run, Pallas kernels for 14% -> 19%
where the time goes in v1:
time: 46.5 us; the launch traced here: 46.3 us
  starting transfers between devices  23.2 us (50%)
  waiting for transfers between devices  12.5 us (27%)
  Pallas kernels  9.72 us (21%)
  other arithmetic  0.7 us (2%)
    ppermute x14, starting transfers between devices, shift(): return lax.ppermute(x, axis, [(i, (i + by) % count) for i in range(count)])  21 us
    ppermute x14, waiting for transfers between devices, shift(): return lax.ppermute(x, axis, [(i, (i + by) % count) for i in range(count)])  11 us
    pallas_call x8, Pallas kernels, call(): pl.pallas_call(kernel, out_shape=out_shape, in_specs=specs, scratch_shape...  9.72 us
    ppermute x4, starting transfers between devices, swap(): return lax.ppermute(x, 'gx', one + [(b, a) for a, b in one])  2.19 us
    ppermute x4, waiting for transfers between devices, swap(): return lax.ppermute(x, 'gx', one + [(b, a) for a, b in one])  1.48 us
  transfers between devices with their start and end apart: 18, of which 7 were waited for; matrix products, arithmetic and copies ran while one was open for 0% of the time, Pallas kernels for 19%

profile of v1, /device:TPU:0, one launch (start us, length us, event | category | flops | bytes accessed | tf_op | source)
XLA Modules:
  0.0 46.3 jit_solution(11154566885583586327)
XLA Ops:
  0.0 1.0 %shard_map.118 = (f32[136,256]{1,0:T(8,128)S(1)}, f32[64,256]{1,0:T(8,128)S(1)}) custom-call(f32[1,1,128,256]{3,2,1,0:T(8,128)} %features_ref.1, f32[1,3,1,128]{3,2,1,0:T(1,128)} %bitcast.11, s32[1,1,128]{2,1,0:T(1,128)} %species_ref.1, f32[1,256,256]{2,1,0:T(8,128)} %weight_ref.1), custom_call_target="tpu_custom_call" | custom-call | flops 1000000 | bytes 395264 | tf_op jit(solution)/shard_map/pallas_call | solution.py:352
  1.0 3.0 %collective-permute-start = (f32[136,256]{1,0:T(8,128)S(1)}, f32[136,256]{1,0:T(8,128)S(1)}, u32[]{:S(2)}, u32[]{:S(2)}) collective-permute-start(f32[136,256]{1,0:T(8,128)S(1)} %get-tuple-element.13.refs_0_), channel_id=1, source_target_pairs={{0,1},{1,2},{2,3},{3,0},{4,5},{5,6},{6,7},{7,4},{8,9},{9,10},{10,1... | collective-permute-start | bytes 417800 | tf_op jit(solution)/shard_map/ppermute | solution.py:364
  4.0 1.5 %collective-permute-start.1 = (f32[136,256]{1,0:T(8,128)S(1)}, f32[136,256]{1,0:T(8,128)S(1)}, u32[]{:S(2)}, u32[]{:S(2)}) collective-permute-start(f32[136,256]{1,0:T(8,128)S(1)} %get-tuple-element.13.refs_0_), channel_id=1, source_target_pairs={{0,2},{1,3},{2,0},{3,1},{4,6},{5,7},{6,4},{7,5},{8,10},{9,11},{10,... | collective-permute-start | bytes 417800 | tf_op jit(solution)/shard_map/ppermute | solution.py:364
  5.5 1.4 %collective-permute-start.2 = (f32[136,256]{1,0:T(8,128)S(1)}, f32[136,256]{1,0:T(8,128)S(1)}, u32[]{:S(2)}, u32[]{:S(2)}) collective-permute-start(f32[136,256]{1,0:T(8,128)S(1)} %get-tuple-element.13.refs_0_), channel_id=1, source_target_pairs={{0,3},{1,0},{2,1},{3,2},{4,7},{5,4},{6,5},{7,6},{8,11},{9,8},{10,9... | collective-permute-start | bytes 417800 | tf_op jit(solution)/shard_map/ppermute | solution.py:364
  7.0 2.5 %collective-permute-done.refs_1_ = f32[136,256]{1,0:T(8,128)S(1)} collective-permute-done((f32[136,256]{1,0:T(8,128)S(1)}, f32[136,256]{1,0:T(8,128)S(1)}, u32[]{:S(2)}, u32[]{:S(2)}) %collective-permute-start) | collective-permute-done | bytes 139296 | tf_op jit(solution)/shard_map/ppermute | solution.py:364
  9.5 2.1 %collective-permute-done.1.refs_2_ = f32[136,256]{1,0:T(8,128)S(1)} collective-permute-done((f32[136,256]{1,0:T(8,128)S(1)}, f32[136,256]{1,0:T(8,128)S(1)}, u32[]{:S(2)}, u32[]{:S(2)}) %collective-permute-start.1) | collective-permute-done | bytes 139296 | tf_op jit(solution)/shard_map/ppermute | solution.py:364
  12.0 3.7 %collective-permute-start.10 = (f32[64,256]{1,0:T(8,128)S(1)}, f32[64,256]{1,0:T(8,128)S(1)}, u32[]{:S(2)}, u32[]{:S(2)}) collective-permute-start(f32[64,256]{1,0:T(8,128)S(1)} %get-tuple-element.14.refs_0_), channel_id=1, source_target_pairs={{0,24},{4,28},{8,0},{12,4},{16,8},{20,12},{24,16},{28,20},{1,25},{... | collective-permute-start | bytes 196616 | tf_op jit(solution)/shard_map/ppermute | solution.py:364
  15.7 1.0 %collective-permute-start.12 = (f32[64,256]{1,0:T(8,128)S(1)}, f32[64,256]{1,0:T(8,128)S(1)}, u32[]{:S(2)}, u32[]{:S(2)}) collective-permute-start(f32[64,256]{1,0:T(8,128)S(1)} %get-tuple-element.14.refs_0_), channel_id=1, source_target_pairs={{0,8},{4,12},{8,16},{12,20},{16,24},{20,28},{24,0},{28,4},{1,9},{5... | collective-permute-start | bytes 196616 | tf_op jit(solution)/shard_map/ppermute | solution.py:364
  16.7 1.5 %collective-permute-done.10.refs_1_ = f32[64,256]{1,0:T(8,128)S(1)} collective-permute-done((f32[64,256]{1,0:T(8,128)S(1)}, f32[64,256]{1,0:T(8,128)S(1)}, u32[]{:S(2)}, u32[]{:S(2)}) %collective-permute-start.10) | collective-permute-done | bytes 65568 | tf_op jit(solution)/shard_map/ppermute | solution.py:364
  18.2 4.5 %collective-permute-done.11.refs_2_ = f32[64,256]{1,0:T(8,128)S(1)} collective-permute-done((f32[64,256]{1,0:T(8,128)S(1)}, f32[64,256]{1,0:T(8,128)S(1)}, u32[]{:S(2)}, u32[]{:S(2)}) %collective-permute-start.11) | collective-permute-done | bytes 65568 | tf_op jit(solution)/shard_map/ppermute | solution.py:364
  22.8 2.0 %collective-permute-start.4 = (f32[136,256]{1,0:T(8,128)S(1)}, f32[136,256]{1,0:T(8,128)S(1)}, u32[]{:S(2)}, u32[]{:S(2)}) collective-permute-start(f32[136,256]{1,0:T(8,128)S(1)} %get-tuple-element.13.refs_0_), channel_id=1, source_target_pairs={{4,8},{12,16},{20,24},{28,0},{8,4},{16,12},{24,20},{0,28},{5,9},{1... | collective-permute-start | bytes 417800 | tf_op jit(solution)/shard_map/ppermute | solution.py:370
  24.8 1.1 %shard_map.121.refs_0_ = f32[56,128]{1,0:T(8,128)S(1)} custom-call(f32[4,136,256]{2,1,0:T(8,128)S(1)} %shard_map.119.own_ref.refs_0_, f32[4,136,256]{2,1,0:T(8,128)S(1)} %collective-permute-done.3.pair_ref.refs_1_, s32[3,512]{1,0:T(4,128)S(1)} %copy-done.1, f32[2,56,8]{2,1,0:T(8,128)S(1)} %copy-done), custom_call_target="tpu_custom_call" | custom-call | flops 176160768 | bytes 1123840 | tf_op jit(solution)/shard_map/pallas_call | solution.py:352
  26.1 1.8 %collective-permute-start.8 = (f32[56,128]{1,0:T(8,128)S(1)}, f32[56,128]{1,0:T(8,128)S(1)}, u32[]{:S(2)}, u32[]{:S(2)}) collective-permute-start(f32[56,128]{1,0:T(8,128)S(1)} %shard_map.121.refs_0_), channel_id=1, source_target_pairs={{0,16},{4,20},{8,24},{12,28},{16,0},{20,4},{24,8},{28,12},{1,17},{... | collective-permute-start | bytes 86024 | tf_op jit(solution)/shard_map/ppermute | solution.py:364
  27.8 1.9 %collective-permute-start.9 = (f32[56,128]{1,0:T(8,128)S(1)}, f32[56,128]{1,0:T(8,128)S(1)}, u32[]{:S(2)}, u32[]{:S(2)}) collective-permute-start(f32[56,128]{1,0:T(8,128)S(1)} %shard_map.121.refs_0_), channel_id=1, source_target_pairs={{0,24},{4,28},{8,0},{12,4},{16,8},{20,12},{24,16},{28,20},{1,25},{... | collective-permute-start | bytes 86024 | tf_op jit(solution)/shard_map/ppermute | solution.py:364
  29.8 0.9 %collective-permute-done.4.across_ref = f32[136,256]{1,0:T(8,128)S(1)} collective-permute-done((f32[136,256]{1,0:T(8,128)S(1)}, f32[136,256]{1,0:T(8,128)S(1)}, u32[]{:S(2)}, u32[]{:S(2)}) %collective-permute-start.4) | collective-permute-done | bytes 139296 | tf_op jit(solution)/shard_map/ppermute | solution.py:370
  30.6 1.7 %collective-permute-start.5 = (f32[136,256]{1,0:T(8,128)S(1)}, f32[136,256]{1,0:T(8,128)S(1)}, u32[]{:S(2)}, u32[]{:S(2)}) collective-permute-start(f32[136,256]{1,0:T(8,128)S(1)} %collective-permute-done.4.across_ref), channel_id=1, source_target_pairs={{0,1},{1,2},{2,3},{3,0},{4,5},{5,6},{6,7},{7,4},{8,9},{9,10},{10,1... | collective-permute-start | bytes 417800 | tf_op jit(solution)/shard_map/ppermute | solution.py:364
  32.4 1.2 %collective-permute-start.6 = (f32[136,256]{1,0:T(8,128)S(1)}, f32[136,256]{1,0:T(8,128)S(1)}, u32[]{:S(2)}, u32[]{:S(2)}) collective-permute-start(f32[136,256]{1,0:T(8,128)S(1)} %collective-permute-done.4.across_ref), channel_id=1, source_target_pairs={{0,3},{1,0},{2,1},{3,2},{4,7},{5,4},{6,5},{7,6},{8,11},{9,8},{10,9... | collective-permute-start | bytes 417800 | tf_op jit(solution)/shard_map/ppermute | solution.py:364
  33.6 0.9 %shard_map.123.own_ref = f32[112,256]{1,0:T(8,128)S(1)} custom-call(f32[56,128]{1,0:T(8,128)S(1)} %shard_map.121.refs_0_, f32[56,128]{1,0:T(8,128)S(1)} %collective-permute-done.7.refs_1_, f32[56,128]{1,0:T(8,128)S(1)} %collective-permute-done.8.refs_2_, f32[56,128]{1,0:T(8,128)S(1)} %collective-permute-done.9.refs_3_, ...), custom_call_target="tpu_custom_call" | custom-call | flops 88080384 | bytes 648704 | tf_op jit(solution)/shard_map/pallas_call | solution.py:352
  34.6 0.7 %shard_map.124 = (bf16[512,224]{1,0:T(8,128)(2,1)S(1)}, bf16[512,224]{1,0:T(8,128)(2,1)S(1)}) custom-call(f32[4,136,256]{2,1,0:T(8,128)S(1)} %shard_map.119.own_ref.refs_0_, s32[3,512]{1,0:T(4,128)S(1)} %copy-done.1, f32[2,56,8]{2,1,0:T(8,128)S(1)} %copy-done), custom_call_target="tpu_custom_call" | custom-call | flops 100000000 | bytes 566784 | tf_op jit(solution)/shard_map/pallas_call | solution.py:352
  36.3 0.8 %collective-permute-start.15 = (f32[128,256]{1,0:T(8,128)S(1)}, f32[128,256]{1,0:T(8,128)S(1)}, u32[]{:S(2)}, u32[]{:S(2)}) collective-permute-start(f32[128,256]{1,0:T(8,128)S(1)} %get-tuple-element.18), channel_id=1, source_target_pairs={{0,3},{1,0},{2,1},{3,2},{4,7},{5,4},{6,5},{7,6},{8,11},{9,8},{10,9... | collective-permute-start | bytes 393224 | tf_op jit(solution)/shard_map/ppermute | solution.py:364
  37.1 1.5 %collective-permute-start.16 = (f32[128,256]{1,0:T(8,128)S(1)}, f32[128,256]{1,0:T(8,128)S(1)}, u32[]{:S(2)}, u32[]{:S(2)}) collective-permute-start(f32[128,256]{1,0:T(8,128)S(1)} %get-tuple-element.19), channel_id=1, source_target_pairs={{0,2},{1,3},{2,0},{3,1},{4,6},{5,7},{6,4},{7,5},{8,10},{9,11},{10,... | collective-permute-start | bytes 393224 | tf_op jit(solution)/shard_map/ppermute | solution.py:364
  38.7 1.2 %collective-permute-start.17 = (f32[128,256]{1,0:T(8,128)S(1)}, f32[128,256]{1,0:T(8,128)S(1)}, u32[]{:S(2)}, u32[]{:S(2)}) collective-permute-start(f32[128,256]{1,0:T(8,128)S(1)} %get-tuple-element.20), channel_id=1, source_target_pairs={{0,1},{1,2},{2,3},{3,0},{4,5},{5,6},{6,7},{7,4},{8,9},{9,10},{10,1... | collective-permute-start | bytes 393224 | tf_op jit(solution)/shard_map/ppermute | solution.py:364
  39.9 5.6 %shard_map.120 = f32[128,256]{1,0:T(8,128)S(1)} custom-call(f32[4,136,256]{2,1,0:T(8,128)S(1)} %shard_map.119.own_ref.refs_0_, f32[4,136,256]{2,1,0:T(8,128)S(1)} %collective-permute-done.3.pair_ref.refs_1_, f32[136,256]{1,0:T(8,128)S(1)} %collective-permute-done.4.across_ref, f32[136,256]{1,0:T(8,128)S(1)} %collective-permute-done.5.left_ref, ...), custom_call_target="tpu_custom_call" | custom-call | flops 4000000000 | bytes 2195456 | tf_op jit(solution)/shard_map/pallas_call | solution.py:352
  45.6 0.7 %add_bitcast_fusion = f32[1,1,128,256]{3,2,1,0:T(8,128)} fusion(f32[128,256]{1,0:T(8,128)S(1)} %collective-permute-done.17, f32[128,256]{1,0:T(8,128)S(1)} %collective-permute-done.16, f32[128,256]{1,0:T(8,128)S(1)} %collective-permute-done.15, f32[128,256]{1,0:T(8,128)S(1)} %shard_map.120, f32[128,256]{1,0:T(8,128)S(1)} %get-tuple-element.17), kind=kLoop, calls=%fused_computation | loop fusion | flops 131072 | bytes 786432 | tf_op jit(solution)/shard_map/broadcast_in_dim | solution.py:494
  (37 shorter events, 1.8 us)
Async XLA Ops:
  1.0 8.5 %collective-permute-start = (f32[136,256]{1,0:T(8,128)S(1)}, f32[136,256]{1,0:T(8,128)S(1)}, u32[]{:S(2)}, u32[]{:S(2)}) collective-permute-start(f32[136,256]{1,0:T(8,128)S(1)} %get-tuple-element.13.refs_0_), channel_id=1, source_target_pairs={{0,1},{1,2},{2,3},{3,0},{4,5},{5,6},{6,7},{7,4},{8,9},{9,10},{10,1... | collective-permute-start | bytes 417800 | tf_op jit(solution)/shard_map/ppermute | solution.py:364
  4.0 7.6 %collective-permute-start.1 = (f32[136,256]{1,0:T(8,128)S(1)}, f32[136,256]{1,0:T(8,128)S(1)}, u32[]{:S(2)}, u32[]{:S(2)}) collective-permute-start(f32[136,256]{1,0:T(8,128)S(1)} %get-tuple-element.13.refs_0_), channel_id=1, source_target_pairs={{0,2},{1,3},{2,0},{3,1},{4,6},{5,7},{6,4},{7,5},{8,10},{9,11},{10,... | collective-permute-start | bytes 417800 | tf_op jit(solution)/shard_map/ppermute | solution.py:364
  5.5 6.3 %collective-permute-start.2 = (f32[136,256]{1,0:T(8,128)S(1)}, f32[136,256]{1,0:T(8,128)S(1)}, u32[]{:S(2)}, u32[]{:S(2)}) collective-permute-start(f32[136,256]{1,0:T(8,128)S(1)} %get-tuple-element.13.refs_0_), channel_id=1, source_target_pairs={{0,3},{1,0},{2,1},{3,2},{4,7},{5,4},{6,5},{7,6},{8,11},{9,8},{10,9... | collective-permute-start | bytes 417800 | tf_op jit(solution)/shard_map/ppermute | solution.py:364
  11.9 12.9 %collective-permute-start.3 = (f32[4,136,256]{2,1,0:T(8,128)S(1)}, f32[4,136,256]{2,1,0:T(8,128)S(1)}, u32[]{:S(2)}, u32[]{:S(2)}) collective-permute-start(f32[4,136,256]{2,1,0:T(8,128)S(1)} %shard_map.119.own_ref.refs_0_), channel_id=1, source_target_pairs={{0,4},{8,12},{16,20},{24,28},{4,0},{12,8},{20,16},{28,24},{1,5},{9... | collective-permute-start | bytes 1671176 | tf_op jit(solution)/shard_map/ppermute | solution.py:370
  12.0 12.8 %copy-start = (f32[2,56,8]{2,1,0:T(8,128)S(1)}, f32[2,56,8]{2,1,0:T(8,128)}, u32[]{:S(2)}) copy-start(f32[2,56,8]{2,1,0:T(8,128)} %constant.2.clone.refs_3_.refs_7_.refs_2_) | copy-start | bytes 10756
  12.0 12.8 %copy-start.1 = (s32[3,512]{1,0:T(4,128)S(1)}, s32[3,512]{1,0:T(4,128)}, u32[]{:S(2)}) copy-start(s32[3,512]{1,0:T(4,128)} %refs_1_.1) | copy-start | bytes 18436
  12.0 6.2 %collective-permute-start.10 = (f32[64,256]{1,0:T(8,128)S(1)}, f32[64,256]{1,0:T(8,128)S(1)}, u32[]{:S(2)}, u32[]{:S(2)}) collective-permute-start(f32[64,256]{1,0:T(8,128)S(1)} %get-tuple-element.14.refs_0_), channel_id=1, source_target_pairs={{0,24},{4,28},{8,0},{12,4},{16,8},{20,12},{24,16},{28,20},{1,25},{... | collective-permute-start | bytes 196616 | tf_op jit(solution)/shard_map/ppermute | solution.py:364
  15.7 7.1 %collective-permute-start.11 = (f32[64,256]{1,0:T(8,128)S(1)}, f32[64,256]{1,0:T(8,128)S(1)}, u32[]{:S(2)}, u32[]{:S(2)}) collective-permute-start(f32[64,256]{1,0:T(8,128)S(1)} %get-tuple-element.14.refs_0_), channel_id=1, source_target_pairs={{0,16},{4,20},{8,24},{12,28},{16,0},{20,4},{24,8},{28,12},{1,17},{... | collective-permute-start | bytes 196616 | tf_op jit(solution)/shard_map/ppermute | solution.py:364
  15.7 7.1 %collective-permute-start.12 = (f32[64,256]{1,0:T(8,128)S(1)}, f32[64,256]{1,0:T(8,128)S(1)}, u32[]{:S(2)}, u32[]{:S(2)}) collective-permute-start(f32[64,256]{1,0:T(8,128)S(1)} %get-tuple-element.14.refs_0_), channel_id=1, source_target_pairs={{0,8},{4,12},{8,16},{12,20},{16,24},{20,28},{24,0},{28,4},{1,9},{5... | collective-permute-start | bytes 196616 | tf_op jit(solution)/shard_map/ppermute | solution.py:364
  22.8 9.6 %collective-permute-start.13 = (f32[4,64,256]{2,1,0:T(8,128)S(1)}, f32[4,64,256]{2,1,0:T(8,128)S(1)}, u32[]{:S(2)}, u32[]{:S(2)}) collective-permute-start(f32[4,64,256]{2,1,0:T(8,128)S(1)} %shard_map.122.refs_4_), channel_id=1, source_target_pairs={{0,4},{8,12},{16,20},{24,28},{4,0},{12,8},{20,16},{28,24},{1,5},{9... | collective-permute-start | bytes 786440 | tf_op jit(solution)/shard_map/ppermute | solution.py:370
  22.8 7.8 %collective-permute-start.4 = (f32[136,256]{1,0:T(8,128)S(1)}, f32[136,256]{1,0:T(8,128)S(1)}, u32[]{:S(2)}, u32[]{:S(2)}) collective-permute-start(f32[136,256]{1,0:T(8,128)S(1)} %get-tuple-element.13.refs_0_), channel_id=1, source_target_pairs={{4,8},{12,16},{20,24},{28,0},{8,4},{16,12},{24,20},{0,28},{5,9},{1... | collective-permute-start | bytes 417800 | tf_op jit(solution)/shard_map/ppermute | solution.py:370
  25.9 7.7 %collective-permute-start.7 = (f32[56,128]{1,0:T(8,128)S(1)}, f32[56,128]{1,0:T(8,128)S(1)}, u32[]{:S(2)}, u32[]{:S(2)}) collective-permute-start(f32[56,128]{1,0:T(8,128)S(1)} %shard_map.121.refs_0_), channel_id=1, source_target_pairs={{0,8},{4,12},{8,16},{12,20},{16,24},{20,28},{24,0},{28,4},{1,9},{5... | collective-permute-start | bytes 86024 | tf_op jit(solution)/shard_map/ppermute | solution.py:364
  26.1 7.5 %collective-permute-start.8 = (f32[56,128]{1,0:T(8,128)S(1)}, f32[56,128]{1,0:T(8,128)S(1)}, u32[]{:S(2)}, u32[]{:S(2)}) collective-permute-start(f32[56,128]{1,0:T(8,128)S(1)} %shard_map.121.refs_0_), channel_id=1, source_target_pairs={{0,16},{4,20},{8,24},{12,28},{16,0},{20,4},{24,8},{28,12},{1,17},{... | collective-permute-start | bytes 86024 | tf_op jit(solution)/shard_map/ppermute | solution.py:364
  27.8 5.7 %collective-permute-start.9 = (f32[56,128]{1,0:T(8,128)S(1)}, f32[56,128]{1,0:T(8,128)S(1)}, u32[]{:S(2)}, u32[]{:S(2)}) collective-permute-start(f32[56,128]{1,0:T(8,128)S(1)} %shard_map.121.refs_0_), channel_id=1, source_target_pairs={{0,24},{4,28},{8,0},{12,4},{16,8},{20,12},{24,16},{28,20},{1,25},{... | collective-permute-start | bytes 86024 | tf_op jit(solution)/shard_map/ppermute | solution.py:364
  30.6 9.2 %collective-permute-start.5 = (f32[136,256]{1,0:T(8,128)S(1)}, f32[136,256]{1,0:T(8,128)S(1)}, u32[]{:S(2)}, u32[]{:S(2)}) collective-permute-start(f32[136,256]{1,0:T(8,128)S(1)} %collective-permute-done.4.across_ref), channel_id=1, source_target_pairs={{0,1},{1,2},{2,3},{3,0},{4,5},{5,6},{6,7},{7,4},{8,9},{9,10},{10,1... | collective-permute-start | bytes 417800 | tf_op jit(solution)/shard_map/ppermute | solution.py:364
  32.4 7.5 %collective-permute-start.6 = (f32[136,256]{1,0:T(8,128)S(1)}, f32[136,256]{1,0:T(8,128)S(1)}, u32[]{:S(2)}, u32[]{:S(2)}) collective-permute-start(f32[136,256]{1,0:T(8,128)S(1)} %collective-permute-done.4.across_ref), channel_id=1, source_target_pairs={{0,3},{1,0},{2,1},{3,2},{4,7},{5,4},{6,5},{7,6},{8,11},{9,8},{10,9... | collective-permute-start | bytes 417800 | tf_op jit(solution)/shard_map/ppermute | solution.py:364
  34.5 1.4 %collective-permute-start.14 = (f32[112,256]{1,0:T(8,128)S(1)}, f32[112,256]{1,0:T(8,128)S(1)}, u32[]{:S(2)}, u32[]{:S(2)}) collective-permute-start(f32[112,256]{1,0:T(8,128)S(1)} %shard_map.123.own_ref), channel_id=1, source_target_pairs={{0,4},{8,12},{16,20},{24,28},{4,0},{12,8},{20,16},{28,24},{1,5},{9... | collective-permute-start | bytes 344072 | tf_op jit(solution)/shard_map/ppermute | solution.py:370
  35.9 4.0 %copy-start.2 = (f32[256,256]{1,0:T(8,128)S(1)}, f32[256,256]{1,0:T(8,128)}, u32[]{:S(2)}) copy-start(f32[256,256]{1,0:T(8,128)} %value_ref.1) | copy-start | bytes 786436
  35.9 4.0 %copy-start.3 = (f32[256,256]{1,0:T(8,128)S(1)}, f32[256,256]{1,0:T(8,128)}, u32[]{:S(2)}) copy-start(f32[256,256]{1,0:T(8,128)} %mixing_ref.1) | copy-start | bytes 786436
  35.9 4.0 %copy-start.4 = (f32[64,256]{1,0:T(8,128)S(1)}, f32[64,256]{1,0:T(8,128)}, u32[]{:S(2)}) copy-start(f32[64,256]{1,0:T(8,128)} %radial_ref.1) | copy-start | bytes 196612
  35.9 4.0 %copy-start.5 = (f32[64,256]{1,0:T(8,128)S(1)}, f32[64,256]{1,0:T(8,128)}, u32[]{:S(2)}) copy-start(f32[64,256]{1,0:T(8,128)} %embed_ref.1) | copy-start | bytes 196612
  36.3 9.3 %collective-permute-start.15 = (f32[128,256]{1,0:T(8,128)S(1)}, f32[128,256]{1,0:T(8,128)S(1)}, u32[]{:S(2)}, u32[]{:S(2)}) collective-permute-start(f32[128,256]{1,0:T(8,128)S(1)} %get-tuple-element.18), channel_id=1, source_target_pairs={{0,3},{1,0},{2,1},{3,2},{4,7},{5,4},{6,5},{7,6},{8,11},{9,8},{10,9... | collective-permute-start | bytes 393224 | tf_op jit(solution)/shard_map/ppermute | solution.py:364
  37.1 8.4 %collective-permute-start.16 = (f32[128,256]{1,0:T(8,128)S(1)}, f32[128,256]{1,0:T(8,128)S(1)}, u32[]{:S(2)}, u32[]{:S(2)}) collective-permute-start(f32[128,256]{1,0:T(8,128)S(1)} %get-tuple-element.19), channel_id=1, source_target_pairs={{0,2},{1,3},{2,0},{3,1},{4,6},{5,7},{6,4},{7,5},{8,10},{9,11},{10,... | collective-permute-start | bytes 393224 | tf_op jit(solution)/shard_map/ppermute | solution.py:364
  38.7 6.9 %collective-permute-start.17 = (f32[128,256]{1,0:T(8,128)S(1)}, f32[128,256]{1,0:T(8,128)S(1)}, u32[]{:S(2)}, u32[]{:S(2)}) collective-permute-start(f32[128,256]{1,0:T(8,128)S(1)} %get-tuple-element.20), channel_id=1, source_target_pairs={{0,1},{1,2},{2,3},{3,0},{4,5},{5,6},{6,7},{7,4},{8,9},{9,10},{10,1... | collective-permute-start | bytes 393224 | tf_op jit(solution)/shard_map/ppermute | solution.py:364
  (2 other events, 7.2 us)

commit v2 on v1

--- a/solution.py
+++ b/solution.py
@@ -121,11 +121,11 @@
     return lateral.astype(F32), transverse.astype(F32), parity
 
 
-def pack_kernel(
-    sizes, features_ref, offsets_ref, species_ref, weight_ref, out_ref, rows_ref, *scratch
-):
+def pack_kernel(sizes, features_ref, offsets_ref, species_ref, weight_ref, *refs):
     atoms, channels, _, span1 = sizes[:4]
-    offsets_scratch, species_scratch, sems = scratch
+    *refs, offsets_scratch, species_scratch, sems = refs
+    tables = len(refs) // 2 - 1
+    sources, out_ref, rows_ref, copies_to = refs[:tables], refs[tables], refs[tables + 1], refs[tables + 2 :]
     width = channels // span1
     start = pl.multiple_of(lax.axis_index("gy") * width, math.gcd(width, 8))
     copies = [
@@ -134,6 +134,8 @@
         pltpu.make_async_copy(features_ref.at[0, 0], out_ref.at[0:atoms], sems.at[2]),
         pltpu.make_async_copy(weight_ref.at[0, pl.ds(start, width)], rows_ref, sems.at[3]),
     ]
+    for n, (source, target) in enumerate(zip(sources, copies_to)):
+        copies.append(pltpu.make_async_copy(source, target, sems.at[4 + n]))
     for copy in copies:
         copy.start()
     out_ref[atoms:] = jnp.zeros((EXTRA, channels), F32)
@@ -152,37 +154,45 @@
         refs[-1][n] = ref[...]
 
 
-def structure_kernel(sizes, rows, canonical, *refs):
+def column_kernel(*refs):
+    blocks, (own_ref, sides_ref) = refs[:-2], refs[-2:]
+    for n, ref in enumerate(blocks):
+        own_ref[n] = ref[...]
+    sides_ref[0] = blocks[1][...]
+    sides_ref[1] = blocks[-1][...]
+
+
+def structure_kernel(sizes, rows, canonical, paired, *refs):
     atoms, channels, _, span1 = sizes[:4]
-    own_ref, pair_ref, vectors_ref = refs[:3]
-    basis_ref, out_ref = refs[3] if canonical else None, refs[-1]
+    blocks_ref, vectors_ref = refs[:2]
+    basis_ref, out_ref = refs[2] if canonical else None, refs[-1]
     lateral, transverse, parity = place()
     triples = rows_of(basis_ref, vectors_ref, rows, parity)
-    cosines, sines, features = [], [], []
-    for ref, row in ((own_ref, lateral), (pair_ref, lateral + 1.0 - 2.0 * parity.astype(F32))):
-        for back in range(span1):
-            packed = ref.at[back]
-            cosine, sine = phases(sizes, triples, row, transverse - back, packed)
-            cosines.append(cosine)
-            sines.append(sine)
-            features.append(packed[:atoms])
+    row = lateral + 1.0 - 2.0 * parity.astype(F32) if paired else lateral
+    cosines, sines = [], []
+    for back in range(span1):
+        cosine, sine = phases(sizes, triples, row, transverse - back, blocks_ref.at[back])
+        cosines.append(cosine)
+        sines.append(sine)
     table = jnp.concatenate(
         [jnp.concatenate(cosines, axis=1), jnp.concatenate(sines, axis=1)], axis=0
     )
-    sums = dot3(split(table), split(jnp.concatenate(features, axis=0)))
+    features = jnp.concatenate([blocks_ref[back, :atoms] for back in range(span1)], axis=0)
+    sums = dot3(split(table), split(features))
     width = channels // span1
     for half in range(2):
         part = sums[half * rows : (half + 1) * rows]
         mine = jnp.zeros((rows, width), F32)
         for c in range(span1):
             mine = jnp.where(transverse == c, part[:, c * width : (c + 1) * width], mine)
-        out_ref[:, half * width : (half + 1) * width] = mine
+        at = slice(half * width, (half + 1) * width)
+        out_ref[:, at] = mine + refs[-2][:, at] if paired else mine
 
 
 def table_kernel(sizes, rows, canonical, *refs):
-    atoms, _, _, span1 = sizes[:4]
+    atoms, _, span0, span1, group = sizes
     own_ref, vectors_ref = refs[:2]
-    basis_ref, (high_ref, low_ref) = refs[2] if canonical else None, refs[-2:]
+    basis_ref, (high_ref, low_ref, weight_ref) = refs[2] if canonical else None, refs[-3:]
     lateral, transverse, parity = place()
     sides = [rows_of(basis_ref, vectors_ref, rows, p) for p in (parity, 1 - parity)]
     for back in range(span1):
@@ -193,18 +203,10 @@
         at = slice(back * atoms, (back + 1) * atoms)
         high_ref[at], low_ref[at] = split(jnp.transpose(jnp.concatenate(parts, axis=0)))
 
-
-def filter_kernel(sizes, rows, canonical, *refs):
-    _, channels, span0, span1, group = sizes
-    pairs = span0 // 2
-    sums, (own_ref, pair_ref, vectors_ref) = refs[:pairs], refs[pairs : pairs + 3]
-    basis_ref, out_ref = refs[pairs + 3] if canonical else None, refs[-1]
-    lateral, _, parity = place()
-    triples = rows_of(basis_ref, vectors_ref, rows, parity)
-    n0, n1, n2 = triples
+    n0, n1, n2 = sides[0]
     waves = (FULL_TURN * n0 / span0, FULL_TURN * n1 / span1, FULL_TURN * n2)
     damp = jnp.exp(-SMEARING * sum(w * w for w in waves))
-
+    pairs = span0 // 2
     number = iota((1, span0), 1).astype(F32)
     side = quotient(number, pairs)
     turn = number - pairs * side
@@ -221,18 +223,30 @@
     else:
         picks = kind * rows + iota((rows, 1), 0).astype(F32)
         counts = (quotient(picks, group) == row).astype(F32)
-    weights = counts * damp
-
+    weight_ref[...] = counts * damp
+
+
+def filter_kernel(sizes, *refs):
+    channels, span0, span1 = sizes[1:4]
+    pairs = span0 // 2
+    sums, (own_ref, pair_ref, weight_ref, out_ref) = refs[:pairs], refs[pairs:]
     total = sums[0][...]
     for ref in sums[1:]:
         total = total + ref[...]
     width = channels // span1
-    mixed = jnp.zeros((2 * rows, channels), F32)
-    for n in range(span0):
-        scaled = total * weights[:, n : n + 1]
-        both = jnp.concatenate([scaled[:, :width], scaled[:, width:]], axis=0)
-        weight = own_ref[n] if n < pairs else pair_ref[n - pairs]
-        mixed = mixed + dot3(split(both), split(weight))
+    weights = weight_ref[...]
+    mixed = None
+    for side, ref in enumerate((own_ref, pair_ref)):
+        at = range(side * pairs, (side + 1) * pairs)
+        both = jnp.concatenate(
+            [
+                jnp.concatenate([total[:, :width] * weights[:, n : n + 1] for n in at], axis=1),
+                jnp.concatenate([total[:, width:] * weights[:, n : n + 1] for n in at], axis=1),
+            ],
+            axis=0,
+        )
+        part = dot3(split(both), split(ref[...].reshape(pairs * width, channels)))
+        mixed = part if mixed is None else mixed + part
     out_ref[...] = mixed
 
 
@@ -244,15 +258,31 @@
         outs[back][...] = everything[back * atoms : (back + 1) * atoms]
 
 
+def hot_kernel(sizes, listed_ref, mask_ref, out_ref):
+    atoms, _, span0, span1, slots = sizes[:5]
+    lateral, transverse, parity = place()
+    listed = listed_ref[...].astype(F32)
+    source = quotient(listed, atoms)
+    source0 = quotient(source, span1)
+    shift0 = source0 - lateral + 1.0
+    shift0 = shift0 - span0 * quotient(shift0, span0)
+    shift1 = source - source0 * span1 - transverse + 1.0
+    shift1 = shift1 - span1 * quotient(shift1, span1)
+    line = (shift0 - 1.0) * (1.0 - 2.0 * parity.astype(F32)) + 1.0
+    row = (line * 3.0 + shift1) * atoms + (listed - source * atoms)
+    row = jnp.transpose(jnp.where(mask_ref[...] != 0, row, -1.0)).astype(jnp.int32)
+    for slot in range(slots):
+        hot = iota((atoms, 9 * atoms), 1) == row[:, slot : slot + 1]
+        out_ref[slot * atoms : (slot + 1) * atoms] = jnp.where(hot, 1.0, 0.0).astype(BF16)
+
+
 def edge_kernel(
     sizes,
     own_ref,
     pair_ref,
     across_ref,
-    left_ref,
-    right_ref,
-    listed_ref,
-    mask_ref,
+    sides_ref,
+    hot_ref,
     value_ref,
     radial_ref,
     embed_ref,
@@ -260,62 +290,51 @@
     out_ref,
     feature_scratch,
     place_scratch,
-    hot_scratch,
 ):
-    atoms, channels, span0, span1, slots, basis_count, _, lanes = sizes
-    lateral, transverse, parity = place()
+    atoms, channels, _, span1, slots, basis_count, kinds, lanes = sizes
+    parity = place()[2]
     toward = 1.0 - 2.0 * parity.astype(F32)
     last = span1 - 1
-    low_lane = iota((lanes, atoms), 0)
     own_rows = None
     table = (
-        (left_ref, across_ref, right_ref),
+        (sides_ref.at[0], across_ref, sides_ref.at[1]),
         (own_ref.at[1], own_ref.at[0], own_ref.at[last]),
         (pair_ref.at[1], pair_ref.at[0], pair_ref.at[last]),
     )
+    low = iota((16, atoms), 0)
+    kind_rows = iota((lanes - basis_count, atoms), 0)
     for r, row_refs in enumerate(table):
         for d, packed in enumerate(row_refs):
             at = (r * 3 + d) * atoms
             feature_scratch[at : at + atoms] = packed[:atoms]
-            where = jnp.where(
-                low_lane - basis_count == component(packed, atoms, channels, 3).astype(jnp.int32),
-                1.0,
-                0.0,
-            )
-            if r == 1 and d == 1:
-                own_rows = where
+            species = component(packed, atoms, channels, 3).astype(jnp.int32)
+            kind_hot = jnp.where(kind_rows == species, 1.0, 0.0)
+            positions = jnp.zeros((16, atoms), F32)
+            exact = positions
             for n, shift in enumerate(((r - 1.0) * toward, d - 1.0, 0.0)):
                 u = component(packed, atoms, channels, n)
-                if r == 1 and d == 1:
-                    own_rows = jnp.where(low_lane == n, u, own_rows)
+                exact = jnp.where(low == n, u, exact)
                 rest = u + shift
                 for piece in range(3):
                     part = rest.astype(BF16).astype(F32)
-                    where = jnp.where(low_lane == n + 4 * piece, part, where)
+                    positions = jnp.where(low == n + 4 * piece, part, positions)
                     rest = rest - part
+            gap = jnp.zeros((basis_count - 16, atoms), F32)
+            where = jnp.concatenate([positions, gap, kind_hot], axis=0)
             place_scratch[:, at : at + atoms] = where.astype(BF16)
+            if r == 1 and d == 1:
+                own_rows = jnp.concatenate([exact, gap, kind_hot], axis=0)
 
     own = jnp.transpose(own_rows)
     lane = iota((atoms, lanes), 1)
     own_place = jnp.where(lane < 3, own, 0.0)
-    first = split(jnp.concatenate([radial_ref[...], embed_ref[...]], axis=0))
+    missing = lanes - basis_count - kinds
+    first = [radial_ref[...], embed_ref[...]]
+    if missing:
+        first.append(jnp.zeros((missing, channels), F32))
+    first = split(jnp.concatenate(first, axis=0))
     own_kind = jnp.where(lane >= basis_count, own, 0.0).astype(BF16)
     own_before = dot(own_kind, first[0]) + dot(own_kind, first[1])
-
-    listed = listed_ref[...].astype(F32)
-    source = quotient(listed, atoms)
-    source0 = quotient(source, span1)
-    shift0 = source0 - lateral + 1.0
-    shift0 = shift0 - span0 * quotient(shift0, span0)
-    shift1 = source - source0 * span1 - transverse + 1.0
-    shift1 = shift1 - span1 * quotient(shift1, span1)
-    line = (shift0 - 1.0) * toward + 1.0
-    row = (line * 3.0 + shift1) * atoms + (listed - source * atoms)
-    row = jnp.transpose(jnp.where(mask_ref[...] != 0, row, -1.0)).astype(jnp.int32)
-    table_rows = 9 * atoms
-    for slot in range(slots):
-        hot = iota((atoms, table_rows), 1) == row[:, slot : slot + 1]
-        hot_scratch[slot * atoms : (slot + 1) * atoms] = jnp.where(hot, 1.0, 0.0).astype(BF16)
 
     values = split(dot3(split(feature_scratch[...]), split(value_ref[...])))
     mixing = split(mixing_ref[...])
@@ -325,7 +344,7 @@
     total = jnp.zeros((atoms, channels), F32)
     for start in range(0, slots, chunk):
         rows = chunk * atoms
-        hot = hot_scratch[start * atoms : start * atoms + rows]
+        hot = hot_ref[start * atoms : start * atoms + rows]
         near_values = dot(hot, values[0]) + dot(hot, values[1])
         where = dot(hot, place_scratch[...], NT)
         gap = where + pltpu.roll(where, lanes - 4, 1) + pltpu.roll(where, lanes - 8, 1)
@@ -405,56 +424,80 @@
 
     anywhere = pl.BlockSpec(memory_space=pltpu.HBM)
     packed_shape = (atoms + EXTRA, channels)
-    packed, weights = call(
+    packed, weights, *vectors = call(
         functools.partial(pack_kernel, sizes),
         [
             jax.ShapeDtypeStruct(packed_shape, F32),
             jax.ShapeDtypeStruct((width, channels), F32),
-        ],
+        ]
+        + [jax.ShapeDtypeStruct(x.shape, x.dtype) for x in vectors],
         tuple(
             pltpu.with_memory_space_constraint(x, pltpu.HBM)
-            for x in (features, jnp.transpose(offsets, (0, 2, 1, 3)), species, group_filter)
+            for x in (features, jnp.transpose(offsets, (0, 2, 1, 3)), species, group_filter, *vectors)
         ),
         10**6,
         (
             pltpu.VMEM((3, 1, atoms), F32),
             pltpu.VMEM((1, atoms), jnp.int32),
-            pltpu.SemaphoreType.DMA((4,)),
+            pltpu.SemaphoreType.DMA((6,)),
         ),
-        specs=[anywhere] * 4,
+        specs=[anywhere] * (4 + len(vectors)),
     )
     column = [packed] + [shift(packed, "gy", k) for k in range(1, span1)]
     across = swap(packed, first=1)
     weights = [weights] + [shift(weights, "gx", -2 * k) for k in range(1, pairs)]
 
-    own = call(join_kernel, jax.ShapeDtypeStruct((span1, *packed_shape), F32), column, 10**6)
+    own, sides = call(
+        column_kernel,
+        [
+            jax.ShapeDtypeStruct((span1, *packed_shape), F32),
+            jax.ShapeDtypeStruct((2, *packed_shape), F32),
+        ],
+        column,
+        10**6,
+    )
     pair = swap(own)
+    partial_sum = jax.ShapeDtypeStruct((rows, 2 * width), F32)
     total = call(
-        functools.partial(structure_kernel, sizes, rows, canonical),
-        jax.ShapeDtypeStruct((rows, 2 * width), F32),
-        (own, pair, *vectors),
-        24 * rows * span1 * atoms * channels,
+        functools.partial(structure_kernel, sizes, rows, canonical, False),
+        partial_sum,
+        (own, *vectors),
+        12 * rows * span1 * atoms * channels,
+    )
+    total = call(
+        functools.partial(structure_kernel, sizes, rows, canonical, True),
+        partial_sum,
+        (pair, *vectors, total),
+        12 * rows * span1 * atoms * channels,
     )
     totals = [total] + [shift(total, "gx", 2 * k) for k in range(1, pairs)]
     weights = call(join_kernel, jax.ShapeDtypeStruct((pairs, width, channels), F32), weights, 10**6)
     pair_weights = swap(weights)
-    left = shift(across, "gy", 1)
-    right = shift(across, "gy", -1)
+    sides = swap(sides, first=1)
 
     table = jax.ShapeDtypeStruct((span1 * atoms, 4 * rows), BF16)
-    high, low = call(
-        functools.partial(table_kernel, sizes, rows, canonical), [table] * 2, (own, *vectors), 10**8
+    high, low, shares = call(
+        functools.partial(table_kernel, sizes, rows, canonical),
+        [table, table, jax.ShapeDtypeStruct((rows, span0), F32)],
+        (own, *vectors),
+        10**8,
     )
     filtered = call(
-        functools.partial(filter_kernel, sizes, rows, canonical),
+        functools.partial(filter_kernel, sizes),
         jax.ShapeDtypeStruct((2 * rows, channels), F32),
-        (*totals, weights, pair_weights, *vectors),
+        (*totals, weights, pair_weights, shares),
         12 * rows * span0 * width * channels,
     )
     pair_filtered = swap(filtered)
 
     lanes = -(-(basis_count + kinds) // 128) * 128
     edge_sizes = (atoms, channels, span0, span1, slots, basis_count, kinds, lanes)
+    hot = call(
+        functools.partial(hot_kernel, edge_sizes),
+        jax.ShapeDtypeStruct((slots * atoms, 9 * atoms), BF16),
+        (jnp.transpose(neighbours[0, 0]), jnp.transpose(edge_mask[0, 0])),
+        10**8,
+    )
     nearby = call(
         functools.partial(edge_kernel, edge_sizes),
         jax.ShapeDtypeStruct((atoms, channels), F32),
@@ -462,10 +505,8 @@
             own,
             pair,
             across,
-            left,
-            right,
-            jnp.transpose(neighbours[0, 0]),
-            jnp.transpose(edge_mask[0, 0]),
+            sides,
+            hot,
             value_weight,
             radial_weight,
             species_embed,
@@ -475,9 +516,7 @@
         (
             pltpu.VMEM((9 * atoms, channels), F32),
             pltpu.VMEM((lanes, 9 * atoms), BF16),
-            pltpu.VMEM((slots * atoms, 9 * atoms), BF16),
         ),
-        24,
     )
 
     block = jax.ShapeDtypeStruct((atoms, channels), F32)

time: 46.5 us -> 46.8 us (level)
  Pallas kernels: 9.72 us -> 10.4 us
    ppermute x14 -> x12, starting transfers between devices: 21 us -> 19.9 us  [shift(): return lax.ppermute(x, axis, [(i, (i + by) % count) for i in range(count)])]
    ppermute x4 -> x5, starting transfers between devices: 2.19 us -> 3.23 us  [swap(): return lax.ppermute(x, 'gx', one + [(b, a) for a, b in one])]
    ppermute x4 -> x5, waiting for transfers between devices: 1.48 us -> 0.74 us  [swap(): return lax.ppermute(x, 'gx', one + [(b, a) for a, b in one])]
    pallas_call x8 -> x10, Pallas kernels: 9.72 us -> 10.4 us  [call(): pl.pallas_call(kernel, out_shape=out_shape, in_specs=specs, scratch_shape...]
    ppermute x14 -> x12, waiting for transfers between devices: 11 us -> 11.5 us  [shift(): return lax.ppermute(x, axis, [(i, (i + by) % count) for i in range(count)])]
  transfers between devices with their start and end apart: 18 -> 17, of which waited for: 7 -> 9; matrix products, arithmetic and copies ran while one was open for 0% -> 0% of each run, Pallas kernels for 19% -> 20%
where the time goes in v2:
time: 46.8 us; the launch traced here: 46.6 us
  starting transfers between devices  23.1 us (49%)
  waiting for transfers between devices  12.2 us (26%)
  Pallas kernels  10.4 us (22%)
  other arithmetic  0.71 us (2%)
    ppermute x12, starting transfers between devices, shift(): return lax.ppermute(x, axis, [(i, (i + by) % count) for i in range(count)])  19.9 us
    ppermute x12, waiting for transfers between devices, shift(): return lax.ppermute(x, axis, [(i, (i + by) % count) for i in range(count)])  11.5 us
    pallas_call x10, Pallas kernels, call(): pl.pallas_call(kernel, out_shape=out_shape, in_specs=specs, scratch_shape...  10.4 us
    ppermute x5, starting transfers between devices, swap(): return lax.ppermute(x, 'gx', one + [(b, a) for a, b in one])  3.23 us
  transfers between devices with their start and end apart: 17, of which 9 were waited for; matrix products, arithmetic and copies ran while one was open for 0% of the time, Pallas kernels for 20%

profile of v2, /device:TPU:0, one launch (start us, length us, event | category | flops | bytes accessed | tf_op | source)
XLA Modules:
  0.0 46.6 jit_solution(6003204479467196726)
XLA Ops:
  0.0 1.0 %shard_map.118 = (f32[136,256]{1,0:T(8,128)S(1)}, f32[64,256]{1,0:T(8,128)S(1)}, s32[3,512]{1,0:T(4,128)S(1)}, f32[2,56,8]{2,1,0:T(8,128)S(1)}) custom-call(f32[1,1,128,256]{3,2,1,0:T(8,128)} %features_ref.1, f32[1,3,1,128]{3,2,1,0:T(1,128)} %bitcast.11, s32[1,1,128]{2,1,0:T(1,128)} %species_ref.1, f32[1,256,256]{2,1,0:T(8,128)} %weight_ref.1, ...), custom_call_target="tpu_custom_call" | custom-call | flops 1000000 | bytes 404992 | tf_op jit(solution)/shard_map/pallas_call | solution.py:371
  1.1 3.0 %collective-permute-start = (f32[136,256]{1,0:T(8,128)S(1)}, f32[136,256]{1,0:T(8,128)S(1)}, u32[]{:S(2)}, u32[]{:S(2)}) collective-permute-start(f32[136,256]{1,0:T(8,128)S(1)} %get-tuple-element.18.refs_0_), channel_id=1, source_target_pairs={{0,1},{1,2},{2,3},{3,0},{4,5},{5,6},{6,7},{7,4},{8,9},{9,10},{10,1... | collective-permute-start | bytes 417800 | tf_op jit(solution)/shard_map/ppermute | solution.py:383
  4.1 1.5 %collective-permute-start.1 = (f32[136,256]{1,0:T(8,128)S(1)}, f32[136,256]{1,0:T(8,128)S(1)}, u32[]{:S(2)}, u32[]{:S(2)}) collective-permute-start(f32[136,256]{1,0:T(8,128)S(1)} %get-tuple-element.18.refs_0_), channel_id=1, source_target_pairs={{0,2},{1,3},{2,0},{3,1},{4,6},{5,7},{6,4},{7,5},{8,10},{9,11},{10,... | collective-permute-start | bytes 417800 | tf_op jit(solution)/shard_map/ppermute | solution.py:383
  5.6 1.4 %collective-permute-start.2 = (f32[136,256]{1,0:T(8,128)S(1)}, f32[136,256]{1,0:T(8,128)S(1)}, u32[]{:S(2)}, u32[]{:S(2)}) collective-permute-start(f32[136,256]{1,0:T(8,128)S(1)} %get-tuple-element.18.refs_0_), channel_id=1, source_target_pairs={{0,3},{1,0},{2,1},{3,2},{4,7},{5,4},{6,5},{7,6},{8,11},{9,8},{10,9... | collective-permute-start | bytes 417800 | tf_op jit(solution)/shard_map/ppermute | solution.py:383
  7.0 2.5 %collective-permute-done.refs_1_ = f32[136,256]{1,0:T(8,128)S(1)} collective-permute-done((f32[136,256]{1,0:T(8,128)S(1)}, f32[136,256]{1,0:T(8,128)S(1)}, u32[]{:S(2)}, u32[]{:S(2)}) %collective-permute-start) | collective-permute-done | bytes 139296 | tf_op jit(solution)/shard_map/ppermute | solution.py:383
  9.6 2.1 %collective-permute-done.1.refs_2_ = f32[136,256]{1,0:T(8,128)S(1)} collective-permute-done((f32[136,256]{1,0:T(8,128)S(1)}, f32[136,256]{1,0:T(8,128)S(1)}, u32[]{:S(2)}, u32[]{:S(2)}) %collective-permute-start.1) | collective-permute-done | bytes 139296 | tf_op jit(solution)/shard_map/ppermute | solution.py:383
  12.1 2.7 %collective-permute-start.10 = (f32[64,256]{1,0:T(8,128)S(1)}, f32[64,256]{1,0:T(8,128)S(1)}, u32[]{:S(2)}, u32[]{:S(2)}) collective-permute-start(f32[64,256]{1,0:T(8,128)S(1)} %get-tuple-element.23.refs_0_), channel_id=1, source_target_pairs={{0,16},{4,20},{8,24},{12,28},{16,0},{20,4},{24,8},{28,12},{1,17},{... | collective-permute-start | bytes 196616 | tf_op jit(solution)/shard_map/ppermute | solution.py:383
  14.7 1.6 %collective-permute-start.11 = (f32[64,256]{1,0:T(8,128)S(1)}, f32[64,256]{1,0:T(8,128)S(1)}, u32[]{:S(2)}, u32[]{:S(2)}) collective-permute-start(f32[64,256]{1,0:T(8,128)S(1)} %get-tuple-element.23.refs_0_), channel_id=1, source_target_pairs={{0,8},{4,12},{8,16},{12,20},{16,24},{20,28},{24,0},{28,4},{1,9},{5... | collective-permute-start | bytes 196616 | tf_op jit(solution)/shard_map/ppermute | solution.py:383
  16.3 2.2 %collective-permute-start.9 = (f32[64,256]{1,0:T(8,128)S(1)}, f32[64,256]{1,0:T(8,128)S(1)}, u32[]{:S(2)}, u32[]{:S(2)}) collective-permute-start(f32[64,256]{1,0:T(8,128)S(1)} %get-tuple-element.23.refs_0_), channel_id=1, source_target_pairs={{0,24},{4,28},{8,0},{12,4},{16,8},{20,12},{24,16},{28,20},{1,25},{... | collective-permute-start | bytes 196616 | tf_op jit(solution)/shard_map/ppermute | solution.py:383
  18.6 0.6 %collective-permute-done.10.refs_2_ = f32[64,256]{1,0:T(8,128)S(1)} collective-permute-done((f32[64,256]{1,0:T(8,128)S(1)}, f32[64,256]{1,0:T(8,128)S(1)}, u32[]{:S(2)}, u32[]{:S(2)}) %collective-permute-start.10) | collective-permute-done | bytes 65568 | tf_op jit(solution)/shard_map/ppermute | solution.py:383
  19.2 2.2 %collective-permute-done.11.refs_3_ = f32[64,256]{1,0:T(8,128)S(1)} collective-permute-done((f32[64,256]{1,0:T(8,128)S(1)}, f32[64,256]{1,0:T(8,128)S(1)}, u32[]{:S(2)}, u32[]{:S(2)}) %collective-permute-start.11) | collective-permute-done | bytes 65568 | tf_op jit(solution)/shard_map/ppermute | solution.py:383
  21.9 2.9 %collective-permute-start.5 = (f32[2,136,256]{2,1,0:T(8,128)S(1)}, f32[2,136,256]{2,1,0:T(8,128)S(1)}, u32[]{:S(2)}, u32[]{:S(2)}) collective-permute-start(f32[2,136,256]{2,1,0:T(8,128)S(1)} %get-tuple-element.20), channel_id=1, source_target_pairs={{4,8},{12,16},{20,24},{28,0},{8,4},{16,12},{24,20},{0,28},{5,9},{1... | collective-permute-start | bytes 835592 | tf_op jit(solution)/shard_map/ppermute | solution.py:389
  24.8 0.8 %shard_map.122.refs_3_ = f32[56,128]{1,0:T(8,128)S(1)} custom-call(f32[4,136,256]{2,1,0:T(8,128)S(1)} %get-tuple-element.19.own_ref.refs_0_, s32[3,512]{1,0:T(4,128)S(1)} %get-tuple-element.21.refs_1_, f32[2,56,8]{2,1,0:T(8,128)S(1)} %get-tuple-element.22.refs_2_), custom_call_target="tpu_custom_call" | custom-call | flops 88080384 | bytes 566784 | tf_op jit(solution)/shard_map/pallas_call | solution.py:371
  25.6 0.8 %shard_map.123.refs_0_ = f32[56,128]{1,0:T(8,128)S(1)} custom-call(f32[4,136,256]{2,1,0:T(8,128)S(1)} %collective-permute-done.3.pair_ref.refs_0_, s32[3,512]{1,0:T(4,128)S(1)} %get-tuple-element.21.refs_1_, f32[2,56,8]{2,1,0:T(8,128)S(1)} %get-tuple-element.22.refs_2_, f32[56,128]{1,0:T(8,128)S(1)} %shard_map.122.refs_3_), custom_call_target="tpu_custom_call" | custom-call | flops 88080384 | bytes 595456 | tf_op jit(solution)/shard_map/pallas_call | solution.py:371
  26.6 1.7 %collective-permute-start.7 = (f32[56,128]{1,0:T(8,128)S(1)}, f32[56,128]{1,0:T(8,128)S(1)}, u32[]{:S(2)}, u32[]{:S(2)}) collective-permute-start(f32[56,128]{1,0:T(8,128)S(1)} %shard_map.123.refs_0_), channel_id=1, source_target_pairs={{0,16},{4,20},{8,24},{12,28},{16,0},{20,4},{24,8},{28,12},{1,17},{... | collective-permute-start | bytes 86024 | tf_op jit(solution)/shard_map/ppermute | solution.py:383
  28.2 2.1 %collective-permute-start.8 = (f32[56,128]{1,0:T(8,128)S(1)}, f32[56,128]{1,0:T(8,128)S(1)}, u32[]{:S(2)}, u32[]{:S(2)}) collective-permute-start(f32[56,128]{1,0:T(8,128)S(1)} %shard_map.123.refs_0_), channel_id=1, source_target_pairs={{0,24},{4,28},{8,0},{12,4},{16,8},{20,12},{24,16},{28,20},{1,25},{... | collective-permute-start | bytes 86024 | tf_op jit(solution)/shard_map/ppermute | solution.py:383
  30.4 0.9 %shard_map.125 = (bf16[512,224]{1,0:T(8,128)(2,1)S(1)}, bf16[512,224]{1,0:T(8,128)(2,1)S(1)}, f32[56,8]{1,0:T(8,128)S(1)}) custom-call(f32[4,136,256]{2,1,0:T(8,128)S(1)} %get-tuple-element.19.own_ref.refs_0_, s32[3,512]{1,0:T(4,128)S(1)} %get-tuple-element.21.refs_1_, f32[2,56,8]{2,1,0:T(8,128)S(1)} %get-tuple-element.22.refs_2_), custom_call_target="tpu_custom_call" | custom-call | flops 100000000 | bytes 566784 | tf_op jit(solution)/shard_map/pallas_call | solution.py:371
  31.3 2.6 %collective-permute-done.6.refs_1_ = f32[56,128]{1,0:T(8,128)S(1)} collective-permute-done((f32[56,128]{1,0:T(8,128)S(1)}, f32[56,128]{1,0:T(8,128)S(1)}, u32[]{:S(2)}, u32[]{:S(2)}) %collective-permute-start.6) | collective-permute-done | bytes 28704 | tf_op jit(solution)/shard_map/ppermute | solution.py:383
  35.0 0.7 %collective-permute-done.13.pair_ref = f32[112,256]{1,0:T(8,128)S(1)} collective-permute-done((f32[112,256]{1,0:T(8,128)S(1)}, f32[112,256]{1,0:T(8,128)S(1)}, u32[]{:S(2)}, u32[]{:S(2)}) %collective-permute-start.13) | collective-permute-done | bytes 114720 | tf_op jit(solution)/shard_map/ppermute | solution.py:389
  36.2 1.7 %collective-permute-start.14 = (f32[128,256]{1,0:T(8,128)S(1)}, f32[128,256]{1,0:T(8,128)S(1)}, u32[]{:S(2)}, u32[]{:S(2)}) collective-permute-start(f32[128,256]{1,0:T(8,128)S(1)} %get-tuple-element.28), channel_id=1, source_target_pairs={{0,3},{1,0},{2,1},{3,2},{4,7},{5,4},{6,5},{7,6},{8,11},{9,8},{10,9... | collective-permute-start | bytes 393224 | tf_op jit(solution)/shard_map/ppermute | solution.py:383
  37.8 1.6 %collective-permute-start.15 = (f32[128,256]{1,0:T(8,128)S(1)}, f32[128,256]{1,0:T(8,128)S(1)}, u32[]{:S(2)}, u32[]{:S(2)}) collective-permute-start(f32[128,256]{1,0:T(8,128)S(1)} %get-tuple-element.29), channel_id=1, source_target_pairs={{0,2},{1,3},{2,0},{3,1},{4,6},{5,7},{6,4},{7,5},{8,10},{9,11},{10,... | collective-permute-start | bytes 393224 | tf_op jit(solution)/shard_map/ppermute | solution.py:383
  39.7 5.4 %shard_map.121 = f32[128,256]{1,0:T(8,128)S(1)} custom-call(f32[4,136,256]{2,1,0:T(8,128)S(1)} %get-tuple-element.19.own_ref.refs_0_, f32[4,136,256]{2,1,0:T(8,128)S(1)} %collective-permute-done.3.pair_ref.refs_0_, f32[136,256]{1,0:T(8,128)S(1)} %collective-permute-done.4.across_ref, f32[2,136,256]{2,1,0:T(8,128)S(1)} %collective-permute-done.5.sides_ref, ...), custom_call_target="tpu_custom_call" | custom-call | flops 4000000000 | bytes 6905856 | tf_op jit(solution)/shard_map/pallas_call | solution.py:371
  45.2 0.7 %collective-permute-done.15 = f32[128,256]{1,0:T(8,128)S(1)} collective-permute-done((f32[128,256]{1,0:T(8,128)S(1)}, f32[128,256]{1,0:T(8,128)S(1)}, u32[]{:S(2)}, u32[]{:S(2)}) %collective-permute-start.15) | collective-permute-done | bytes 131104 | tf_op jit(solution)/shard_map/ppermute | solution.py:383
  45.9 0.7 %add_bitcast_fusion = f32[1,1,128,256]{3,2,1,0:T(8,128)} fusion(f32[128,256]{1,0:T(8,128)S(1)} %collective-permute-done.16, f32[128,256]{1,0:T(8,128)S(1)} %collective-permute-done.15, f32[128,256]{1,0:T(8,128)S(1)} %collective-permute-done.14, f32[128,256]{1,0:T(8,128)S(1)} %shard_map.121, f32[128,256]{1,0:T(8,128)S(1)} %get-tuple-element.27), kind=kLoop, calls=%fused_computation | loop fusion | flops 131072 | bytes 786432 | tf_op jit(solution)/shard_map/broadcast_in_dim | solution.py:533
  (33 shorter events, 2.8 us)
Async XLA Ops:
  0.0 34.5 %copy-start = (s32[1,1,128,8]{2,3,1,0:T(8,128)S(1)}, s32[1,1,128,8]{2,3,1,0:T(8,128)}, u32[]{:S(2)}) copy-start(s32[1,1,128,8]{2,3,1,0:T(8,128)} %param.15) | copy-start | bytes 12292
  0.0 34.5 %copy-start.1 = (s32[1,1,128,8]{2,3,1,0:T(8,128)S(1)}, s32[1,1,128,8]{2,3,1,0:T(8,128)}, u32[]{:S(2)}) copy-start(s32[1,1,128,8]{2,3,1,0:T(8,128)} %param.16) | copy-start | bytes 12292
  1.1 8.5 %collective-permute-start = (f32[136,256]{1,0:T(8,128)S(1)}, f32[136,256]{1,0:T(8,128)S(1)}, u32[]{:S(2)}, u32[]{:S(2)}) collective-permute-start(f32[136,256]{1,0:T(8,128)S(1)} %get-tuple-element.18.refs_0_), channel_id=1, source_target_pairs={{0,1},{1,2},{2,3},{3,0},{4,5},{5,6},{6,7},{7,4},{8,9},{9,10},{10,1... | collective-permute-start | bytes 417800 | tf_op jit(solution)/shard_map/ppermute | solution.py:383
  4.1 7.6 %collective-permute-start.1 = (f32[136,256]{1,0:T(8,128)S(1)}, f32[136,256]{1,0:T(8,128)S(1)}, u32[]{:S(2)}, u32[]{:S(2)}) collective-permute-start(f32[136,256]{1,0:T(8,128)S(1)} %get-tuple-element.18.refs_0_), channel_id=1, source_target_pairs={{0,2},{1,3},{2,0},{3,1},{4,6},{5,7},{6,4},{7,5},{8,10},{9,11},{10,... | collective-permute-start | bytes 417800 | tf_op jit(solution)/shard_map/ppermute | solution.py:383
  5.6 6.3 %collective-permute-start.2 = (f32[136,256]{1,0:T(8,128)S(1)}, f32[136,256]{1,0:T(8,128)S(1)}, u32[]{:S(2)}, u32[]{:S(2)}) collective-permute-start(f32[136,256]{1,0:T(8,128)S(1)} %get-tuple-element.18.refs_0_), channel_id=1, source_target_pairs={{0,3},{1,0},{2,1},{3,2},{4,7},{5,4},{6,5},{7,6},{8,11},{9,8},{10,9... | collective-permute-start | bytes 417800 | tf_op jit(solution)/shard_map/ppermute | solution.py:383
  12.0 13.6 %collective-permute-start.3 = (f32[4,136,256]{2,1,0:T(8,128)S(1)}, f32[4,136,256]{2,1,0:T(8,128)S(1)}, u32[]{:S(2)}, u32[]{:S(2)}) collective-permute-start(f32[4,136,256]{2,1,0:T(8,128)S(1)} %get-tuple-element.19.own_ref.refs_0_), channel_id=1, source_target_pairs={{0,4},{8,12},{16,20},{24,28},{4,0},{12,8},{20,16},{28,24},{1,5},{9... | collective-permute-start | bytes 1671176 | tf_op jit(solution)/shard_map/ppermute | solution.py:389
  12.1 7.1 %collective-permute-start.10 = (f32[64,256]{1,0:T(8,128)S(1)}, f32[64,256]{1,0:T(8,128)S(1)}, u32[]{:S(2)}, u32[]{:S(2)}) collective-permute-start(f32[64,256]{1,0:T(8,128)S(1)} %get-tuple-element.23.refs_0_), channel_id=1, source_target_pairs={{0,16},{4,20},{8,24},{12,28},{16,0},{20,4},{24,8},{28,12},{1,17},{... | collective-permute-start | bytes 196616 | tf_op jit(solution)/shard_map/ppermute | solution.py:383
  14.7 6.7 %collective-permute-start.11 = (f32[64,256]{1,0:T(8,128)S(1)}, f32[64,256]{1,0:T(8,128)S(1)}, u32[]{:S(2)}, u32[]{:S(2)}) collective-permute-start(f32[64,256]{1,0:T(8,128)S(1)} %get-tuple-element.23.refs_0_), channel_id=1, source_target_pairs={{0,8},{4,12},{8,16},{12,20},{16,24},{20,28},{24,0},{28,4},{1,9},{5... | collective-permute-start | bytes 196616 | tf_op jit(solution)/shard_map/ppermute | solution.py:383
  16.3 5.5 %collective-permute-start.9 = (f32[64,256]{1,0:T(8,128)S(1)}, f32[64,256]{1,0:T(8,128)S(1)}, u32[]{:S(2)}, u32[]{:S(2)}) collective-permute-start(f32[64,256]{1,0:T(8,128)S(1)} %get-tuple-element.23.refs_0_), channel_id=1, source_target_pairs={{0,24},{4,28},{8,0},{12,4},{16,8},{20,12},{24,16},{28,20},{1,25},{... | collective-permute-start | bytes 196616 | tf_op jit(solution)/shard_map/ppermute | solution.py:383
  21.8 9.5 %collective-permute-start.12 = (f32[4,64,256]{2,1,0:T(8,128)S(1)}, f32[4,64,256]{2,1,0:T(8,128)S(1)}, u32[]{:S(2)}, u32[]{:S(2)}) collective-permute-start(f32[4,64,256]{2,1,0:T(8,128)S(1)} %shard_map.124.refs_4_), channel_id=1, source_target_pairs={{0,4},{8,12},{16,20},{24,28},{4,0},{12,8},{20,16},{28,24},{1,5},{9... | collective-permute-start | bytes 786440 | tf_op jit(solution)/shard_map/ppermute | solution.py:389
  21.9 17.8 %collective-permute-start.5 = (f32[2,136,256]{2,1,0:T(8,128)S(1)}, f32[2,136,256]{2,1,0:T(8,128)S(1)}, u32[]{:S(2)}, u32[]{:S(2)}) collective-permute-start(f32[2,136,256]{2,1,0:T(8,128)S(1)} %get-tuple-element.20), channel_id=1, source_target_pairs={{4,8},{12,16},{20,24},{28,0},{8,4},{16,12},{24,20},{0,28},{5,9},{1... | collective-permute-start | bytes 835592 | tf_op jit(solution)/shard_map/ppermute | solution.py:389
  26.4 13.3 %copy-start.2 = (f32[256,256]{1,0:T(8,128)S(1)}, f32[256,256]{1,0:T(8,128)}, u32[]{:S(2)}) copy-start(f32[256,256]{1,0:T(8,128)} %value_ref.1) | copy-start | bytes 786436
  26.5 13.2 %copy-start.3 = (f32[256,256]{1,0:T(8,128)S(1)}, f32[256,256]{1,0:T(8,128)}, u32[]{:S(2)}) copy-start(f32[256,256]{1,0:T(8,128)} %mixing_ref.1) | copy-start | bytes 786436
  26.5 13.2 %copy-start.4 = (f32[64,256]{1,0:T(8,128)S(1)}, f32[64,256]{1,0:T(8,128)}, u32[]{:S(2)}) copy-start(f32[64,256]{1,0:T(8,128)} %radial_ref.1) | copy-start | bytes 196612
  26.5 13.2 %copy-start.5 = (f32[64,256]{1,0:T(8,128)S(1)}, f32[64,256]{1,0:T(8,128)}, u32[]{:S(2)}) copy-start(f32[64,256]{1,0:T(8,128)} %embed_ref.1) | copy-start | bytes 196612
  26.5 7.4 %collective-permute-start.6 = (f32[56,128]{1,0:T(8,128)S(1)}, f32[56,128]{1,0:T(8,128)S(1)}, u32[]{:S(2)}, u32[]{:S(2)}) collective-permute-start(f32[56,128]{1,0:T(8,128)S(1)} %shard_map.123.refs_0_), channel_id=1, source_target_pairs={{0,8},{4,12},{8,16},{12,20},{16,24},{20,28},{24,0},{28,4},{1,9},{5... | collective-permute-start | bytes 86024 | tf_op jit(solution)/shard_map/ppermute | solution.py:383
  26.6 7.4 %collective-permute-start.7 = (f32[56,128]{1,0:T(8,128)S(1)}, f32[56,128]{1,0:T(8,128)S(1)}, u32[]{:S(2)}, u32[]{:S(2)}) collective-permute-start(f32[56,128]{1,0:T(8,128)S(1)} %shard_map.123.refs_0_), channel_id=1, source_target_pairs={{0,16},{4,20},{8,24},{12,28},{16,0},{20,4},{24,8},{28,12},{1,17},{... | collective-permute-start | bytes 86024 | tf_op jit(solution)/shard_map/ppermute | solution.py:383
  28.2 5.7 %collective-permute-start.8 = (f32[56,128]{1,0:T(8,128)S(1)}, f32[56,128]{1,0:T(8,128)S(1)}, u32[]{:S(2)}, u32[]{:S(2)}) collective-permute-start(f32[56,128]{1,0:T(8,128)S(1)} %shard_map.123.refs_0_), channel_id=1, source_target_pairs={{0,24},{4,28},{8,0},{12,4},{16,8},{20,12},{24,16},{28,20},{1,25},{... | collective-permute-start | bytes 86024 | tf_op jit(solution)/shard_map/ppermute | solution.py:383
  31.3 8.4 %collective-permute-start.4 = (f32[136,256]{1,0:T(8,128)S(1)}, f32[136,256]{1,0:T(8,128)S(1)}, u32[]{:S(2)}, u32[]{:S(2)}) collective-permute-start(f32[136,256]{1,0:T(8,128)S(1)} %get-tuple-element.18.refs_0_), channel_id=1, source_target_pairs={{4,8},{12,16},{20,24},{28,0},{8,4},{16,12},{24,20},{0,28},{5,9},{1... | collective-permute-start | bytes 417800 | tf_op jit(solution)/shard_map/ppermute | solution.py:389
  34.4 1.4 %collective-permute-start.13 = (f32[112,256]{1,0:T(8,128)S(1)}, f32[112,256]{1,0:T(8,128)S(1)}, u32[]{:S(2)}, u32[]{:S(2)}) collective-permute-start(f32[112,256]{1,0:T(8,128)S(1)} %shard_map.126.own_ref), channel_id=1, source_target_pairs={{0,4},{8,12},{16,20},{24,28},{4,0},{12,8},{20,16},{28,24},{1,5},{9... | collective-permute-start | bytes 344072 | tf_op jit(solution)/shard_map/ppermute | solution.py:389
  36.2 9.0 %collective-permute-start.14 = (f32[128,256]{1,0:T(8,128)S(1)}, f32[128,256]{1,0:T(8,128)S(1)}, u32[]{:S(2)}, u32[]{:S(2)}) collective-permute-start(f32[128,256]{1,0:T(8,128)S(1)} %get-tuple-element.28), channel_id=1, source_target_pairs={{0,3},{1,0},{2,1},{3,2},{4,7},{5,4},{6,5},{7,6},{8,11},{9,8},{10,9... | collective-permute-start | bytes 393224 | tf_op jit(solution)/shard_map/ppermute | solution.py:383
  37.8 8.1 %collective-permute-start.15 = (f32[128,256]{1,0:T(8,128)S(1)}, f32[128,256]{1,0:T(8,128)S(1)}, u32[]{:S(2)}, u32[]{:S(2)}) collective-permute-start(f32[128,256]{1,0:T(8,128)S(1)} %get-tuple-element.29), channel_id=1, source_target_pairs={{0,2},{1,3},{2,0},{3,1},{4,6},{5,7},{6,4},{7,5},{8,10},{9,11},{10,... | collective-permute-start | bytes 393224 | tf_op jit(solution)/shard_map/ppermute | solution.py:383
  39.4 6.5 %collective-permute-start.16 = (f32[128,256]{1,0:T(8,128)S(1)}, f32[128,256]{1,0:T(8,128)S(1)}, u32[]{:S(2)}, u32[]{:S(2)}) collective-permute-start(f32[128,256]{1,0:T(8,128)S(1)} %get-tuple-element.30), channel_id=1, source_target_pairs={{0,1},{1,2},{2,3},{3,0},{4,5},{5,6},{6,7},{7,4},{8,9},{9,10},{10,1... | collective-permute-start | bytes 393224 | tf_op jit(solution)/shard_map/ppermute | solution.py:383

commit v3 on v2

--- a/solution.py
+++ b/solution.py
@@ -17,6 +17,7 @@
 VERTICAL = 2
 F32 = jnp.float32
 BF16 = jnp.bfloat16
+KNOWN = 7
 EXTRA = 8
 NN = (((1,), (0,)), ((), ()))
 NT = (((1,), (1,)), ((), ()))
@@ -190,18 +191,15 @@
 
 
 def table_kernel(sizes, rows, canonical, *refs):
-    atoms, _, span0, span1, group = sizes
+    _, _, span0, span1, group = sizes
     own_ref, vectors_ref = refs[:2]
     basis_ref, (high_ref, low_ref, weight_ref) = refs[2] if canonical else None, refs[-3:]
     lateral, transverse, parity = place()
     sides = [rows_of(basis_ref, vectors_ref, rows, p) for p in (parity, 1 - parity)]
-    for back in range(span1):
-        packed = own_ref.at[back]
-        parts = []
-        for triples in sides:
-            parts.extend(phases(sizes, triples, lateral, transverse - back, packed))
-        at = slice(back * atoms, (back + 1) * atoms)
-        high_ref[at], low_ref[at] = split(jnp.transpose(jnp.concatenate(parts, axis=0)))
+    parts = []
+    for triples in sides:
+        parts.extend(phases(sizes, triples, lateral, transverse, own_ref.at[0]))
+    high_ref[...], low_ref[...] = split(jnp.transpose(jnp.concatenate(parts, axis=0)))
 
     n0, n1, n2 = sides[0]
     waves = (FULL_TURN * n0 / span0, FULL_TURN * n1 / span1, FULL_TURN * n2)
@@ -250,15 +248,19 @@
     out_ref[...] = mixed
 
 
-def project_kernel(sizes, scale, own_ref, pair_ref, high_ref, low_ref, *outs):
-    atoms, span1 = sizes[0], sizes[3]
+def merge_kernel(*refs):
+    total = refs[0][...]
+    for ref in refs[1:-1]:
+        total = total + ref[...]
+    refs[-1][...] = total
+
+
+def project_kernel(scale, own_ref, pair_ref, high_ref, low_ref, nearby_ref, out_ref):
     filtered = split(jnp.concatenate([own_ref[...], pair_ref[...]], axis=0) * scale)
-    everything = dot3((high_ref[...], low_ref[...]), filtered)
-    for back in range(span1):
-        outs[back][...] = everything[back * atoms : (back + 1) * atoms]
-
-
-def hot_kernel(sizes, listed_ref, mask_ref, out_ref):
+    out_ref[...] = nearby_ref[...] + dot3((high_ref[...], low_ref[...]), filtered)
+
+
+def hot_kernel(sizes, listed_ref, mask_ref, known_ref, far_ref):
     atoms, _, span0, span1, slots = sizes[:5]
     lateral, transverse, parity = place()
     listed = listed_ref[...].astype(F32)
@@ -269,62 +271,82 @@
     shift1 = source - source0 * span1 - transverse + 1.0
     shift1 = shift1 - span1 * quotient(shift1, span1)
     line = (shift0 - 1.0) * (1.0 - 2.0 * parity.astype(F32)) + 1.0
-    row = (line * 3.0 + shift1) * atoms + (listed - source * atoms)
+    far = jnp.where(shift1 == 1.0, 6.0, 7.0 + 0.5 * shift1)
+    block = jnp.where(line == 0.0, far, (line - 1.0) * 3.0 + shift1)
+    row = block * atoms + (listed - source * atoms)
     row = jnp.transpose(jnp.where(mask_ref[...] != 0, row, -1.0)).astype(jnp.int32)
     for slot in range(slots):
-        hot = iota((atoms, 9 * atoms), 1) == row[:, slot : slot + 1]
-        out_ref[slot * atoms : (slot + 1) * atoms] = jnp.where(hot, 1.0, 0.0).astype(BF16)
+        at = slice(slot * atoms, (slot + 1) * atoms)
+        for ref, first, count in ((known_ref, 0, KNOWN), (far_ref, KNOWN, 9 - KNOWN)):
+            hot = iota((atoms, count * atoms), 1) + first * atoms == row[:, slot : slot + 1]
+            ref[at] = jnp.where(hot, 1.0, 0.0).astype(BF16)
+
+
+def block_rows(sizes, packed, shift0, shift1):
+    atoms, channels, _, _, _, basis_count, _, lanes = sizes
+    low = iota((16, atoms), 0)
+    species = component(packed, atoms, channels, 3).astype(jnp.int32)
+    kind_hot = jnp.where(iota((lanes - basis_count, atoms), 0) == species, 1.0, 0.0)
+    positions = jnp.zeros((16, atoms), F32)
+    for n, by in enumerate((shift0, shift1, 0.0)):
+        rest = component(packed, atoms, channels, n) + by
+        for piece in range(3):
+            part = rest.astype(BF16).astype(F32)
+            positions = jnp.where(low == n + 4 * piece, part, positions)
+            rest = rest - part
+    gap = jnp.zeros((basis_count - 16, atoms), F32)
+    return jnp.concatenate([positions, gap, kind_hot], axis=0).astype(BF16)
+
+
+def prepare_kernel(
+    sizes, own_ref, pair_ref, across_ref, value_ref, high_ref, low_ref, place_ref
+):
+    atoms, span1 = sizes[0], sizes[3]
+    toward = 1.0 - 2.0 * place()[2].astype(F32)
+    order = (1, 0, span1 - 1)
+    blocks = [(own_ref.at[n], 0.0, d - 1.0) for d, n in enumerate(order)]
+    blocks += [(pair_ref.at[n], toward, d - 1.0) for d, n in enumerate(order)]
+    blocks.append((across_ref, -toward, 0.0))
+    for n, (packed, shift0, shift1) in enumerate(blocks):
+        at = slice(n * atoms, (n + 1) * atoms)
+        place_ref[:, at] = block_rows(sizes, packed, shift0, shift1)
+    features = jnp.concatenate([packed[:atoms] for packed, _, _ in blocks], axis=0)
+    high_ref[...], low_ref[...] = split(dot3(split(features), split(value_ref[...])))
+
+
+def known_kernel(hot_ref, high_ref, low_ref, out_ref):
+    hot = hot_ref[...]
+    out_ref[...] = dot(hot, high_ref[...]) + dot(hot, low_ref[...])
 
 
 def edge_kernel(
     sizes,
     own_ref,
-    pair_ref,
-    across_ref,
     sides_ref,
     hot_ref,
+    far_ref,
+    place_ref,
+    values_ref,
     value_ref,
     radial_ref,
     embed_ref,
     mixing_ref,
     out_ref,
-    feature_scratch,
-    place_scratch,
 ):
-    atoms, channels, _, span1, slots, basis_count, kinds, lanes = sizes
-    parity = place()[2]
-    toward = 1.0 - 2.0 * parity.astype(F32)
-    last = span1 - 1
-    own_rows = None
-    table = (
-        (sides_ref.at[0], across_ref, sides_ref.at[1]),
-        (own_ref.at[1], own_ref.at[0], own_ref.at[last]),
-        (pair_ref.at[1], pair_ref.at[0], pair_ref.at[last]),
-    )
-    low = iota((16, atoms), 0)
-    kind_rows = iota((lanes - basis_count, atoms), 0)
-    for r, row_refs in enumerate(table):
-        for d, packed in enumerate(row_refs):
-            at = (r * 3 + d) * atoms
-            feature_scratch[at : at + atoms] = packed[:atoms]
-            species = component(packed, atoms, channels, 3).astype(jnp.int32)
-            kind_hot = jnp.where(kind_rows == species, 1.0, 0.0)
-            positions = jnp.zeros((16, atoms), F32)
-            exact = positions
-            for n, shift in enumerate(((r - 1.0) * toward, d - 1.0, 0.0)):
-                u = component(packed, atoms, channels, n)
-                exact = jnp.where(low == n, u, exact)
-                rest = u + shift
-                for piece in range(3):
-                    part = rest.astype(BF16).astype(F32)
-                    positions = jnp.where(low == n + 4 * piece, part, positions)
-                    rest = rest - part
-            gap = jnp.zeros((basis_count - 16, atoms), F32)
-            where = jnp.concatenate([positions, gap, kind_hot], axis=0)
-            place_scratch[:, at : at + atoms] = where.astype(BF16)
-            if r == 1 and d == 1:
-                own_rows = jnp.concatenate([exact, gap, kind_hot], axis=0)
-
+    atoms, channels, _, _, slots, basis_count, kinds, lanes = sizes
+    toward = 1.0 - 2.0 * place()[2].astype(F32)
+    far_place = jnp.concatenate(
+        [block_rows(sizes, sides_ref.at[n], -toward, 2.0 * n - 1.0) for n in range(2)], axis=1
+    )
+    far_features = jnp.concatenate([sides_ref[n, :atoms] for n in range(2)], axis=0)
+    far_values = split(dot3(split(far_features), split(value_ref[...])))
+
+    packed = own_ref.at[0]
+    low = iota((lanes, atoms), 0)
+    species = component(packed, atoms, channels, 3).astype(jnp.int32)
+    own_rows = jnp.where(low - basis_count == species, 1.0, 0.0)
+    for n in range(3):
+        own_rows = jnp.where(low == n, component(packed, atoms, channels, n), own_rows)
     own = jnp.transpose(own_rows)
     lane = iota((atoms, lanes), 1)
     own_place = jnp.where(lane < 3, own, 0.0)
@@ -332,11 +354,11 @@
     first = [radial_ref[...], embed_ref[...]]
     if missing:
         first.append(jnp.zeros((missing, channels), F32))
-    first = split(jnp.concatenate(first, axis=0))
+    first_high, first_low = split(jnp.concatenate(first, axis=0))
+    first_twice = jnp.concatenate([first_high, first_high], axis=0)
     own_kind = jnp.where(lane >= basis_count, own, 0.0).astype(BF16)
-    own_before = dot(own_kind, first[0]) + dot(own_kind, first[1])
-
-    values = split(dot3(split(feature_scratch[...]), split(value_ref[...])))
+    own_before = dot(own_kind, first_high) + dot(own_kind, first_low)
+
     mixing = split(mixing_ref[...])
     centres = lane.astype(F32) * (RADIAL_REACH / (basis_count - 1))
     spread = 2.0 * RADIAL_REACH / (basis_count - 1)
@@ -344,9 +366,10 @@
     total = jnp.zeros((atoms, channels), F32)
     for start in range(0, slots, chunk):
         rows = chunk * atoms
-        hot = hot_ref[start * atoms : start * atoms + rows]
-        near_values = dot(hot, values[0]) + dot(hot, values[1])
-        where = dot(hot, place_scratch[...], NT)
+        at = slice(start * atoms, start * atoms + rows)
+        far = far_ref[at]
+        near_values = values_ref[at] + dot(far, far_values[0]) + dot(far, far_values[1])
+        where = dot(hot_ref[at], place_ref[...], NT) + dot(far, far_place, NT)
         gap = where + pltpu.roll(where, lanes - 4, 1) + pltpu.roll(where, lanes - 8, 1)
         gap = gap.reshape(chunk, atoms, lanes) - own_place[None]
         gap = jnp.where((lane < 3)[None], gap, 0.0)
@@ -357,7 +380,10 @@
             jnp.exp(-scaled * scaled),
             where.reshape(chunk, atoms, lanes),
         ).reshape(rows, lanes)
-        before = dot3(split(inner), first).reshape(chunk, atoms, channels) + own_before[None]
+        inner_high, inner_low = split(inner)
+        before = dot(jnp.concatenate([inner_high, inner_low], axis=1), first_twice)
+        before = (before + dot(inner_high, first_low)).reshape(chunk, atoms, channels)
+        before = before + own_before[None]
         hidden = (before / (1.0 + jnp.exp(-before))).reshape(rows, channels)
         filters = dot3(split(hidden), mixing)
         total = total + jnp.sum((filters * near_values).reshape(chunk, atoms, channels), axis=0)
@@ -475,7 +501,7 @@
     pair_weights = swap(weights)
     sides = swap(sides, first=1)
 
-    table = jax.ShapeDtypeStruct((span1 * atoms, 4 * rows), BF16)
+    table = jax.ShapeDtypeStruct((atoms, 4 * rows), BF16)
     high, low, shares = call(
         functools.partial(table_kernel, sizes, rows, canonical),
         [table, table, jax.ShapeDtypeStruct((rows, span0), F32)],
@@ -488,14 +514,33 @@
         (*totals, weights, pair_weights, shares),
         12 * rows * span0 * width * channels,
     )
+    quarters = [filtered] + [shift(filtered, "gy", k) for k in range(1, span1)]
+    filtered = call(merge_kernel, jax.ShapeDtypeStruct((2 * rows, channels), F32), quarters, 10**6)
     pair_filtered = swap(filtered)
 
     lanes = -(-(basis_count + kinds) // 128) * 128
     edge_sizes = (atoms, channels, span0, span1, slots, basis_count, kinds, lanes)
-    hot = call(
+    edges = slots * atoms
+    hot, far = call(
         functools.partial(hot_kernel, edge_sizes),
-        jax.ShapeDtypeStruct((slots * atoms, 9 * atoms), BF16),
+        [
+            jax.ShapeDtypeStruct((edges, KNOWN * atoms), BF16),
+            jax.ShapeDtypeStruct((edges, (9 - KNOWN) * atoms), BF16),
+        ],
         (jnp.transpose(neighbours[0, 0]), jnp.transpose(edge_mask[0, 0])),
+        10**8,
+    )
+    half = jax.ShapeDtypeStruct((KNOWN * atoms, channels), BF16)
+    value_high, value_low, places = call(
+        functools.partial(prepare_kernel, edge_sizes),
+        [half, half, jax.ShapeDtypeStruct((lanes, KNOWN * atoms), BF16)],
+        (own, pair, across, value_weight),
+        10**8,
+    )
+    near_values = call(
+        known_kernel,
+        jax.ShapeDtypeStruct((edges, channels), F32),
+        (hot, value_high, value_low),
         10**8,
     )
     nearby = call(
@@ -503,33 +548,26 @@
         jax.ShapeDtypeStruct((atoms, channels), F32),
         (
             own,
-            pair,
-            across,
             sides,
             hot,
+            far,
+            places,
+            near_values,
             value_weight,
             radial_weight,
             species_embed,
             mixing_weight,
         ),
         4 * 10**9,
-        (
-            pltpu.VMEM((9 * atoms, channels), F32),
-            pltpu.VMEM((lanes, 9 * atoms), BF16),
-        ),
-    )
-
-    block = jax.ShapeDtypeStruct((atoms, channels), F32)
+    )
+
     scale = 1.0 / math.sqrt(atoms * span0 * span1 * modes)
-    distant = call(
-        functools.partial(project_kernel, sizes, scale),
-        [block] * span1,
-        (filtered, pair_filtered, high, low),
-        24 * rows * span1 * atoms * channels,
-    )
-    result = nearby + distant[0]
-    for k in range(1, span1):
-        result = result + shift(distant[k], "gy", -k)
+    result = call(
+        functools.partial(project_kernel, scale),
+        jax.ShapeDtypeStruct((atoms, channels), F32),
+        (filtered, pair_filtered, high, low, nearby),
+        24 * rows * atoms * channels,
+    )
     return result[None, None]
 
 

time: 46.8 us -> 51.4 us (1.098)
  waiting for transfers between devices: 12.2 us -> 21.9 us
  starting transfers between devices: 23.1 us -> 19.1 us
  other arithmetic: 0.71 us -> 0 us
    ppermute x12, waiting for transfers between devices: 11.5 us -> 21.9 us  [shift(): return lax.ppermute(x, axis, [(i, (i + by) % count) for i in range(count)])]
    ppermute x12, starting transfers between devices: 19.9 us -> 15.3 us  [shift(): return lax.ppermute(x, axis, [(i, (i + by) % count) for i in range(count)])]
    ppermute x5, waiting for transfers between devices: 0.74 us -> 0.01 us  [swap(): return lax.ppermute(x, 'gx', one + [(b, a) for a, b in one])]
    broadcast_in_dim x1 -> x0, other arithmetic: 0.71 us -> none  [shards(): return result[None, None]]
    ppermute x5, starting transfers between devices: 3.23 us -> 3.82 us  [swap(): return lax.ppermute(x, 'gx', one + [(b, a) for a, b in one])]
    pallas_call x10 -> x13, Pallas kernels: 10.4 us -> 10 us  [call(): pl.pallas_call(kernel, out_shape=out_shape, in_specs=specs, scratch_shape...]
  transfers between devices with their start and end apart: 17 -> 17, of which waited for: 9 -> 10; matrix products, arithmetic and copies ran while one was open for 0% -> 0% of each run, Pallas kernels for 20% -> 16%
where the time goes in v3:
time: 51.4 us; the launch traced here: 51.3 us
  waiting for transfers between devices  21.9 us (43%)
  starting transfers between devices  19.1 us (37%)
  Pallas kernels  10 us (19%)
    ppermute x12, waiting for transfers between devices, shift(): return lax.ppermute(x, axis, [(i, (i + by) % count) for i in range(count)])  21.9 us
    ppermute x12, starting transfers between devices, shift(): return lax.ppermute(x, axis, [(i, (i + by) % count) for i in range(count)])  15.3 us
    pallas_call x13, Pallas kernels, call(): pl.pallas_call(kernel, out_shape=out_shape, in_specs=specs, scratch_shape...  10 us
    ppermute x5, starting transfers between devices, swap(): return lax.ppermute(x, 'gx', one + [(b, a) for a, b in one])  3.82 us
  transfers between devices with their start and end apart: 17, of which 10 were waited for; matrix products, arithmetic and copies ran while one was open for 0% of the time, Pallas kernels for 16%

profile of v3, /device:TPU:0, one launch (start us, length us, event | category | flops | bytes accessed | tf_op | source)
XLA Modules:
  0.0 51.3 jit_solution(469141365919197769)
XLA Ops:
  0.0 1.0 %shard_map.118 = (f32[136,256]{1,0:T(8,128)S(1)}, f32[64,256]{1,0:T(8,128)S(1)}, s32[3,512]{1,0:T(4,128)S(1)}, f32[2,56,8]{2,1,0:T(8,128)S(1)}) custom-call(f32[1,1,128,256]{3,2,1,0:T(8,128)} %features_ref.1, f32[1,3,1,128]{3,2,1,0:T(1,128)} %bitcast.10, s32[1,1,128]{2,1,0:T(1,128)} %species_ref.1, f32[1,256,256]{2,1,0:T(8,128)} %weight_ref.1, ...), custom_call_target="tpu_custom_call" | custom-call | flops 1000000 | bytes 404992 | tf_op jit(solution)/shard_map/pallas_call | solution.py:397
  1.0 4.0 %collective-permute-start.2 = (f32[136,256]{1,0:T(8,128)S(1)}, f32[136,256]{1,0:T(8,128)S(1)}, u32[]{:S(2)}, u32[]{:S(2)}) collective-permute-start(f32[136,256]{1,0:T(8,128)S(1)} %get-tuple-element.19.refs_0_), channel_id=1, source_target_pairs={{0,3},{1,0},{2,1},{3,2},{4,7},{5,4},{6,5},{7,6},{8,11},{9,8},{10,9... | collective-permute-start | bytes 417800 | tf_op jit(solution)/shard_map/ppermute | solution.py:409
  6.1 3.0 %collective-permute-done.2.refs_3_ = f32[136,256]{1,0:T(8,128)S(1)} collective-permute-done((f32[136,256]{1,0:T(8,128)S(1)}, f32[136,256]{1,0:T(8,128)S(1)}, u32[]{:S(2)}, u32[]{:S(2)}) %collective-permute-start.2) | collective-permute-done | bytes 139296 | tf_op jit(solution)/shard_map/ppermute | solution.py:409
  9.1 4.1 %collective-permute-done.1.refs_2_ = f32[136,256]{1,0:T(8,128)S(1)} collective-permute-done((f32[136,256]{1,0:T(8,128)S(1)}, f32[136,256]{1,0:T(8,128)S(1)}, u32[]{:S(2)}, u32[]{:S(2)}) %collective-permute-start.1) | collective-permute-done | bytes 139296 | tf_op jit(solution)/shard_map/ppermute | solution.py:409
  13.3 1.6 %collective-permute-start.9 = (f32[64,256]{1,0:T(8,128)S(1)}, f32[64,256]{1,0:T(8,128)S(1)}, u32[]{:S(2)}, u32[]{:S(2)}) collective-permute-start(f32[64,256]{1,0:T(8,128)S(1)} %get-tuple-element.23.refs_0_), channel_id=1, source_target_pairs={{0,8},{4,12},{8,16},{12,20},{16,24},{20,28},{24,0},{28,4},{1,9},{5... | collective-permute-start | bytes 196616 | tf_op jit(solution)/shard_map/ppermute | solution.py:409
  14.9 2.6 %collective-permute-start.8 = (f32[64,256]{1,0:T(8,128)S(1)}, f32[64,256]{1,0:T(8,128)S(1)}, u32[]{:S(2)}, u32[]{:S(2)}) collective-permute-start(f32[64,256]{1,0:T(8,128)S(1)} %get-tuple-element.23.refs_0_), channel_id=1, source_target_pairs={{0,16},{4,20},{8,24},{12,28},{16,0},{20,4},{24,8},{28,12},{1,17},{... | collective-permute-start | bytes 196616 | tf_op jit(solution)/shard_map/ppermute | solution.py:409
  17.5 1.3 %collective-permute-start.7 = (f32[64,256]{1,0:T(8,128)S(1)}, f32[64,256]{1,0:T(8,128)S(1)}, u32[]{:S(2)}, u32[]{:S(2)}) collective-permute-start(f32[64,256]{1,0:T(8,128)S(1)} %get-tuple-element.23.refs_0_), channel_id=1, source_target_pairs={{0,24},{4,28},{8,0},{12,4},{16,8},{20,12},{24,16},{28,20},{1,25},{... | collective-permute-start | bytes 196616 | tf_op jit(solution)/shard_map/ppermute | solution.py:409
  18.9 0.9 %collective-permute-done.9.refs_3_ = f32[64,256]{1,0:T(8,128)S(1)} collective-permute-done((f32[64,256]{1,0:T(8,128)S(1)}, f32[64,256]{1,0:T(8,128)S(1)}, u32[]{:S(2)}, u32[]{:S(2)}) %collective-permute-start.9) | collective-permute-done | bytes 65568 | tf_op jit(solution)/shard_map/ppermute | solution.py:409
  19.8 2.8 %collective-permute-done.8.refs_2_ = f32[64,256]{1,0:T(8,128)S(1)} collective-permute-done((f32[64,256]{1,0:T(8,128)S(1)}, f32[64,256]{1,0:T(8,128)S(1)}, u32[]{:S(2)}, u32[]{:S(2)}) %collective-permute-start.8) | collective-permute-done | bytes 65568 | tf_op jit(solution)/shard_map/ppermute | solution.py:409
  22.9 2.8 %collective-permute-start.15 = (f32[2,136,256]{2,1,0:T(8,128)S(1)}, f32[2,136,256]{2,1,0:T(8,128)S(1)}, u32[]{:S(2)}, u32[]{:S(2)}) collective-permute-start(f32[2,136,256]{2,1,0:T(8,128)S(1)} %get-tuple-element.27), channel_id=1, source_target_pairs={{4,8},{12,16},{20,24},{28,0},{8,4},{16,12},{24,20},{0,28},{5,9},{1... | collective-permute-start | bytes 835592 | tf_op jit(solution)/shard_map/ppermute | solution.py:415
  25.7 0.8 %collective-permute-start.16 = (f32[136,256]{1,0:T(8,128)S(1)}, f32[136,256]{1,0:T(8,128)S(1)}, u32[]{:S(2)}, u32[]{:S(2)}) collective-permute-start(f32[136,256]{1,0:T(8,128)S(1)} %get-tuple-element.19.refs_0_), channel_id=1, source_target_pairs={{4,8},{12,16},{20,24},{28,0},{8,4},{16,12},{24,20},{0,28},{5,9},{1... | collective-permute-start | bytes 417800 | tf_op jit(solution)/shard_map/ppermute | solution.py:415
  26.5 0.8 %shard_map.120.refs_3_ = f32[56,128]{1,0:T(8,128)S(1)} custom-call(f32[4,136,256]{2,1,0:T(8,128)S(1)} %get-tuple-element.20.refs_0_.own_ref, s32[3,512]{1,0:T(4,128)S(1)} %get-tuple-element.21.refs_1_, f32[2,56,8]{2,1,0:T(8,128)S(1)} %get-tuple-element.22.refs_2_), custom_call_target="tpu_custom_call" | custom-call | flops 88080384 | bytes 566784 | tf_op jit(solution)/shard_map/pallas_call | solution.py:397
  27.3 0.8 %shard_map.121.refs_0_ = f32[56,128]{1,0:T(8,128)S(1)} custom-call(f32[4,136,256]{2,1,0:T(8,128)S(1)} %collective-permute-done.3.refs_0_.pair_ref, s32[3,512]{1,0:T(4,128)S(1)} %get-tuple-element.21.refs_1_, f32[2,56,8]{2,1,0:T(8,128)S(1)} %get-tuple-element.22.refs_2_, f32[56,128]{1,0:T(8,128)S(1)} %shard_map.120.refs_3_), custom_call_target="tpu_custom_call" | custom-call | flops 88080384 | bytes 595456 | tf_op jit(solution)/shard_map/pallas_call | solution.py:397
  28.1 1.0 %collective-permute-start.6 = (f32[56,128]{1,0:T(8,128)S(1)}, f32[56,128]{1,0:T(8,128)S(1)}, u32[]{:S(2)}, u32[]{:S(2)}) collective-permute-start(f32[56,128]{1,0:T(8,128)S(1)} %shard_map.121.refs_0_), channel_id=1, source_target_pairs={{0,24},{4,28},{8,0},{12,4},{16,8},{20,12},{24,16},{28,20},{1,25},{... | collective-permute-start | bytes 86024 | tf_op jit(solution)/shard_map/ppermute | solution.py:409
  29.5 0.7 %collective-permute-start.4 = (f32[56,128]{1,0:T(8,128)S(1)}, f32[56,128]{1,0:T(8,128)S(1)}, u32[]{:S(2)}, u32[]{:S(2)}) collective-permute-start(f32[56,128]{1,0:T(8,128)S(1)} %shard_map.121.refs_0_), channel_id=1, source_target_pairs={{0,8},{4,12},{8,16},{12,20},{16,24},{20,28},{24,0},{28,4},{1,9},{5... | collective-permute-start | bytes 86024 | tf_op jit(solution)/shard_map/ppermute | solution.py:409
  30.6 5.6 %collective-permute-done.6.refs_3_ = f32[56,128]{1,0:T(8,128)S(1)} collective-permute-done((f32[56,128]{1,0:T(8,128)S(1)}, f32[56,128]{1,0:T(8,128)S(1)}, u32[]{:S(2)}, u32[]{:S(2)}) %collective-permute-start.6) | collective-permute-done | bytes 28704 | tf_op jit(solution)/shard_map/ppermute | solution.py:409
  36.2 2.9 %collective-permute-done.5.refs_2_ = f32[56,128]{1,0:T(8,128)S(1)} collective-permute-done((f32[56,128]{1,0:T(8,128)S(1)}, f32[56,128]{1,0:T(8,128)S(1)}, u32[]{:S(2)}, u32[]{:S(2)}) %collective-permute-start.5) | collective-permute-done | bytes 28704 | tf_op jit(solution)/shard_map/ppermute | solution.py:409
  40.1 1.3 %collective-permute-start.12 = (f32[112,256]{1,0:T(8,128)S(1)}, f32[112,256]{1,0:T(8,128)S(1)}, u32[]{:S(2)}, u32[]{:S(2)}) collective-permute-start(f32[112,256]{1,0:T(8,128)S(1)} %shard_map.124.refs_0_), channel_id=1, source_target_pairs={{0,2},{1,3},{2,0},{3,1},{4,6},{5,7},{6,4},{7,5},{8,10},{9,11},{10,... | collective-permute-start | bytes 344072 | tf_op jit(solution)/shard_map/ppermute | solution.py:409
  41.3 0.7 %collective-permute-start.11 = (f32[112,256]{1,0:T(8,128)S(1)}, f32[112,256]{1,0:T(8,128)S(1)}, u32[]{:S(2)}, u32[]{:S(2)}) collective-permute-start(f32[112,256]{1,0:T(8,128)S(1)} %shard_map.124.refs_0_), channel_id=1, source_target_pairs={{0,1},{1,2},{2,3},{3,0},{4,5},{5,6},{6,7},{7,4},{8,9},{9,10},{10,1... | collective-permute-start | bytes 344072 | tf_op jit(solution)/shard_map/ppermute | solution.py:409
  43.2 1.2 %shard_map.128.values_ref = f32[1024,256]{1,0:T(8,128)S(1)} custom-call(bf16[1024,896]{1,0:T(8,128)(2,1)S(1)} %get-tuple-element.28.hot_ref, bf16[896,256]{1,0:T(8,128)(2,1)S(1)} %get-tuple-element.31.high_ref, bf16[896,256]{1,0:T(8,128)(2,1)S(1)} %get-tuple-element.32.low_ref), custom_call_target="tpu_custom_call" | custom-call | flops 100000000 | bytes 5505024 | tf_op jit(solution)/shard_map/pallas_call | solution.py:397
  44.8 1.0 %collective-permute-done.12.refs_2_ = f32[112,256]{1,0:T(8,128)S(1)} collective-permute-done((f32[112,256]{1,0:T(8,128)S(1)}, f32[112,256]{1,0:T(8,128)S(1)}, u32[]{:S(2)}, u32[]{:S(2)}) %collective-permute-start.12) | collective-permute-done | bytes 114720 | tf_op jit(solution)/shard_map/ppermute | solution.py:409
  45.8 1.2 %collective-permute-done.11.refs_1_ = f32[112,256]{1,0:T(8,128)S(1)} collective-permute-done((f32[112,256]{1,0:T(8,128)S(1)}, f32[112,256]{1,0:T(8,128)S(1)}, u32[]{:S(2)}, u32[]{:S(2)}) %collective-permute-start.11) | collective-permute-done | bytes 114720 | tf_op jit(solution)/shard_map/ppermute | solution.py:409
  47.2 3.2 %shard_map.129.nearby_ref = f32[128,256]{1,0:T(8,128)S(1)} custom-call(f32[4,136,256]{2,1,0:T(8,128)S(1)} %get-tuple-element.20.refs_0_.own_ref, f32[2,136,256]{2,1,0:T(8,128)S(1)} %collective-permute-done.15.sides_ref, bf16[1024,896]{1,0:T(8,128)(2,1)S(1)} %get-tuple-element.28.hot_ref, bf16[1024,256]{1,0:T(8,128)(2,1)S(1)} %get-tuple-element.29.far_ref, ...), custom_call_target="tpu_custom_call" | custom-call | flops 4000000000 | bytes 7716864 | tf_op jit(solution)/shard_map/pallas_call | solution.py:397
  50.4 0.9 %shard_map.130 = f32[128,256]{1,0:T(8,128)} custom-call(f32[112,256]{1,0:T(8,128)S(1)} %shard_map.125.own_ref, f32[112,256]{1,0:T(8,128)S(1)} %collective-permute-done.14.pair_ref, bf16[128,224]{1,0:T(8,128)(2,1)S(1)} %get-tuple-element.25.high_ref, bf16[128,224]{1,0:T(8,128)(2,1)S(1)} %get-tuple-element.26.low_ref, f32[128,256]{1,0:T(8,128)S(1)} %shard_map.129.nearby_ref), custom_call_target="tpu_custom_call" | custom-call | flops 44040192 | bytes 589824 | tf_op jit(solution)/shard_map/pallas_call | solution.py:397
  (35 shorter events, 4.9 us)
Async XLA Ops:
  1.0 41.0 %copy-start.4 = (s32[1,1,128,8]{2,3,1,0:T(8,128)S(1)}, s32[1,1,128,8]{2,3,1,0:T(8,128)}, u32[]{:S(2)}) copy-start(s32[1,1,128,8]{2,3,1,0:T(8,128)} %param.15) | copy-start | bytes 12292
  1.0 41.0 %copy-start.5 = (s32[1,1,128,8]{2,3,1,0:T(8,128)S(1)}, s32[1,1,128,8]{2,3,1,0:T(8,128)}, u32[]{:S(2)}) copy-start(s32[1,1,128,8]{2,3,1,0:T(8,128)} %param.16) | copy-start | bytes 12292
  1.0 8.0 %collective-permute-start.2 = (f32[136,256]{1,0:T(8,128)S(1)}, f32[136,256]{1,0:T(8,128)S(1)}, u32[]{:S(2)}, u32[]{:S(2)}) collective-permute-start(f32[136,256]{1,0:T(8,128)S(1)} %get-tuple-element.19.refs_0_), channel_id=1, source_target_pairs={{0,3},{1,0},{2,1},{3,2},{4,7},{5,4},{6,5},{7,6},{8,11},{9,8},{10,9... | collective-permute-start | bytes 417800 | tf_op jit(solution)/shard_map/ppermute | solution.py:409
  5.0 8.1 %collective-permute-start.1 = (f32[136,256]{1,0:T(8,128)S(1)}, f32[136,256]{1,0:T(8,128)S(1)}, u32[]{:S(2)}, u32[]{:S(2)}) collective-permute-start(f32[136,256]{1,0:T(8,128)S(1)} %get-tuple-element.19.refs_0_), channel_id=1, source_target_pairs={{0,2},{1,3},{2,0},{3,1},{4,6},{5,7},{6,4},{7,5},{8,10},{9,11},{10,... | collective-permute-start | bytes 417800 | tf_op jit(solution)/shard_map/ppermute | solution.py:409
  5.5 7.6 %collective-permute-start = (f32[136,256]{1,0:T(8,128)S(1)}, f32[136,256]{1,0:T(8,128)S(1)}, u32[]{:S(2)}, u32[]{:S(2)}) collective-permute-start(f32[136,256]{1,0:T(8,128)S(1)} %get-tuple-element.19.refs_0_), channel_id=1, source_target_pairs={{0,1},{1,2},{2,3},{3,0},{4,5},{5,6},{6,7},{7,4},{8,9},{9,10},{10,1... | collective-permute-start | bytes 417800 | tf_op jit(solution)/shard_map/ppermute | solution.py:409
  13.2 29.4 %copy-start = (f32[256,256]{1,0:T(8,128)S(1)}, f32[256,256]{1,0:T(8,128)}, u32[]{:S(2)}) copy-start(f32[256,256]{1,0:T(8,128)} %value_ref.3) | copy-start | bytes 786436
  13.2 14.1 %collective-permute-start.3 = (f32[4,136,256]{2,1,0:T(8,128)S(1)}, f32[4,136,256]{2,1,0:T(8,128)S(1)}, u32[]{:S(2)}, u32[]{:S(2)}) collective-permute-start(f32[4,136,256]{2,1,0:T(8,128)S(1)} %get-tuple-element.20.refs_0_.own_ref), channel_id=1, source_target_pairs={{0,4},{8,12},{16,20},{24,28},{4,0},{12,8},{20,16},{28,24},{1,5},{9... | collective-permute-start | bytes 1671176 | tf_op jit(solution)/shard_map/ppermute | solution.py:415
  13.3 6.5 %collective-permute-start.9 = (f32[64,256]{1,0:T(8,128)S(1)}, f32[64,256]{1,0:T(8,128)S(1)}, u32[]{:S(2)}, u32[]{:S(2)}) collective-permute-start(f32[64,256]{1,0:T(8,128)S(1)} %get-tuple-element.23.refs_0_), channel_id=1, source_target_pairs={{0,8},{4,12},{8,16},{12,20},{16,24},{20,28},{24,0},{28,4},{1,9},{5... | collective-permute-start | bytes 196616 | tf_op jit(solution)/shard_map/ppermute | solution.py:409
  14.9 7.6 %collective-permute-start.8 = (f32[64,256]{1,0:T(8,128)S(1)}, f32[64,256]{1,0:T(8,128)S(1)}, u32[]{:S(2)}, u32[]{:S(2)}) collective-permute-start(f32[64,256]{1,0:T(8,128)S(1)} %get-tuple-element.23.refs_0_), channel_id=1, source_target_pairs={{0,16},{4,20},{8,24},{12,28},{16,0},{20,4},{24,8},{28,12},{1,17},{... | collective-permute-start | bytes 196616 | tf_op jit(solution)/shard_map/ppermute | solution.py:409
  17.5 5.3 %collective-permute-start.7 = (f32[64,256]{1,0:T(8,128)S(1)}, f32[64,256]{1,0:T(8,128)S(1)}, u32[]{:S(2)}, u32[]{:S(2)}) collective-permute-start(f32[64,256]{1,0:T(8,128)S(1)} %get-tuple-element.23.refs_0_), channel_id=1, source_target_pairs={{0,24},{4,28},{8,0},{12,4},{16,8},{20,12},{24,16},{28,20},{1,25},{... | collective-permute-start | bytes 196616 | tf_op jit(solution)/shard_map/ppermute | solution.py:409
  22.8 6.7 %collective-permute-start.10 = (f32[4,64,256]{2,1,0:T(8,128)S(1)}, f32[4,64,256]{2,1,0:T(8,128)S(1)}, u32[]{:S(2)}, u32[]{:S(2)}) collective-permute-start(f32[4,64,256]{2,1,0:T(8,128)S(1)} %shard_map.122.refs_4_), channel_id=1, source_target_pairs={{0,4},{8,12},{16,20},{24,28},{4,0},{12,8},{20,16},{28,24},{1,5},{9... | collective-permute-start | bytes 786440 | tf_op jit(solution)/shard_map/ppermute | solution.py:415
  22.9 24.2 %collective-permute-start.15 = (f32[2,136,256]{2,1,0:T(8,128)S(1)}, f32[2,136,256]{2,1,0:T(8,128)S(1)}, u32[]{:S(2)}, u32[]{:S(2)}) collective-permute-start(f32[2,136,256]{2,1,0:T(8,128)S(1)} %get-tuple-element.27), channel_id=1, source_target_pairs={{4,8},{12,16},{20,24},{28,0},{8,4},{16,12},{24,20},{0,28},{5,9},{1... | collective-permute-start | bytes 835592 | tf_op jit(solution)/shard_map/ppermute | solution.py:415
  25.7 16.9 %collective-permute-start.16 = (f32[136,256]{1,0:T(8,128)S(1)}, f32[136,256]{1,0:T(8,128)S(1)}, u32[]{:S(2)}, u32[]{:S(2)}) collective-permute-start(f32[136,256]{1,0:T(8,128)S(1)} %get-tuple-element.19.refs_0_), channel_id=1, source_target_pairs={{4,8},{12,16},{20,24},{28,0},{8,4},{16,12},{24,20},{0,28},{5,9},{1... | collective-permute-start | bytes 417800 | tf_op jit(solution)/shard_map/ppermute | solution.py:415
  28.1 8.0 %collective-permute-start.6 = (f32[56,128]{1,0:T(8,128)S(1)}, f32[56,128]{1,0:T(8,128)S(1)}, u32[]{:S(2)}, u32[]{:S(2)}) collective-permute-start(f32[56,128]{1,0:T(8,128)S(1)} %shard_map.121.refs_0_), channel_id=1, source_target_pairs={{0,24},{4,28},{8,0},{12,4},{16,8},{20,12},{24,16},{28,20},{1,25},{... | collective-permute-start | bytes 86024 | tf_op jit(solution)/shard_map/ppermute | solution.py:409
  29.1 10.0 %collective-permute-start.5 = (f32[56,128]{1,0:T(8,128)S(1)}, f32[56,128]{1,0:T(8,128)S(1)}, u32[]{:S(2)}, u32[]{:S(2)}) collective-permute-start(f32[56,128]{1,0:T(8,128)S(1)} %shard_map.121.refs_0_), channel_id=1, source_target_pairs={{0,16},{4,20},{8,24},{12,28},{16,0},{20,4},{24,8},{28,12},{1,17},{... | collective-permute-start | bytes 86024 | tf_op jit(solution)/shard_map/ppermute | solution.py:409
  29.5 9.6 %collective-permute-start.4 = (f32[56,128]{1,0:T(8,128)S(1)}, f32[56,128]{1,0:T(8,128)S(1)}, u32[]{:S(2)}, u32[]{:S(2)}) collective-permute-start(f32[56,128]{1,0:T(8,128)S(1)} %shard_map.121.refs_0_), channel_id=1, source_target_pairs={{0,8},{4,12},{8,16},{12,20},{16,24},{20,28},{24,0},{28,4},{1,9},{5... | collective-permute-start | bytes 86024 | tf_op jit(solution)/shard_map/ppermute | solution.py:409
  39.5 5.3 %collective-permute-start.13 = (f32[112,256]{1,0:T(8,128)S(1)}, f32[112,256]{1,0:T(8,128)S(1)}, u32[]{:S(2)}, u32[]{:S(2)}) collective-permute-start(f32[112,256]{1,0:T(8,128)S(1)} %shard_map.124.refs_0_), channel_id=1, source_target_pairs={{0,3},{1,0},{2,1},{3,2},{4,7},{5,4},{6,5},{7,6},{8,11},{9,8},{10,9... | collective-permute-start | bytes 344072 | tf_op jit(solution)/shard_map/ppermute | solution.py:409
  40.1 5.7 %collective-permute-start.12 = (f32[112,256]{1,0:T(8,128)S(1)}, f32[112,256]{1,0:T(8,128)S(1)}, u32[]{:S(2)}, u32[]{:S(2)}) collective-permute-start(f32[112,256]{1,0:T(8,128)S(1)} %shard_map.124.refs_0_), channel_id=1, source_target_pairs={{0,2},{1,3},{2,0},{3,1},{4,6},{5,7},{6,4},{7,5},{8,10},{9,11},{10,... | collective-permute-start | bytes 344072 | tf_op jit(solution)/shard_map/ppermute | solution.py:409
  41.3 5.7 %collective-permute-start.11 = (f32[112,256]{1,0:T(8,128)S(1)}, f32[112,256]{1,0:T(8,128)S(1)}, u32[]{:S(2)}, u32[]{:S(2)}) collective-permute-start(f32[112,256]{1,0:T(8,128)S(1)} %shard_map.124.refs_0_), channel_id=1, source_target_pairs={{0,1},{1,2},{2,3},{3,0},{4,5},{5,6},{6,7},{7,4},{8,9},{9,10},{10,1... | collective-permute-start | bytes 344072 | tf_op jit(solution)/shard_map/ppermute | solution.py:409
  43.2 3.9 %copy-start.1 = (f32[256,256]{1,0:T(8,128)S(1)}, f32[256,256]{1,0:T(8,128)}, u32[]{:S(2)}) copy-start(f32[256,256]{1,0:T(8,128)} %mixing_ref.1) | copy-start | bytes 786436
  43.2 3.9 %copy-start.2 = (f32[64,256]{1,0:T(8,128)S(1)}, f32[64,256]{1,0:T(8,128)}, u32[]{:S(2)}) copy-start(f32[64,256]{1,0:T(8,128)} %radial_ref.1) | copy-start | bytes 196612
  43.2 3.9 %copy-start.3 = (f32[64,256]{1,0:T(8,128)S(1)}, f32[64,256]{1,0:T(8,128)}, u32[]{:S(2)}) copy-start(f32[64,256]{1,0:T(8,128)} %embed_ref.1) | copy-start | bytes 196612
  47.0 3.4 %collective-permute-start.14 = (f32[112,256]{1,0:T(8,128)S(1)}, f32[112,256]{1,0:T(8,128)S(1)}, u32[]{:S(2)}, u32[]{:S(2)}) collective-permute-start(f32[112,256]{1,0:T(8,128)S(1)} %shard_map.125.own_ref), channel_id=1, source_target_pairs={{0,4},{8,12},{16,20},{24,28},{4,0},{12,8},{20,16},{28,24},{1,5},{9... | collective-permute-start | bytes 344072 | tf_op jit(solution)/shard_map/ppermute | solution.py:415

commit v4 on v3

--- a/solution.py
+++ b/solution.py
@@ -193,13 +193,13 @@
 def table_kernel(sizes, rows, canonical, *refs):
     _, _, span0, span1, group = sizes
     own_ref, vectors_ref = refs[:2]
-    basis_ref, (high_ref, low_ref, weight_ref) = refs[2] if canonical else None, refs[-3:]
+    basis_ref, weight_ref = refs[2] if canonical else None, refs[-1]
+    halves = (refs[-5:-3], refs[-3:-1])
     lateral, transverse, parity = place()
     sides = [rows_of(basis_ref, vectors_ref, rows, p) for p in (parity, 1 - parity)]
-    parts = []
-    for triples in sides:
-        parts.extend(phases(sizes, triples, lateral, transverse, own_ref.at[0]))
-    high_ref[...], low_ref[...] = split(jnp.transpose(jnp.concatenate(parts, axis=0)))
+    for triples, half in zip(sides, halves):
+        parts = phases(sizes, triples, lateral, transverse, own_ref.at[0])
+        half[0][...], half[1][...] = split(jnp.transpose(jnp.concatenate(parts, axis=0)))
 
     n0, n1, n2 = sides[0]
     waves = (FULL_TURN * n0 / span0, FULL_TURN * n1 / span1, FULL_TURN * n2)
@@ -255,9 +255,9 @@
     refs[-1][...] = total
 
 
-def project_kernel(scale, own_ref, pair_ref, high_ref, low_ref, nearby_ref, out_ref):
-    filtered = split(jnp.concatenate([own_ref[...], pair_ref[...]], axis=0) * scale)
-    out_ref[...] = nearby_ref[...] + dot3((high_ref[...], low_ref[...]), filtered)
+def project_kernel(scale, filtered_ref, high_ref, low_ref, sum_ref, out_ref):
+    filtered = split(filtered_ref[...] * scale)
+    out_ref[...] = sum_ref[...] + dot3((high_ref[...], low_ref[...]), filtered)
 
 
 def hot_kernel(sizes, listed_ref, mask_ref, known_ref, far_ref):
@@ -501,10 +501,10 @@
     pair_weights = swap(weights)
     sides = swap(sides, first=1)
 
-    table = jax.ShapeDtypeStruct((atoms, 4 * rows), BF16)
-    high, low, shares = call(
+    table = jax.ShapeDtypeStruct((atoms, 2 * rows), BF16)
+    *halves, shares = call(
         functools.partial(table_kernel, sizes, rows, canonical),
-        [table, table, jax.ShapeDtypeStruct((rows, span0), F32)],
+        [table] * 4 + [jax.ShapeDtypeStruct((rows, span0), F32)],
         (own, *vectors),
         10**8,
     )
@@ -562,12 +562,14 @@
     )
 
     scale = 1.0 / math.sqrt(atoms * span0 * span1 * modes)
-    result = call(
-        functools.partial(project_kernel, scale),
-        jax.ShapeDtypeStruct((atoms, channels), F32),
-        (filtered, pair_filtered, high, low, nearby),
-        24 * rows * atoms * channels,
-    )
+    result = nearby
+    for half, tables in ((filtered, halves[:2]), (pair_filtered, halves[2:])):
+        result = call(
+            functools.partial(project_kernel, scale),
+            jax.ShapeDtypeStruct((atoms, channels), F32),
+            (half, *tables, result),
+            12 * rows * atoms * channels,
+        )
     return result[None, None]
 
 

time: 51.4 us -> 51.6 us (level)
    pallas_call x13 -> x14, Pallas kernels: 10 us -> 10.2 us  [call(): pl.pallas_call(kernel, out_shape=out_shape, in_specs=specs, scratch_shape...]
where the time goes in v4:
time: 51.6 us; the launch traced here: 51.5 us
  waiting for transfers between devices  21.9 us (42%)
  starting transfers between devices  19.1 us (37%)
  Pallas kernels  10.2 us (20%)
    ppermute x12, waiting for transfers between devices, shift(): return lax.ppermute(x, axis, [(i, (i + by) % count) for i in range(count)])  21.9 us
    ppermute x12, starting transfers between devices, shift(): return lax.ppermute(x, axis, [(i, (i + by) % count) for i in range(count)])  15.3 us
    pallas_call x14, Pallas kernels, call(): pl.pallas_call(kernel, out_shape=out_shape, in_specs=specs, scratch_shape...  10.2 us
    ppermute x5, starting transfers between devices, swap(): return lax.ppermute(x, 'gx', one + [(b, a) for a, b in one])  3.82 us
  transfers between devices with their start and end apart: 17, of which 10 were waited for; matrix products, arithmetic and copies ran while one was open for 0% of the time, Pallas kernels for 16%

profile of v4, /device:TPU:0, one launch (start us, length us, event | category | flops | bytes accessed | tf_op | source)
XLA Modules:
  0.0 51.5 jit_solution(16537979667633788580)
XLA Ops:
  0.0 1.0 %shard_map.118 = (f32[136,256]{1,0:T(8,128)S(1)}, f32[64,256]{1,0:T(8,128)S(1)}, s32[3,512]{1,0:T(4,128)S(1)}, f32[2,56,8]{2,1,0:T(8,128)S(1)}) custom-call(f32[1,1,128,256]{3,2,1,0:T(8,128)} %features_ref.1, f32[1,3,1,128]{3,2,1,0:T(1,128)} %bitcast.10, s32[1,1,128]{2,1,0:T(1,128)} %species_ref.1, f32[1,256,256]{2,1,0:T(8,128)} %weight_ref.1, ...), custom_call_target="tpu_custom_call" | custom-call | flops 1000000 | bytes 404992 | tf_op jit(solution)/shard_map/pallas_call | solution.py:397
  1.0 4.0 %collective-permute-start.2 = (f32[136,256]{1,0:T(8,128)S(1)}, f32[136,256]{1,0:T(8,128)S(1)}, u32[]{:S(2)}, u32[]{:S(2)}) collective-permute-start(f32[136,256]{1,0:T(8,128)S(1)} %get-tuple-element.21.refs_0_), channel_id=1, source_target_pairs={{0,3},{1,0},{2,1},{3,2},{4,7},{5,4},{6,5},{7,6},{8,11},{9,8},{10,9... | collective-permute-start | bytes 417800 | tf_op jit(solution)/shard_map/ppermute | solution.py:409
  6.1 3.0 %collective-permute-done.2.refs_3_ = f32[136,256]{1,0:T(8,128)S(1)} collective-permute-done((f32[136,256]{1,0:T(8,128)S(1)}, f32[136,256]{1,0:T(8,128)S(1)}, u32[]{:S(2)}, u32[]{:S(2)}) %collective-permute-start.2) | collective-permute-done | bytes 139296 | tf_op jit(solution)/shard_map/ppermute | solution.py:409
  9.1 4.1 %collective-permute-done.1.refs_2_ = f32[136,256]{1,0:T(8,128)S(1)} collective-permute-done((f32[136,256]{1,0:T(8,128)S(1)}, f32[136,256]{1,0:T(8,128)S(1)}, u32[]{:S(2)}, u32[]{:S(2)}) %collective-permute-start.1) | collective-permute-done | bytes 139296 | tf_op jit(solution)/shard_map/ppermute | solution.py:409
  13.3 1.6 %collective-permute-start.9 = (f32[64,256]{1,0:T(8,128)S(1)}, f32[64,256]{1,0:T(8,128)S(1)}, u32[]{:S(2)}, u32[]{:S(2)}) collective-permute-start(f32[64,256]{1,0:T(8,128)S(1)} %get-tuple-element.25.refs_0_), channel_id=1, source_target_pairs={{0,8},{4,12},{8,16},{12,20},{16,24},{20,28},{24,0},{28,4},{1,9},{5... | collective-permute-start | bytes 196616 | tf_op jit(solution)/shard_map/ppermute | solution.py:409
  14.9 2.6 %collective-permute-start.8 = (f32[64,256]{1,0:T(8,128)S(1)}, f32[64,256]{1,0:T(8,128)S(1)}, u32[]{:S(2)}, u32[]{:S(2)}) collective-permute-start(f32[64,256]{1,0:T(8,128)S(1)} %get-tuple-element.25.refs_0_), channel_id=1, source_target_pairs={{0,16},{4,20},{8,24},{12,28},{16,0},{20,4},{24,8},{28,12},{1,17},{... | collective-permute-start | bytes 196616 | tf_op jit(solution)/shard_map/ppermute | solution.py:409
  17.5 1.3 %collective-permute-start.7 = (f32[64,256]{1,0:T(8,128)S(1)}, f32[64,256]{1,0:T(8,128)S(1)}, u32[]{:S(2)}, u32[]{:S(2)}) collective-permute-start(f32[64,256]{1,0:T(8,128)S(1)} %get-tuple-element.25.refs_0_), channel_id=1, source_target_pairs={{0,24},{4,28},{8,0},{12,4},{16,8},{20,12},{24,16},{28,20},{1,25},{... | collective-permute-start | bytes 196616 | tf_op jit(solution)/shard_map/ppermute | solution.py:409
  18.9 0.9 %collective-permute-done.9.refs_3_ = f32[64,256]{1,0:T(8,128)S(1)} collective-permute-done((f32[64,256]{1,0:T(8,128)S(1)}, f32[64,256]{1,0:T(8,128)S(1)}, u32[]{:S(2)}, u32[]{:S(2)}) %collective-permute-start.9) | collective-permute-done | bytes 65568 | tf_op jit(solution)/shard_map/ppermute | solution.py:409
  19.8 2.8 %collective-permute-done.8.refs_2_ = f32[64,256]{1,0:T(8,128)S(1)} collective-permute-done((f32[64,256]{1,0:T(8,128)S(1)}, f32[64,256]{1,0:T(8,128)S(1)}, u32[]{:S(2)}, u32[]{:S(2)}) %collective-permute-start.8) | collective-permute-done | bytes 65568 | tf_op jit(solution)/shard_map/ppermute | solution.py:409
  22.9 2.8 %collective-permute-start.15 = (f32[2,136,256]{2,1,0:T(8,128)S(1)}, f32[2,136,256]{2,1,0:T(8,128)S(1)}, u32[]{:S(2)}, u32[]{:S(2)}) collective-permute-start(f32[2,136,256]{2,1,0:T(8,128)S(1)} %get-tuple-element.31), channel_id=1, source_target_pairs={{4,8},{12,16},{20,24},{28,0},{8,4},{16,12},{24,20},{0,28},{5,9},{1... | collective-permute-start | bytes 835592 | tf_op jit(solution)/shard_map/ppermute | solution.py:415
  25.7 0.8 %collective-permute-start.16 = (f32[136,256]{1,0:T(8,128)S(1)}, f32[136,256]{1,0:T(8,128)S(1)}, u32[]{:S(2)}, u32[]{:S(2)}) collective-permute-start(f32[136,256]{1,0:T(8,128)S(1)} %get-tuple-element.21.refs_0_), channel_id=1, source_target_pairs={{4,8},{12,16},{20,24},{28,0},{8,4},{16,12},{24,20},{0,28},{5,9},{1... | collective-permute-start | bytes 417800 | tf_op jit(solution)/shard_map/ppermute | solution.py:415
  26.5 0.8 %shard_map.120.refs_3_ = f32[56,128]{1,0:T(8,128)S(1)} custom-call(f32[4,136,256]{2,1,0:T(8,128)S(1)} %get-tuple-element.22.refs_0_.own_ref, s32[3,512]{1,0:T(4,128)S(1)} %get-tuple-element.23.refs_1_, f32[2,56,8]{2,1,0:T(8,128)S(1)} %get-tuple-element.24.refs_2_), custom_call_target="tpu_custom_call" | custom-call | flops 88080384 | bytes 566784 | tf_op jit(solution)/shard_map/pallas_call | solution.py:397
  27.3 0.8 %shard_map.121.refs_0_ = f32[56,128]{1,0:T(8,128)S(1)} custom-call(f32[4,136,256]{2,1,0:T(8,128)S(1)} %collective-permute-done.3.refs_0_.pair_ref, s32[3,512]{1,0:T(4,128)S(1)} %get-tuple-element.23.refs_1_, f32[2,56,8]{2,1,0:T(8,128)S(1)} %get-tuple-element.24.refs_2_, f32[56,128]{1,0:T(8,128)S(1)} %shard_map.120.refs_3_), custom_call_target="tpu_custom_call" | custom-call | flops 88080384 | bytes 595456 | tf_op jit(solution)/shard_map/pallas_call | solution.py:397
  28.1 1.0 %collective-permute-start.6 = (f32[56,128]{1,0:T(8,128)S(1)}, f32[56,128]{1,0:T(8,128)S(1)}, u32[]{:S(2)}, u32[]{:S(2)}) collective-permute-start(f32[56,128]{1,0:T(8,128)S(1)} %shard_map.121.refs_0_), channel_id=1, source_target_pairs={{0,24},{4,28},{8,0},{12,4},{16,8},{20,12},{24,16},{28,20},{1,25},{... | collective-permute-start | bytes 86024 | tf_op jit(solution)/shard_map/ppermute | solution.py:409
  29.5 0.7 %collective-permute-start.4 = (f32[56,128]{1,0:T(8,128)S(1)}, f32[56,128]{1,0:T(8,128)S(1)}, u32[]{:S(2)}, u32[]{:S(2)}) collective-permute-start(f32[56,128]{1,0:T(8,128)S(1)} %shard_map.121.refs_0_), channel_id=1, source_target_pairs={{0,8},{4,12},{8,16},{12,20},{16,24},{20,28},{24,0},{28,4},{1,9},{5... | collective-permute-start | bytes 86024 | tf_op jit(solution)/shard_map/ppermute | solution.py:409
  30.6 5.6 %collective-permute-done.6.refs_3_ = f32[56,128]{1,0:T(8,128)S(1)} collective-permute-done((f32[56,128]{1,0:T(8,128)S(1)}, f32[56,128]{1,0:T(8,128)S(1)}, u32[]{:S(2)}, u32[]{:S(2)}) %collective-permute-start.6) | collective-permute-done | bytes 28704 | tf_op jit(solution)/shard_map/ppermute | solution.py:409
  36.2 2.9 %collective-permute-done.5.refs_2_ = f32[56,128]{1,0:T(8,128)S(1)} collective-permute-done((f32[56,128]{1,0:T(8,128)S(1)}, f32[56,128]{1,0:T(8,128)S(1)}, u32[]{:S(2)}, u32[]{:S(2)}) %collective-permute-start.5) | collective-permute-done | bytes 28704 | tf_op jit(solution)/shard_map/ppermute | solution.py:409
  40.1 1.3 %collective-permute-start.12 = (f32[112,256]{1,0:T(8,128)S(1)}, f32[112,256]{1,0:T(8,128)S(1)}, u32[]{:S(2)}, u32[]{:S(2)}) collective-permute-start(f32[112,256]{1,0:T(8,128)S(1)} %shard_map.124.refs_0_), channel_id=1, source_target_pairs={{0,2},{1,3},{2,0},{3,1},{4,6},{5,7},{6,4},{7,5},{8,10},{9,11},{10,... | collective-permute-start | bytes 344072 | tf_op jit(solution)/shard_map/ppermute | solution.py:409
  41.3 0.7 %collective-permute-start.11 = (f32[112,256]{1,0:T(8,128)S(1)}, f32[112,256]{1,0:T(8,128)S(1)}, u32[]{:S(2)}, u32[]{:S(2)}) collective-permute-start(f32[112,256]{1,0:T(8,128)S(1)} %shard_map.124.refs_0_), channel_id=1, source_target_pairs={{0,1},{1,2},{2,3},{3,0},{4,5},{5,6},{6,7},{7,4},{8,9},{9,10},{10,1... | collective-permute-start | bytes 344072 | tf_op jit(solution)/shard_map/ppermute | solution.py:409
  43.2 1.2 %shard_map.128.values_ref = f32[1024,256]{1,0:T(8,128)S(1)} custom-call(bf16[1024,896]{1,0:T(8,128)(2,1)S(1)} %get-tuple-element.32.hot_ref, bf16[896,256]{1,0:T(8,128)(2,1)S(1)} %get-tuple-element.35.high_ref, bf16[896,256]{1,0:T(8,128)(2,1)S(1)} %get-tuple-element.36.low_ref), custom_call_target="tpu_custom_call" | custom-call | flops 100000000 | bytes 5505024 | tf_op jit(solution)/shard_map/pallas_call | solution.py:397
  44.8 1.0 %collective-permute-done.12.refs_2_ = f32[112,256]{1,0:T(8,128)S(1)} collective-permute-done((f32[112,256]{1,0:T(8,128)S(1)}, f32[112,256]{1,0:T(8,128)S(1)}, u32[]{:S(2)}, u32[]{:S(2)}) %collective-permute-start.12) | collective-permute-done | bytes 114720 | tf_op jit(solution)/shard_map/ppermute | solution.py:409
  45.8 1.2 %collective-permute-done.11.refs_1_ = f32[112,256]{1,0:T(8,128)S(1)} collective-permute-done((f32[112,256]{1,0:T(8,128)S(1)}, f32[112,256]{1,0:T(8,128)S(1)}, u32[]{:S(2)}, u32[]{:S(2)}) %collective-permute-start.11) | collective-permute-done | bytes 114720 | tf_op jit(solution)/shard_map/ppermute | solution.py:409
  47.2 3.2 %shard_map.129.sum_ref = f32[128,256]{1,0:T(8,128)S(1)} custom-call(f32[4,136,256]{2,1,0:T(8,128)S(1)} %get-tuple-element.22.refs_0_.own_ref, f32[2,136,256]{2,1,0:T(8,128)S(1)} %collective-permute-done.15.sides_ref, bf16[1024,896]{1,0:T(8,128)(2,1)S(1)} %get-tuple-element.32.hot_ref, bf16[1024,256]{1,0:T(8,128)(2,1)S(1)} %get-tuple-element.33.far_ref, ...), custom_call_target="tpu_custom_call" | custom-call | flops 4000000000 | bytes 7716864 | tf_op jit(solution)/shard_map/pallas_call | solution.py:397
  50.6 0.9 %shard_map.131 = f32[128,256]{1,0:T(8,128)} custom-call(f32[112,256]{1,0:T(8,128)S(1)} %collective-permute-done.14.filtered_ref, bf16[128,112]{1,0:T(8,128)(2,1)S(1)} %get-tuple-element.27.high_ref, bf16[128,112]{1,0:T(8,128)(2,1)S(1)} %get-tuple-element.28.low_ref, f32[128,256]{1,0:T(8,128)S(1)} %shard_map.130.sum_ref), custom_call_target="tpu_custom_call" | custom-call | flops 22020096 | bytes 360448 | tf_op jit(solution)/shard_map/pallas_call | solution.py:397
  (36 shorter events, 5.1 us)
Async XLA Ops:
  1.0 41.0 %copy-start.4 = (s32[1,1,128,8]{2,3,1,0:T(8,128)S(1)}, s32[1,1,128,8]{2,3,1,0:T(8,128)}, u32[]{:S(2)}) copy-start(s32[1,1,128,8]{2,3,1,0:T(8,128)} %param.15) | copy-start | bytes 12292
  1.0 41.0 %copy-start.5 = (s32[1,1,128,8]{2,3,1,0:T(8,128)S(1)}, s32[1,1,128,8]{2,3,1,0:T(8,128)}, u32[]{:S(2)}) copy-start(s32[1,1,128,8]{2,3,1,0:T(8,128)} %param.16) | copy-start | bytes 12292
  1.0 8.0 %collective-permute-start.2 = (f32[136,256]{1,0:T(8,128)S(1)}, f32[136,256]{1,0:T(8,128)S(1)}, u32[]{:S(2)}, u32[]{:S(2)}) collective-permute-start(f32[136,256]{1,0:T(8,128)S(1)} %get-tuple-element.21.refs_0_), channel_id=1, source_target_pairs={{0,3},{1,0},{2,1},{3,2},{4,7},{5,4},{6,5},{7,6},{8,11},{9,8},{10,9... | collective-permute-start | bytes 417800 | tf_op jit(solution)/shard_map/ppermute | solution.py:409
  5.0 8.1 %collective-permute-start.1 = (f32[136,256]{1,0:T(8,128)S(1)}, f32[136,256]{1,0:T(8,128)S(1)}, u32[]{:S(2)}, u32[]{:S(2)}) collective-permute-start(f32[136,256]{1,0:T(8,128)S(1)} %get-tuple-element.21.refs_0_), channel_id=1, source_target_pairs={{0,2},{1,3},{2,0},{3,1},{4,6},{5,7},{6,4},{7,5},{8,10},{9,11},{10,... | collective-permute-start | bytes 417800 | tf_op jit(solution)/shard_map/ppermute | solution.py:409
  5.5 7.6 %collective-permute-start = (f32[136,256]{1,0:T(8,128)S(1)}, f32[136,256]{1,0:T(8,128)S(1)}, u32[]{:S(2)}, u32[]{:S(2)}) collective-permute-start(f32[136,256]{1,0:T(8,128)S(1)} %get-tuple-element.21.refs_0_), channel_id=1, source_target_pairs={{0,1},{1,2},{2,3},{3,0},{4,5},{5,6},{6,7},{7,4},{8,9},{9,10},{10,1... | collective-permute-start | bytes 417800 | tf_op jit(solution)/shard_map/ppermute | solution.py:409
  13.2 29.4 %copy-start = (f32[256,256]{1,0:T(8,128)S(1)}, f32[256,256]{1,0:T(8,128)}, u32[]{:S(2)}) copy-start(f32[256,256]{1,0:T(8,128)} %value_ref.3) | copy-start | bytes 786436
  13.2 14.1 %collective-permute-start.3 = (f32[4,136,256]{2,1,0:T(8,128)S(1)}, f32[4,136,256]{2,1,0:T(8,128)S(1)}, u32[]{:S(2)}, u32[]{:S(2)}) collective-permute-start(f32[4,136,256]{2,1,0:T(8,128)S(1)} %get-tuple-element.22.refs_0_.own_ref), channel_id=1, source_target_pairs={{0,4},{8,12},{16,20},{24,28},{4,0},{12,8},{20,16},{28,24},{1,5},{9... | collective-permute-start | bytes 1671176 | tf_op jit(solution)/shard_map/ppermute | solution.py:415
  13.3 6.5 %collective-permute-start.9 = (f32[64,256]{1,0:T(8,128)S(1)}, f32[64,256]{1,0:T(8,128)S(1)}, u32[]{:S(2)}, u32[]{:S(2)}) collective-permute-start(f32[64,256]{1,0:T(8,128)S(1)} %get-tuple-element.25.refs_0_), channel_id=1, source_target_pairs={{0,8},{4,12},{8,16},{12,20},{16,24},{20,28},{24,0},{28,4},{1,9},{5... | collective-permute-start | bytes 196616 | tf_op jit(solution)/shard_map/ppermute | solution.py:409
  14.9 7.6 %collective-permute-start.8 = (f32[64,256]{1,0:T(8,128)S(1)}, f32[64,256]{1,0:T(8,128)S(1)}, u32[]{:S(2)}, u32[]{:S(2)}) collective-permute-start(f32[64,256]{1,0:T(8,128)S(1)} %get-tuple-element.25.refs_0_), channel_id=1, source_target_pairs={{0,16},{4,20},{8,24},{12,28},{16,0},{20,4},{24,8},{28,12},{1,17},{... | collective-permute-start | bytes 196616 | tf_op jit(solution)/shard_map/ppermute | solution.py:409
  17.5 5.3 %collective-permute-start.7 = (f32[64,256]{1,0:T(8,128)S(1)}, f32[64,256]{1,0:T(8,128)S(1)}, u32[]{:S(2)}, u32[]{:S(2)}) collective-permute-start(f32[64,256]{1,0:T(8,128)S(1)} %get-tuple-element.25.refs_0_), channel_id=1, source_target_pairs={{0,24},{4,28},{8,0},{12,4},{16,8},{20,12},{24,16},{28,20},{1,25},{... | collective-permute-start | bytes 196616 | tf_op jit(solution)/shard_map/ppermute | solution.py:409
  22.8 6.7 %collective-permute-start.10 = (f32[4,64,256]{2,1,0:T(8,128)S(1)}, f32[4,64,256]{2,1,0:T(8,128)S(1)}, u32[]{:S(2)}, u32[]{:S(2)}) collective-permute-start(f32[4,64,256]{2,1,0:T(8,128)S(1)} %shard_map.122.refs_4_), channel_id=1, source_target_pairs={{0,4},{8,12},{16,20},{24,28},{4,0},{12,8},{20,16},{28,24},{1,5},{9... | collective-permute-start | bytes 786440 | tf_op jit(solution)/shard_map/ppermute | solution.py:415
  22.9 24.2 %collective-permute-start.15 = (f32[2,136,256]{2,1,0:T(8,128)S(1)}, f32[2,136,256]{2,1,0:T(8,128)S(1)}, u32[]{:S(2)}, u32[]{:S(2)}) collective-permute-start(f32[2,136,256]{2,1,0:T(8,128)S(1)} %get-tuple-element.31), channel_id=1, source_target_pairs={{4,8},{12,16},{20,24},{28,0},{8,4},{16,12},{24,20},{0,28},{5,9},{1... | collective-permute-start | bytes 835592 | tf_op jit(solution)/shard_map/ppermute | solution.py:415
  25.7 16.9 %collective-permute-start.16 = (f32[136,256]{1,0:T(8,128)S(1)}, f32[136,256]{1,0:T(8,128)S(1)}, u32[]{:S(2)}, u32[]{:S(2)}) collective-permute-start(f32[136,256]{1,0:T(8,128)S(1)} %get-tuple-element.21.refs_0_), channel_id=1, source_target_pairs={{4,8},{12,16},{20,24},{28,0},{8,4},{16,12},{24,20},{0,28},{5,9},{1... | collective-permute-start | bytes 417800 | tf_op jit(solution)/shard_map/ppermute | solution.py:415
  28.1 8.0 %collective-permute-start.6 = (f32[56,128]{1,0:T(8,128)S(1)}, f32[56,128]{1,0:T(8,128)S(1)}, u32[]{:S(2)}, u32[]{:S(2)}) collective-permute-start(f32[56,128]{1,0:T(8,128)S(1)} %shard_map.121.refs_0_), channel_id=1, source_target_pairs={{0,24},{4,28},{8,0},{12,4},{16,8},{20,12},{24,16},{28,20},{1,25},{... | collective-permute-start | bytes 86024 | tf_op jit(solution)/shard_map/ppermute | solution.py:409
  29.1 10.0 %collective-permute-start.5 = (f32[56,128]{1,0:T(8,128)S(1)}, f32[56,128]{1,0:T(8,128)S(1)}, u32[]{:S(2)}, u32[]{:S(2)}) collective-permute-start(f32[56,128]{1,0:T(8,128)S(1)} %shard_map.121.refs_0_), channel_id=1, source_target_pairs={{0,16},{4,20},{8,24},{12,28},{16,0},{20,4},{24,8},{28,12},{1,17},{... | collective-permute-start | bytes 86024 | tf_op jit(solution)/shard_map/ppermute | solution.py:409
  29.5 9.6 %collective-permute-start.4 = (f32[56,128]{1,0:T(8,128)S(1)}, f32[56,128]{1,0:T(8,128)S(1)}, u32[]{:S(2)}, u32[]{:S(2)}) collective-permute-start(f32[56,128]{1,0:T(8,128)S(1)} %shard_map.121.refs_0_), channel_id=1, source_target_pairs={{0,8},{4,12},{8,16},{12,20},{16,24},{20,28},{24,0},{28,4},{1,9},{5... | collective-permute-start | bytes 86024 | tf_op jit(solution)/shard_map/ppermute | solution.py:409
  39.5 5.3 %collective-permute-start.13 = (f32[112,256]{1,0:T(8,128)S(1)}, f32[112,256]{1,0:T(8,128)S(1)}, u32[]{:S(2)}, u32[]{:S(2)}) collective-permute-start(f32[112,256]{1,0:T(8,128)S(1)} %shard_map.124.refs_0_), channel_id=1, source_target_pairs={{0,3},{1,0},{2,1},{3,2},{4,7},{5,4},{6,5},{7,6},{8,11},{9,8},{10,9... | collective-permute-start | bytes 344072 | tf_op jit(solution)/shard_map/ppermute | solution.py:409
  40.1 5.7 %collective-permute-start.12 = (f32[112,256]{1,0:T(8,128)S(1)}, f32[112,256]{1,0:T(8,128)S(1)}, u32[]{:S(2)}, u32[]{:S(2)}) collective-permute-start(f32[112,256]{1,0:T(8,128)S(1)} %shard_map.124.refs_0_), channel_id=1, source_target_pairs={{0,2},{1,3},{2,0},{3,1},{4,6},{5,7},{6,4},{7,5},{8,10},{9,11},{10,... | collective-permute-start | bytes 344072 | tf_op jit(solution)/shard_map/ppermute | solution.py:409
  41.3 5.7 %collective-permute-start.11 = (f32[112,256]{1,0:T(8,128)S(1)}, f32[112,256]{1,0:T(8,128)S(1)}, u32[]{:S(2)}, u32[]{:S(2)}) collective-permute-start(f32[112,256]{1,0:T(8,128)S(1)} %shard_map.124.refs_0_), channel_id=1, source_target_pairs={{0,1},{1,2},{2,3},{3,0},{4,5},{5,6},{6,7},{7,4},{8,9},{9,10},{10,1... | collective-permute-start | bytes 344072 | tf_op jit(solution)/shard_map/ppermute | solution.py:409
  43.2 3.9 %copy-start.1 = (f32[256,256]{1,0:T(8,128)S(1)}, f32[256,256]{1,0:T(8,128)}, u32[]{:S(2)}) copy-start(f32[256,256]{1,0:T(8,128)} %mixing_ref.1) | copy-start | bytes 786436
  43.2 3.9 %copy-start.2 = (f32[64,256]{1,0:T(8,128)S(1)}, f32[64,256]{1,0:T(8,128)}, u32[]{:S(2)}) copy-start(f32[64,256]{1,0:T(8,128)} %radial_ref.1) | copy-start | bytes 196612
  43.2 3.9 %copy-start.3 = (f32[64,256]{1,0:T(8,128)S(1)}, f32[64,256]{1,0:T(8,128)}, u32[]{:S(2)}) copy-start(f32[64,256]{1,0:T(8,128)} %embed_ref.1) | copy-start | bytes 196612
  47.0 3.6 %collective-permute-start.14 = (f32[112,256]{1,0:T(8,128)S(1)}, f32[112,256]{1,0:T(8,128)S(1)}, u32[]{:S(2)}, u32[]{:S(2)}) collective-permute-start(f32[112,256]{1,0:T(8,128)S(1)} %shard_map.125.filtered_ref), channel_id=1, source_target_pairs={{0,4},{8,12},{16,20},{24,28},{4,0},{12,8},{20,16},{28,24},{1,5},{9... | collective-permute-start | bytes 344072 | tf_op jit(solution)/shard_map/ppermute | solution.py:415

commit v5 on v4

--- a/solution.py
+++ b/solution.py
@@ -314,18 +314,18 @@
     high_ref[...], low_ref[...] = split(dot3(split(features), split(value_ref[...])))
 
 
-def known_kernel(hot_ref, high_ref, low_ref, out_ref):
+def known_kernel(hot_ref, high_ref, low_ref, place_ref, values_ref, where_ref):
     hot = hot_ref[...]
-    out_ref[...] = dot(hot, high_ref[...]) + dot(hot, low_ref[...])
+    values_ref[...] = dot(hot, high_ref[...]) + dot(hot, low_ref[...])
+    where_ref[...] = dot(hot, place_ref[...], NT)
 
 
 def edge_kernel(
     sizes,
     own_ref,
     sides_ref,
-    hot_ref,
     far_ref,
-    place_ref,
+    where_ref,
     values_ref,
     value_ref,
     radial_ref,
@@ -369,7 +369,7 @@
         at = slice(start * atoms, start * atoms + rows)
         far = far_ref[at]
         near_values = values_ref[at] + dot(far, far_values[0]) + dot(far, far_values[1])
-        where = dot(hot_ref[at], place_ref[...], NT) + dot(far, far_place, NT)
+        where = where_ref[at] + dot(far, far_place, NT)
         gap = where + pltpu.roll(where, lanes - 4, 1) + pltpu.roll(where, lanes - 8, 1)
         gap = gap.reshape(chunk, atoms, lanes) - own_place[None]
         gap = jnp.where((lane < 3)[None], gap, 0.0)
@@ -537,10 +537,13 @@
         (own, pair, across, value_weight),
         10**8,
     )
-    near_values = call(
+    near_values, where = call(
         known_kernel,
-        jax.ShapeDtypeStruct((edges, channels), F32),
-        (hot, value_high, value_low),
+        [
+            jax.ShapeDtypeStruct((edges, channels), F32),
+            jax.ShapeDtypeStruct((edges, lanes), F32),
+        ],
+        (hot, value_high, value_low, places),
         10**8,
     )
     nearby = call(
@@ -549,9 +552,8 @@
         (
             own,
             sides,
-            hot,
             far,
-            places,
+            where,
             near_values,
             value_weight,
             radial_weight,

time: 51.6 us -> 51.6 us (level)
  transfers between devices with their start and end apart: 17 -> 17, of which waited for: 10 -> 9; matrix products, arithmetic and copies ran while one was open for 0% -> 0% of each run, Pallas kernels for 16% -> 17%
where the time goes in v5:
time: 51.6 us; the launch traced here: 51.4 us
  waiting for transfers between devices  21.4 us (41%)
  starting transfers between devices  19.1 us (37%)
  Pallas kernels  10.6 us (21%)
    ppermute x12, waiting for transfers between devices, shift(): return lax.ppermute(x, axis, [(i, (i + by) % count) for i in range(count)])  21.4 us
    ppermute x12, starting transfers between devices, shift(): return lax.ppermute(x, axis, [(i, (i + by) % count) for i in range(count)])  15.3 us
    pallas_call x14, Pallas kernels, call(): pl.pallas_call(kernel, out_shape=out_shape, in_specs=specs, scratch_shape...  10.6 us
    ppermute x5, starting transfers between devices, swap(): return lax.ppermute(x, 'gx', one + [(b, a) for a, b in one])  3.82 us
  transfers between devices with their start and end apart: 17, of which 9 were waited for; matrix products, arithmetic and copies ran while one was open for 0% of the time, Pallas kernels for 17%

profile of v5, /device:TPU:0, one launch (start us, length us, event | category | flops | bytes accessed | tf_op | source)
XLA Modules:
  0.0 51.4 jit_solution(14955936662449782991)
XLA Ops:
  0.0 1.0 %shard_map.118 = (f32[136,256]{1,0:T(8,128)S(1)}, f32[64,256]{1,0:T(8,128)S(1)}, s32[3,512]{1,0:T(4,128)S(1)}, f32[2,56,8]{2,1,0:T(8,128)S(1)}) custom-call(f32[1,1,128,256]{3,2,1,0:T(8,128)} %features_ref.1, f32[1,3,1,128]{3,2,1,0:T(1,128)} %bitcast.10, s32[1,1,128]{2,1,0:T(1,128)} %species_ref.1, f32[1,256,256]{2,1,0:T(8,128)} %weight_ref.1, ...), custom_call_target="tpu_custom_call" | custom-call | flops 1000000 | bytes 404992 | tf_op jit(solution)/shard_map/pallas_call | solution.py:397
  1.0 4.0 %collective-permute-start.2 = (f32[136,256]{1,0:T(8,128)S(1)}, f32[136,256]{1,0:T(8,128)S(1)}, u32[]{:S(2)}, u32[]{:S(2)}) collective-permute-start(f32[136,256]{1,0:T(8,128)S(1)} %get-tuple-element.23.refs_0_), channel_id=1, source_target_pairs={{0,3},{1,0},{2,1},{3,2},{4,7},{5,4},{6,5},{7,6},{8,11},{9,8},{10,9... | collective-permute-start | bytes 417800 | tf_op jit(solution)/shard_map/ppermute | solution.py:409
  6.1 3.0 %collective-permute-done.2.refs_3_ = f32[136,256]{1,0:T(8,128)S(1)} collective-permute-done((f32[136,256]{1,0:T(8,128)S(1)}, f32[136,256]{1,0:T(8,128)S(1)}, u32[]{:S(2)}, u32[]{:S(2)}) %collective-permute-start.2) | collective-permute-done | bytes 139296 | tf_op jit(solution)/shard_map/ppermute | solution.py:409
  9.1 4.1 %collective-permute-done.1.refs_2_ = f32[136,256]{1,0:T(8,128)S(1)} collective-permute-done((f32[136,256]{1,0:T(8,128)S(1)}, f32[136,256]{1,0:T(8,128)S(1)}, u32[]{:S(2)}, u32[]{:S(2)}) %collective-permute-start.1) | collective-permute-done | bytes 139296 | tf_op jit(solution)/shard_map/ppermute | solution.py:409
  13.3 1.6 %collective-permute-start.9 = (f32[64,256]{1,0:T(8,128)S(1)}, f32[64,256]{1,0:T(8,128)S(1)}, u32[]{:S(2)}, u32[]{:S(2)}) collective-permute-start(f32[64,256]{1,0:T(8,128)S(1)} %get-tuple-element.27.refs_0_), channel_id=1, source_target_pairs={{0,8},{4,12},{8,16},{12,20},{16,24},{20,28},{24,0},{28,4},{1,9},{5... | collective-permute-start | bytes 196616 | tf_op jit(solution)/shard_map/ppermute | solution.py:409
  14.9 2.6 %collective-permute-start.8 = (f32[64,256]{1,0:T(8,128)S(1)}, f32[64,256]{1,0:T(8,128)S(1)}, u32[]{:S(2)}, u32[]{:S(2)}) collective-permute-start(f32[64,256]{1,0:T(8,128)S(1)} %get-tuple-element.27.refs_0_), channel_id=1, source_target_pairs={{0,16},{4,20},{8,24},{12,28},{16,0},{20,4},{24,8},{28,12},{1,17},{... | collective-permute-start | bytes 196616 | tf_op jit(solution)/shard_map/ppermute | solution.py:409
  17.5 1.3 %collective-permute-start.7 = (f32[64,256]{1,0:T(8,128)S(1)}, f32[64,256]{1,0:T(8,128)S(1)}, u32[]{:S(2)}, u32[]{:S(2)}) collective-permute-start(f32[64,256]{1,0:T(8,128)S(1)} %get-tuple-element.27.refs_0_), channel_id=1, source_target_pairs={{0,24},{4,28},{8,0},{12,4},{16,8},{20,12},{24,16},{28,20},{1,25},{... | collective-permute-start | bytes 196616 | tf_op jit(solution)/shard_map/ppermute | solution.py:409
  18.9 0.9 %collective-permute-done.9.refs_3_ = f32[64,256]{1,0:T(8,128)S(1)} collective-permute-done((f32[64,256]{1,0:T(8,128)S(1)}, f32[64,256]{1,0:T(8,128)S(1)}, u32[]{:S(2)}, u32[]{:S(2)}) %collective-permute-start.9) | collective-permute-done | bytes 65568 | tf_op jit(solution)/shard_map/ppermute | solution.py:409
  19.8 2.8 %collective-permute-done.8.refs_2_ = f32[64,256]{1,0:T(8,128)S(1)} collective-permute-done((f32[64,256]{1,0:T(8,128)S(1)}, f32[64,256]{1,0:T(8,128)S(1)}, u32[]{:S(2)}, u32[]{:S(2)}) %collective-permute-start.8) | collective-permute-done | bytes 65568 | tf_op jit(solution)/shard_map/ppermute | solution.py:409
  22.9 2.8 %collective-permute-start.15 = (f32[2,136,256]{2,1,0:T(8,128)S(1)}, f32[2,136,256]{2,1,0:T(8,128)S(1)}, u32[]{:S(2)}, u32[]{:S(2)}) collective-permute-start(f32[2,136,256]{2,1,0:T(8,128)S(1)} %get-tuple-element.33), channel_id=1, source_target_pairs={{4,8},{12,16},{20,24},{28,0},{8,4},{16,12},{24,20},{0,28},{5,9},{1... | collective-permute-start | bytes 835592 | tf_op jit(solution)/shard_map/ppermute | solution.py:415
  25.7 0.8 %collective-permute-start.16 = (f32[136,256]{1,0:T(8,128)S(1)}, f32[136,256]{1,0:T(8,128)S(1)}, u32[]{:S(2)}, u32[]{:S(2)}) collective-permute-start(f32[136,256]{1,0:T(8,128)S(1)} %get-tuple-element.23.refs_0_), channel_id=1, source_target_pairs={{4,8},{12,16},{20,24},{28,0},{8,4},{16,12},{24,20},{0,28},{5,9},{1... | collective-permute-start | bytes 417800 | tf_op jit(solution)/shard_map/ppermute | solution.py:415
  26.5 0.8 %shard_map.120.refs_3_ = f32[56,128]{1,0:T(8,128)S(1)} custom-call(f32[4,136,256]{2,1,0:T(8,128)S(1)} %get-tuple-element.24.refs_0_.own_ref, s32[3,512]{1,0:T(4,128)S(1)} %get-tuple-element.25.refs_1_, f32[2,56,8]{2,1,0:T(8,128)S(1)} %get-tuple-element.26.refs_2_), custom_call_target="tpu_custom_call" | custom-call | flops 88080384 | bytes 566784 | tf_op jit(solution)/shard_map/pallas_call | solution.py:397
  27.3 0.8 %shard_map.121.refs_0_ = f32[56,128]{1,0:T(8,128)S(1)} custom-call(f32[4,136,256]{2,1,0:T(8,128)S(1)} %collective-permute-done.3.refs_0_.pair_ref, s32[3,512]{1,0:T(4,128)S(1)} %get-tuple-element.25.refs_1_, f32[2,56,8]{2,1,0:T(8,128)S(1)} %get-tuple-element.26.refs_2_, f32[56,128]{1,0:T(8,128)S(1)} %shard_map.120.refs_3_), custom_call_target="tpu_custom_call" | custom-call | flops 88080384 | bytes 595456 | tf_op jit(solution)/shard_map/pallas_call | solution.py:397
  28.1 1.0 %collective-permute-start.6 = (f32[56,128]{1,0:T(8,128)S(1)}, f32[56,128]{1,0:T(8,128)S(1)}, u32[]{:S(2)}, u32[]{:S(2)}) collective-permute-start(f32[56,128]{1,0:T(8,128)S(1)} %shard_map.121.refs_0_), channel_id=1, source_target_pairs={{0,24},{4,28},{8,0},{12,4},{16,8},{20,12},{24,16},{28,20},{1,25},{... | collective-permute-start | bytes 86024 | tf_op jit(solution)/shard_map/ppermute | solution.py:409
  29.5 0.7 %collective-permute-start.4 = (f32[56,128]{1,0:T(8,128)S(1)}, f32[56,128]{1,0:T(8,128)S(1)}, u32[]{:S(2)}, u32[]{:S(2)}) collective-permute-start(f32[56,128]{1,0:T(8,128)S(1)} %shard_map.121.refs_0_), channel_id=1, source_target_pairs={{0,8},{4,12},{8,16},{12,20},{16,24},{20,28},{24,0},{28,4},{1,9},{5... | collective-permute-start | bytes 86024 | tf_op jit(solution)/shard_map/ppermute | solution.py:409
  30.6 5.6 %collective-permute-done.6.refs_3_ = f32[56,128]{1,0:T(8,128)S(1)} collective-permute-done((f32[56,128]{1,0:T(8,128)S(1)}, f32[56,128]{1,0:T(8,128)S(1)}, u32[]{:S(2)}, u32[]{:S(2)}) %collective-permute-start.6) | collective-permute-done | bytes 28704 | tf_op jit(solution)/shard_map/ppermute | solution.py:409
  36.2 2.9 %collective-permute-done.5.refs_2_ = f32[56,128]{1,0:T(8,128)S(1)} collective-permute-done((f32[56,128]{1,0:T(8,128)S(1)}, f32[56,128]{1,0:T(8,128)S(1)}, u32[]{:S(2)}, u32[]{:S(2)}) %collective-permute-start.5) | collective-permute-done | bytes 28704 | tf_op jit(solution)/shard_map/ppermute | solution.py:409
  40.1 1.2 %collective-permute-start.12 = (f32[112,256]{1,0:T(8,128)S(1)}, f32[112,256]{1,0:T(8,128)S(1)}, u32[]{:S(2)}, u32[]{:S(2)}) collective-permute-start(f32[112,256]{1,0:T(8,128)S(1)} %shard_map.124.refs_0_), channel_id=1, source_target_pairs={{0,2},{1,3},{2,0},{3,1},{4,6},{5,7},{6,4},{7,5},{8,10},{9,11},{10,... | collective-permute-start | bytes 344072 | tf_op jit(solution)/shard_map/ppermute | solution.py:409
  41.3 0.7 %collective-permute-start.11 = (f32[112,256]{1,0:T(8,128)S(1)}, f32[112,256]{1,0:T(8,128)S(1)}, u32[]{:S(2)}, u32[]{:S(2)}) collective-permute-start(f32[112,256]{1,0:T(8,128)S(1)} %shard_map.124.refs_0_), channel_id=1, source_target_pairs={{0,1},{1,2},{2,3},{3,0},{4,5},{5,6},{6,7},{7,4},{8,9},{9,10},{10,1... | collective-permute-start | bytes 344072 | tf_op jit(solution)/shard_map/ppermute | solution.py:409
  43.3 1.7 %shard_map.128 = (f32[1024,256]{1,0:T(8,128)S(1)}, f32[1024,128]{1,0:T(8,128)S(1)}) custom-call(bf16[1024,896]{1,0:T(8,128)(2,1)S(1)} %get-tuple-element.35.hot_ref, bf16[896,256]{1,0:T(8,128)(2,1)S(1)} %get-tuple-element.36.high_ref, bf16[896,256]{1,0:T(8,128)(2,1)S(1)} %get-tuple-element.37.low_ref, bf16[128,896]{1,0:T(8,128)(2,1)S(1)} %get-tuple-element.38.place_ref), custom_call_target="tpu_custom_call" | custom-call | flops 100000000 | bytes 5963776 | tf_op jit(solution)/shard_map/pallas_call | solution.py:397
  45.0 0.8 %collective-permute-done.12.refs_2_ = f32[112,256]{1,0:T(8,128)S(1)} collective-permute-done((f32[112,256]{1,0:T(8,128)S(1)}, f32[112,256]{1,0:T(8,128)S(1)}, u32[]{:S(2)}, u32[]{:S(2)}) %collective-permute-start.12) | collective-permute-done | bytes 114720 | tf_op jit(solution)/shard_map/ppermute | solution.py:409
  45.8 1.2 %collective-permute-done.11.refs_1_ = f32[112,256]{1,0:T(8,128)S(1)} collective-permute-done((f32[112,256]{1,0:T(8,128)S(1)}, f32[112,256]{1,0:T(8,128)S(1)}, u32[]{:S(2)}, u32[]{:S(2)}) %collective-permute-start.11) | collective-permute-done | bytes 114720 | tf_op jit(solution)/shard_map/ppermute | solution.py:409
  47.2 3.2 %shard_map.129.sum_ref = f32[128,256]{1,0:T(8,128)S(1)} custom-call(f32[4,136,256]{2,1,0:T(8,128)S(1)} %get-tuple-element.24.refs_0_.own_ref, f32[2,136,256]{2,1,0:T(8,128)S(1)} %collective-permute-done.15.sides_ref, bf16[1024,256]{1,0:T(8,128)(2,1)S(1)} %get-tuple-element.34.far_ref, f32[1024,128]{1,0:T(8,128)S(1)} %get-tuple-element.39.where_ref, ...), custom_call_target="tpu_custom_call" | custom-call | flops 4000000000 | bytes 4112384 | tf_op jit(solution)/shard_map/pallas_call | solution.py:397
  50.6 0.9 %shard_map.131 = f32[128,256]{1,0:T(8,128)} custom-call(f32[112,256]{1,0:T(8,128)S(1)} %collective-permute-done.14.filtered_ref, bf16[128,112]{1,0:T(8,128)(2,1)S(1)} %get-tuple-element.29.high_ref, bf16[128,112]{1,0:T(8,128)(2,1)S(1)} %get-tuple-element.30.low_ref, f32[128,256]{1,0:T(8,128)S(1)} %shard_map.130.sum_ref), custom_call_target="tpu_custom_call" | custom-call | flops 22020096 | bytes 360448 | tf_op jit(solution)/shard_map/pallas_call | solution.py:397
  (36 shorter events, 4.8 us)
Async XLA Ops:
  1.0 41.0 %copy-start.4 = (s32[1,1,128,8]{2,3,1,0:T(8,128)S(1)}, s32[1,1,128,8]{2,3,1,0:T(8,128)}, u32[]{:S(2)}) copy-start(s32[1,1,128,8]{2,3,1,0:T(8,128)} %param.15) | copy-start | bytes 12292
  1.0 41.0 %copy-start.5 = (s32[1,1,128,8]{2,3,1,0:T(8,128)S(1)}, s32[1,1,128,8]{2,3,1,0:T(8,128)}, u32[]{:S(2)}) copy-start(s32[1,1,128,8]{2,3,1,0:T(8,128)} %param.16) | copy-start | bytes 12292
  1.0 8.0 %collective-permute-start.2 = (f32[136,256]{1,0:T(8,128)S(1)}, f32[136,256]{1,0:T(8,128)S(1)}, u32[]{:S(2)}, u32[]{:S(2)}) collective-permute-start(f32[136,256]{1,0:T(8,128)S(1)} %get-tuple-element.23.refs_0_), channel_id=1, source_target_pairs={{0,3},{1,0},{2,1},{3,2},{4,7},{5,4},{6,5},{7,6},{8,11},{9,8},{10,9... | collective-permute-start | bytes 417800 | tf_op jit(solution)/shard_map/ppermute | solution.py:409
  5.0 8.1 %collective-permute-start.1 = (f32[136,256]{1,0:T(8,128)S(1)}, f32[136,256]{1,0:T(8,128)S(1)}, u32[]{:S(2)}, u32[]{:S(2)}) collective-permute-start(f32[136,256]{1,0:T(8,128)S(1)} %get-tuple-element.23.refs_0_), channel_id=1, source_target_pairs={{0,2},{1,3},{2,0},{3,1},{4,6},{5,7},{6,4},{7,5},{8,10},{9,11},{10,... | collective-permute-start | bytes 417800 | tf_op jit(solution)/shard_map/ppermute | solution.py:409
  5.5 7.6 %collective-permute-start = (f32[136,256]{1,0:T(8,128)S(1)}, f32[136,256]{1,0:T(8,128)S(1)}, u32[]{:S(2)}, u32[]{:S(2)}) collective-permute-start(f32[136,256]{1,0:T(8,128)S(1)} %get-tuple-element.23.refs_0_), channel_id=1, source_target_pairs={{0,1},{1,2},{2,3},{3,0},{4,5},{5,6},{6,7},{7,4},{8,9},{9,10},{10,1... | collective-permute-start | bytes 417800 | tf_op jit(solution)/shard_map/ppermute | solution.py:409
  13.2 29.4 %copy-start = (f32[256,256]{1,0:T(8,128)S(1)}, f32[256,256]{1,0:T(8,128)}, u32[]{:S(2)}) copy-start(f32[256,256]{1,0:T(8,128)} %value_ref.3) | copy-start | bytes 786436
  13.2 14.1 %collective-permute-start.3 = (f32[4,136,256]{2,1,0:T(8,128)S(1)}, f32[4,136,256]{2,1,0:T(8,128)S(1)}, u32[]{:S(2)}, u32[]{:S(2)}) collective-permute-start(f32[4,136,256]{2,1,0:T(8,128)S(1)} %get-tuple-element.24.refs_0_.own_ref), channel_id=1, source_target_pairs={{0,4},{8,12},{16,20},{24,28},{4,0},{12,8},{20,16},{28,24},{1,5},{9... | collective-permute-start | bytes 1671176 | tf_op jit(solution)/shard_map/ppermute | solution.py:415
  13.3 6.5 %collective-permute-start.9 = (f32[64,256]{1,0:T(8,128)S(1)}, f32[64,256]{1,0:T(8,128)S(1)}, u32[]{:S(2)}, u32[]{:S(2)}) collective-permute-start(f32[64,256]{1,0:T(8,128)S(1)} %get-tuple-element.27.refs_0_), channel_id=1, source_target_pairs={{0,8},{4,12},{8,16},{12,20},{16,24},{20,28},{24,0},{28,4},{1,9},{5... | collective-permute-start | bytes 196616 | tf_op jit(solution)/shard_map/ppermute | solution.py:409
  14.9 7.6 %collective-permute-start.8 = (f32[64,256]{1,0:T(8,128)S(1)}, f32[64,256]{1,0:T(8,128)S(1)}, u32[]{:S(2)}, u32[]{:S(2)}) collective-permute-start(f32[64,256]{1,0:T(8,128)S(1)} %get-tuple-element.27.refs_0_), channel_id=1, source_target_pairs={{0,16},{4,20},{8,24},{12,28},{16,0},{20,4},{24,8},{28,12},{1,17},{... | collective-permute-start | bytes 196616 | tf_op jit(solution)/shard_map/ppermute | solution.py:409
  17.5 5.3 %collective-permute-start.7 = (f32[64,256]{1,0:T(8,128)S(1)}, f32[64,256]{1,0:T(8,128)S(1)}, u32[]{:S(2)}, u32[]{:S(2)}) collective-permute-start(f32[64,256]{1,0:T(8,128)S(1)} %get-tuple-element.27.refs_0_), channel_id=1, source_target_pairs={{0,24},{4,28},{8,0},{12,4},{16,8},{20,12},{24,16},{28,20},{1,25},{... | collective-permute-start | bytes 196616 | tf_op jit(solution)/shard_map/ppermute | solution.py:409
  22.8 6.7 %collective-permute-start.10 = (f32[4,64,256]{2,1,0:T(8,128)S(1)}, f32[4,64,256]{2,1,0:T(8,128)S(1)}, u32[]{:S(2)}, u32[]{:S(2)}) collective-permute-start(f32[4,64,256]{2,1,0:T(8,128)S(1)} %shard_map.122.refs_4_), channel_id=1, source_target_pairs={{0,4},{8,12},{16,20},{24,28},{4,0},{12,8},{20,16},{28,24},{1,5},{9... | collective-permute-start | bytes 786440 | tf_op jit(solution)/shard_map/ppermute | solution.py:415
  22.9 24.2 %collective-permute-start.15 = (f32[2,136,256]{2,1,0:T(8,128)S(1)}, f32[2,136,256]{2,1,0:T(8,128)S(1)}, u32[]{:S(2)}, u32[]{:S(2)}) collective-permute-start(f32[2,136,256]{2,1,0:T(8,128)S(1)} %get-tuple-element.33), channel_id=1, source_target_pairs={{4,8},{12,16},{20,24},{28,0},{8,4},{16,12},{24,20},{0,28},{5,9},{1... | collective-permute-start | bytes 835592 | tf_op jit(solution)/shard_map/ppermute | solution.py:415
  25.7 16.9 %collective-permute-start.16 = (f32[136,256]{1,0:T(8,128)S(1)}, f32[136,256]{1,0:T(8,128)S(1)}, u32[]{:S(2)}, u32[]{:S(2)}) collective-permute-start(f32[136,256]{1,0:T(8,128)S(1)} %get-tuple-element.23.refs_0_), channel_id=1, source_target_pairs={{4,8},{12,16},{20,24},{28,0},{8,4},{16,12},{24,20},{0,28},{5,9},{1... | collective-permute-start | bytes 417800 | tf_op jit(solution)/shard_map/ppermute | solution.py:415
  28.1 8.0 %collective-permute-start.6 = (f32[56,128]{1,0:T(8,128)S(1)}, f32[56,128]{1,0:T(8,128)S(1)}, u32[]{:S(2)}, u32[]{:S(2)}) collective-permute-start(f32[56,128]{1,0:T(8,128)S(1)} %shard_map.121.refs_0_), channel_id=1, source_target_pairs={{0,24},{4,28},{8,0},{12,4},{16,8},{20,12},{24,16},{28,20},{1,25},{... | collective-permute-start | bytes 86024 | tf_op jit(solution)/shard_map/ppermute | solution.py:409
  29.1 10.0 %collective-permute-start.5 = (f32[56,128]{1,0:T(8,128)S(1)}, f32[56,128]{1,0:T(8,128)S(1)}, u32[]{:S(2)}, u32[]{:S(2)}) collective-permute-start(f32[56,128]{1,0:T(8,128)S(1)} %shard_map.121.refs_0_), channel_id=1, source_target_pairs={{0,16},{4,20},{8,24},{12,28},{16,0},{20,4},{24,8},{28,12},{1,17},{... | collective-permute-start | bytes 86024 | tf_op jit(solution)/shard_map/ppermute | solution.py:409
  29.5 9.6 %collective-permute-start.4 = (f32[56,128]{1,0:T(8,128)S(1)}, f32[56,128]{1,0:T(8,128)S(1)}, u32[]{:S(2)}, u32[]{:S(2)}) collective-permute-start(f32[56,128]{1,0:T(8,128)S(1)} %shard_map.121.refs_0_), channel_id=1, source_target_pairs={{0,8},{4,12},{8,16},{12,20},{16,24},{20,28},{24,0},{28,4},{1,9},{5... | collective-permute-start | bytes 86024 | tf_op jit(solution)/shard_map/ppermute | solution.py:409
  39.5 5.5 %collective-permute-start.13 = (f32[112,256]{1,0:T(8,128)S(1)}, f32[112,256]{1,0:T(8,128)S(1)}, u32[]{:S(2)}, u32[]{:S(2)}) collective-permute-start(f32[112,256]{1,0:T(8,128)S(1)} %shard_map.124.refs_0_), channel_id=1, source_target_pairs={{0,3},{1,0},{2,1},{3,2},{4,7},{5,4},{6,5},{7,6},{8,11},{9,8},{10,9... | collective-permute-start | bytes 344072 | tf_op jit(solution)/shard_map/ppermute | solution.py:409
  40.1 5.7 %collective-permute-start.12 = (f32[112,256]{1,0:T(8,128)S(1)}, f32[112,256]{1,0:T(8,128)S(1)}, u32[]{:S(2)}, u32[]{:S(2)}) collective-permute-start(f32[112,256]{1,0:T(8,128)S(1)} %shard_map.124.refs_0_), channel_id=1, source_target_pairs={{0,2},{1,3},{2,0},{3,1},{4,6},{5,7},{6,4},{7,5},{8,10},{9,11},{10,... | collective-permute-start | bytes 344072 | tf_op jit(solution)/shard_map/ppermute | solution.py:409
  41.3 5.7 %collective-permute-start.11 = (f32[112,256]{1,0:T(8,128)S(1)}, f32[112,256]{1,0:T(8,128)S(1)}, u32[]{:S(2)}, u32[]{:S(2)}) collective-permute-start(f32[112,256]{1,0:T(8,128)S(1)} %shard_map.124.refs_0_), channel_id=1, source_target_pairs={{0,1},{1,2},{2,3},{3,0},{4,5},{5,6},{6,7},{7,4},{8,9},{9,10},{10,1... | collective-permute-start | bytes 344072 | tf_op jit(solution)/shard_map/ppermute | solution.py:409
  43.2 3.9 %copy-start.1 = (f32[256,256]{1,0:T(8,128)S(1)}, f32[256,256]{1,0:T(8,128)}, u32[]{:S(2)}) copy-start(f32[256,256]{1,0:T(8,128)} %mixing_ref.1) | copy-start | bytes 786436
  43.2 3.9 %copy-start.2 = (f32[64,256]{1,0:T(8,128)S(1)}, f32[64,256]{1,0:T(8,128)}, u32[]{:S(2)}) copy-start(f32[64,256]{1,0:T(8,128)} %radial_ref.1) | copy-start | bytes 196612
  43.2 3.9 %copy-start.3 = (f32[64,256]{1,0:T(8,128)S(1)}, f32[64,256]{1,0:T(8,128)}, u32[]{:S(2)}) copy-start(f32[64,256]{1,0:T(8,128)} %embed_ref.1) | copy-start | bytes 196612
  47.1 3.5 %collective-permute-start.14 = (f32[112,256]{1,0:T(8,128)S(1)}, f32[112,256]{1,0:T(8,128)S(1)}, u32[]{:S(2)}, u32[]{:S(2)}) collective-permute-start(f32[112,256]{1,0:T(8,128)S(1)} %shard_map.125.filtered_ref), channel_id=1, source_target_pairs={{0,4},{8,12},{16,20},{24,28},{4,0},{12,8},{20,16},{28,24},{1,5},{9... | collective-permute-start | bytes 344072 | tf_op jit(solution)/shard_map/ppermute | solution.py:415
